TPU v7x, 256 devices: a whole 4x4x8 slice. The times are simulated.
256 devices in a mesh: rows: 128 (over y_lo, x, z, core), feat: 2 (over y_hi).
Axes of the slice: x: 4, y: 4 (y_hi: 2, y_lo: 2; y = y_hi * 2 + y_lo), z: 8, core: 2. Of those that a mesh axis runs over, the one named last changes fastest.
Arguments:
- train_cells: bfloat16 [8192, 1536], P('rows', 'feat'), may hold values from -24 to 24
- test_cells: bfloat16 [4096, 1536], P('rows', 'feat'), may hold values from -24 to 24
- feat_weights: bfloat16 [4, 192, 192], replicated
- row_weights: bfloat16 [4, 192, 192], replicated
- mlp_up: bfloat16 [192, 768], replicated, may hold values from -0.4375 to 0.4375
- mlp_down: bfloat16 [768, 192], replicated, may hold values from -0.21875 to 0.21875
Outputs:
- train_out: bfloat16 [8192, 1536], P('rows', 'feat')
- test_out: bfloat16 [4096, 1536], P('rows', 'feat')
All inputs are finite; a program needn't handle non-finite values.
Results may differ from a plain program's by a relative error of at most 0.017.
Values may be sent and summed in bfloat16 or wider, within the bound.
No kernel may reach another device: no remote copies, remote signals or barrier semaphores. Data moves between devices by JAX's collectives and lax.ppermute only.
A program may use at most 128 MiB of HBM per device.

v0:
```python
import math

import jax
import jax.numpy as jnp
from jax import lax
from jax.experimental import pallas as pl
from jax.experimental.pallas import tpu as pltpu
from jax.sharding import Mesh
from jax.sharding import PartitionSpec as P

E = 192
HEADS = 6
HD = 32
GROUPS = 4
FEATS = 8
TRAIN_ROWS = 64
TEST_ROWS = 32
ROWS = TRAIN_ROWS + TEST_ROWS
SIDE = 4
LANES = 128
REST = E - LANES
TRAIN_PACK = TRAIN_ROWS + TRAIN_ROWS // 2
PACK = ROWS + ROWS // 2
OWN_Q = GROUPS * ROWS
ALL_Q = 2 * OWN_Q
SOURCES = GROUPS * SIDE
KEYS = SOURCES * TRAIN_ROWS
SUMS = HD + 16
FOLD = E + 16
PROBES = 64
BLOCK = SOURCES * TRAIN_PACK
STATE = HD + 8

eps_norm = 1e-05
far_below = -3e38
safe_size = 2.0**60
log2_scale = HD ** (-0.5) * math.log2(math.e)


bf16 = jnp.bfloat16
f32 = jnp.float32


def mm(left, right):
    return jnp.dot(left, right, preferred_element_type=f32)


def mm_nt(left, right):
    return lax.dot_general(left, right, (((1,), (1,)), ((), ())), preferred_element_type=f32)


def layer_norm(values_in):
    centred = values_in - jnp.mean(values_in, axis=-1, keepdims=True)
    spread = jnp.mean(centred * centred, axis=-1, keepdims=True)
    return centred * lax.rsqrt(spread + eps_norm)


def call(kernel, outs, args, flops, scratch=(), limit=12):
    in_vmem = pl.BlockSpec(memory_space=pltpu.VMEM)
    return pl.pallas_call(
        kernel,
        out_shape=outs,
        in_specs=[in_vmem] * len(args),
        out_specs=[in_vmem] * len(outs),
        scratch_shapes=list(scratch),
        compiler_params=pltpu.CompilerParams(vmem_limit_bytes=limit * 2**20),
        cost_estimate=pl.CostEstimate(flops=flops, transcendentals=0, bytes_accessed=2**20),
    )(*args)


def pack_rows(rows):
    half = rows.shape[0] // 2
    rest = rows[:, LANES:]
    return [rows[:, :LANES], jnp.concatenate([rest[:half], rest[half:]], axis=1)]


def pack(rows):
    parts = pack_rows(rows[:TRAIN_ROWS]) + pack_rows(rows[TRAIN_ROWS:])
    return jnp.concatenate(parts, axis=0).astype(bf16)


def unpack_rows(packed):
    height = packed.shape[0] * 2 // 3
    rest = packed[height:]
    rest = jnp.concatenate([rest[:, :REST], rest[:, REST:]], axis=0)
    return jnp.concatenate([packed[:height], rest], axis=1)


def unpack(packed):
    packed = packed.astype(f32)
    parts = [unpack_rows(packed[:TRAIN_PACK]), unpack_rows(packed[TRAIN_PACK:])]
    return jnp.concatenate(parts, axis=0)


def near_kernel(train_ref, test_ref, weights_ref, cells_ref, query_ref, key_ref, value_ref):
    parts = []
    for index in range(GROUPS):
        span = slice(index * E, (index + 1) * E)
        cell = [one_ref[:, span].astype(f32) for one_ref in (train_ref, test_ref)]
        cell = jnp.concatenate(cell, axis=0)
        cells_ref[index] = cell
        parts.append(layer_norm(cell).astype(bf16))
    normed = jnp.concatenate(parts, axis=0)
    query_ref[...] = (mm(normed, weights_ref[0]) * log2_scale).astype(bf16)
    key_ref[...] = mm(normed, weights_ref[1]).astype(bf16)
    value_ref[...] = mm(normed, weights_ref[2]).astype(bf16)


def before_kernel(
    other_ref, weights_ref, cells_ref, query_ref, key_ref, value_ref, after_ref, send_ref
):
    parts = []
    for index in range(GROUPS):
        cell = other_ref[:, index * E : (index + 1) * E].astype(f32)
        parts.append(layer_norm(cell).astype(bf16))
    normed = jnp.concatenate(parts, axis=0)
    far_keys = mm(normed, weights_ref[1]).astype(bf16)
    far_values = mm(normed, weights_ref[2]).astype(bf16)
    queries = query_ref[...]
    keys = jnp.concatenate([key_ref[...], far_keys], axis=0)
    values = jnp.concatenate([value_ref[...], far_values], axis=0).astype(f32)
    head_of = lax.broadcasted_iota(jnp.int32, (E, 128), 0) >> 5
    gather = jnp.where(head_of == lax.broadcasted_iota(jnp.int32, (E, 128), 1), 1.0, 0.0).astype(bf16)
    head_to = lax.broadcasted_iota(jnp.int32, (128, E), 1) >> 5
    spread = jnp.where(head_to == lax.broadcasted_iota(jnp.int32, (128, E), 0), 1.0, 0.0).astype(bf16)
    mixtures = []
    for index in range(GROUPS):
        asked = queries[index * ROWS : (index + 1) * ROWS]
        products = jnp.concatenate(
            [asked * keys[j * ROWS : (j + 1) * ROWS] for j in range(FEATS)], axis=0
        )
        scores = mm(products, gather)
        pieces = [scores[j * ROWS : (j + 1) * ROWS] for j in range(FEATS)]
        peak = pieces[0]
        for one in pieces[1:]:
            peak = jnp.maximum(peak, one)
        weights = [jnp.exp2(one - peak) for one in pieces]
        total = weights[0]
        for one in weights[1:]:
            total = total + one
        high = total.astype(bf16)
        low = (total - high.astype(f32)).astype(bf16)
        wide = mm(jnp.concatenate([one.astype(bf16) for one in weights] + [high, low], axis=0), spread)
        mixed = wide[:ROWS] * values[:ROWS]
        for j in range(1, FEATS):
            mixed = mixed + wide[j * ROWS : (j + 1) * ROWS] * values[j * ROWS : (j + 1) * ROWS]
        whole = wide[FEATS * ROWS : (FEATS + 1) * ROWS] + wide[(FEATS + 1) * ROWS :]
        mixtures.append((mixed / whole).astype(bf16))
    moved = mm(jnp.concatenate(mixtures, axis=0), weights_ref[3]).astype(bf16).astype(f32)
    for index in range(GROUPS):
        after = cells_ref[index] + moved[index * ROWS : (index + 1) * ROWS]
        after_ref[index] = after
        send_ref[index] = pack(layer_norm(after))


def fold_kernel(own_ref, other_ref, weights_ref, folded_ref, turned_ref):
    turned_ref[...] = weights_ref[2].astype(f32).T.astype(bf16)
    parts = [unpack(one_ref[index]) for one_ref in (own_ref, other_ref) for index in range(GROUPS)]
    asked = jnp.concatenate(parts, axis=0).astype(bf16)
    probes = jnp.concatenate([parts[0][:PROBES], parts[GROUPS][:PROBES]], axis=0).astype(bf16)
    queries = (mm(asked, weights_ref[0]) * log2_scale).astype(bf16)
    weight = weights_ref[1]
    row = lax.broadcasted_iota(jnp.int32, (FOLD - E, ALL_Q), 0)
    for head in range(HEADS):
        part = slice(head * HD, (head + 1) * HD)
        folded = mm_nt(weight[:, part], queries[:, part]).astype(bf16)
        peak = jnp.max(mm(probes, folded), axis=0, keepdims=True)
        folded_ref[head, :E, :] = folded
        folded_ref[head, E:, :] = jnp.where(row == 0, -peak, 0.0).astype(bf16)


def stack_kernel(*refs):
    height = GROUPS * TRAIN_PACK
    for index in range(SIDE):
        refs[-1][index * height : (index + 1) * height, :] = refs[index][...]


def unpack_keys(packed_refs, keys_ref):
    half = TRAIN_ROWS // 2
    each = SOURCES // len(packed_refs)
    for source in range(SOURCES):
        packed_ref = packed_refs[source // each]
        low = source * TRAIN_ROWS
        top = source % each * TRAIN_PACK
        rest = packed_ref[top + TRAIN_ROWS : top + TRAIN_PACK, :]
        keys_ref[low : low + TRAIN_ROWS, :LANES] = packed_ref[top : top + TRAIN_ROWS, :]
        keys_ref[low : low + half, LANES:E] = rest[:, :REST]
        keys_ref[low + half : low + TRAIN_ROWS, LANES:E] = rest[:, REST:]
    keys_ref[:, E:] = jnp.ones((KEYS, FOLD - E), bf16)


def turn_values(wv_ref, keys_ref, values_ref):
    values = mm_nt(wv_ref[...], keys_ref[:, :E]).astype(bf16)
    for head in range(HEADS):
        values_ref[head, 0:HD, :] = values[head * HD : (head + 1) * HD, :]
        values_ref[head, HD:SUMS, :] = jnp.ones((SUMS - HD, KEYS), bf16)


def attend_kernel(first, packed_refs, refs):
    wv_ref, folded_ref = refs[:2]
    mix_out, keys_ref, values_ref = refs[-3:]
    unpack_keys(packed_refs, keys_ref)
    turn_values(wv_ref, keys_ref, values_ref)

    def work(head):
        weights = jnp.exp2(mm(keys_ref[...], folded_ref[head])).astype(bf16)
        mixed = mm(values_ref[head], weights)
        if not first:
            mixed = mixed + refs[2][head]
        mix_out[head] = mixed

    for head in range(HEADS):
        work(head)


def attend_last_kernel(
    left_ref,
    right_ref,
    wv_ref,
    folded_ref,
    mix_ref,
    first_ref,
    second_ref,
    third_ref,
    stay_ref,
    leave_ref,
    keys_ref,
    values_ref,
    total_ref,
    peak_ref,
    blocks_ref,
    scores_ref,
):
    attend_kernel(
        False,
        (left_ref, right_ref),
        (wv_ref, folded_ref, mix_ref, total_ref, keys_ref, values_ref),
    )
    for head in range(HEADS):
        peak_ref[head] = -folded_ref[head, E:, :].astype(f32)[:8]
    over = jnp.where(jnp.abs(total_ref[...]) < safe_size, 0.0, 1.0)

    @pl.when(jnp.max(over) > 0.0)
    def _():
        for index, one_ref in enumerate((first_ref, second_ref, third_ref)):
            blocks_ref[index] = one_ref[...]
        blocks_ref[SIDE - 1, : BLOCK // 2] = left_ref[...]
        blocks_ref[SIDE - 1, BLOCK // 2 :] = right_ref[...]
        peak_ref[...] = jnp.full(peak_ref.shape, far_below, f32)
        total_ref[...] = jnp.zeros(total_ref.shape, f32)

        def one_block(index, carry):
            unpack_keys((blocks_ref.at[index],), keys_ref)
            turn_values(wv_ref, keys_ref, values_ref)

            def work(head, kept):
                scores_ref[...] = mm(keys_ref[:, :E], folded_ref[head, :E, :])
                old = peak_ref[head][0:1, :]
                peak = jnp.maximum(jnp.max(scores_ref[...], axis=0, keepdims=True), old)
                weights = jnp.exp2(scores_ref[...] - peak).astype(bf16)
                mixed = mm(values_ref[head], weights)
                total_ref[head] = total_ref[head] * jnp.exp2(old - peak) + mixed
                peak_ref[head] = jnp.broadcast_to(peak, (8, ALL_Q))
                return kept

            lax.fori_loop(0, HEADS, work, 0)
            return carry

        lax.fori_loop(0, SIDE, one_block, 0)

    for head in range(HEADS):
        total = total_ref[head]
        joined = jnp.concatenate(
            [total[: HD + 1], peak_ref[head][0:1, :], total[HD + 2 : STATE]], axis=0
        )
        stay_ref[head] = joined[:, :OWN_Q]
        leave_ref[head] = joined[:, OWN_Q:]


mix_shape = jax.ShapeDtypeStruct((HEADS, SUMS, ALL_Q), f32)
attend_scratch = [pltpu.VMEM((KEYS, FOLD), bf16), pltpu.VMEM((HEADS, SUMS, KEYS), bf16)]
attend_flops = 4 * HEADS * KEYS * ALL_Q * E


def attend(args):
    first = len(args) == 3
    return call(
        lambda *refs: attend_kernel(first, refs[:1], refs[1:]),
        [mix_shape],
        args,
        attend_flops,
        scratch=attend_scratch,
        limit=20,
    )[0]


def attend_last(args):
    return call(
        attend_last_kernel,
        [jax.ShapeDtypeStruct((HEADS, STATE, OWN_Q), f32)] * 2,
        args,
        attend_flops,
        scratch=attend_scratch
        + [
            pltpu.VMEM((HEADS, SUMS, ALL_Q), f32),
            pltpu.VMEM((HEADS, 8, ALL_Q), f32),
            pltpu.VMEM((SIDE, BLOCK, LANES), bf16),
            pltpu.VMEM((KEYS, ALL_Q), f32),
        ],
        limit=20,
    )


def merge_kernel(stay_ref, came_ref, send_ref):
    parts = []
    for head in range(HEADS):
        stay = stay_ref[head]
        came = came_ref[head]
        peak = jnp.maximum(stay[HD + 1 : HD + 2], came[HD + 1 : HD + 2])
        fade_stay = jnp.exp2(stay[HD + 1 : HD + 2] - peak)
        fade_came = jnp.exp2(came[HD + 1 : HD + 2] - peak)
        total = stay[HD : HD + 1] * fade_stay + came[HD : HD + 1] * fade_came
        mixed = stay[:HD] * fade_stay + came[:HD] * fade_came
        parts.append(mixed / total)
    turned = jnp.concatenate(parts, axis=0).T
    for peer in range(GROUPS):
        send_ref[peer] = pack(turned[peer * ROWS : (peer + 1) * ROWS])


def after_kernel(came_ref, after_ref, wo_ref, up_ref, down_ref, train_ref, test_ref):
    mixes = [unpack(came_ref[index]) for index in range(GROUPS)]
    row_mix = jnp.concatenate(mixes, axis=0).astype(bf16)
    after_row = after_ref[...].reshape(GROUPS * ROWS, E) + mm(row_mix, wo_ref[...])
    third = layer_norm(after_row).astype(bf16)
    raised = mm(third, up_ref[...])
    hidden = (0.5 * raised * (1.0 + lax.erf(raised * (0.5**0.5)))).astype(bf16)
    result = (after_row + mm(hidden, down_ref[...])).astype(bf16)
    for index in range(GROUPS):
        low = index * ROWS
        left = index * E
        train_ref[:, left : left + E] = result[low : low + TRAIN_ROWS]
        test_ref[:, left : left + E] = result[low + TRAIN_ROWS : low + ROWS]


def shift(size, by):
    return [(index, (index + by) % size) for index in range(size)]


def layer(train_cells, test_cells, feat_weights, row_weights, mlp_up, mlp_down):
    swap = [(0, 1), (1, 0)]
    joined = jnp.concatenate([train_cells, test_cells], axis=0)
    other = lax.ppermute(joined, "feat", swap)
    wide = (GROUPS * ROWS, E)
    near = call(
        near_kernel,
        [jax.ShapeDtypeStruct((GROUPS, ROWS, E), f32)] + [jax.ShapeDtypeStruct(wide, bf16)] * 3,
        (train_cells, test_cells, feat_weights),
        10**9,
    )
    after_feat, pieces = call(
        before_kernel,
        [
            jax.ShapeDtypeStruct((GROUPS, ROWS, E), f32),
            jax.ShapeDtypeStruct((GROUPS, PACK, LANES), bf16),
        ],
        (other, feat_weights, *near),
        10**9,
    )
    classes = ("y_lo", "z_lo")
    received = lax.all_to_all(pieces, classes, split_axis=0, concat_axis=0, tiled=True)
    keys = received[:, :TRAIN_PACK].reshape(GROUPS * TRAIN_PACK, LANES)
    column = [keys]
    for by in (1, 3, 2):
        column.append(lax.ppermute(keys, "z_hi", shift(SIDE, by)))
    received_other = lax.ppermute(received, "core", swap)
    folded, value_turned = call(
        fold_kernel,
        [
            jax.ShapeDtypeStruct((HEADS, FOLD, ALL_Q), bf16),
            jax.ShapeDtypeStruct((E, E), bf16),
        ],
        (received, received_other, row_weights),
        10**9,
    )
    column, folded = lax.optimization_barrier((column, folded))
    keys = call(
        stack_kernel,
        [jax.ShapeDtypeStruct((SIDE * GROUPS * TRAIN_PACK, LANES), bf16)],
        column,
        10**6,
        limit=4,
    )[0]
    above = lax.ppermute(keys, "x", shift(4, 1))
    below = lax.ppermute(keys, "x", shift(4, 3))
    mix = attend((keys, value_turned, folded))
    mix, above, below = lax.optimization_barrier((mix, above, below))
    far_above = lax.ppermute(above[: BLOCK // 2], "x", shift(4, 1))
    far_below_keys = lax.ppermute(below[BLOCK // 2 :], "x", shift(4, 3))
    mix = attend((above, value_turned, folded, mix))
    mix = attend((below, value_turned, folded, mix))
    stay, leave = attend_last(
        (far_above, far_below_keys, value_turned, folded, mix, keys, above, below)
    )
    came = lax.ppermute(leave, "core", swap)
    mixed = call(
        merge_kernel, [jax.ShapeDtypeStruct((GROUPS, PACK, LANES), bf16)], (stay, came), 10**7
    )[0]
    returned = lax.all_to_all(mixed, classes, split_axis=0, concat_axis=0, tiled=True)
    train_out, test_out = call(
        after_kernel,
        [
            jax.ShapeDtypeStruct((TRAIN_ROWS, GROUPS * E), bf16),
            jax.ShapeDtypeStruct((TEST_ROWS, GROUPS * E), bf16),
        ],
        (returned, after_feat, row_weights[3], mlp_up, mlp_down),
        10**9,
    )
    return (train_out, test_out)


def solution(mesh):
    split = Mesh(
        mesh.devices.reshape(2, 4, 4, 2, 2, 2), ("y_lo", "x", "z_hi", "z_lo", "core", "feat")
    )
    rows = ("y_lo", "x", "z_hi", "z_lo", "core")
    return jax.shard_map(
        layer,
        mesh=split,
        in_specs=(P(rows, "feat"), P(rows, "feat"), P(), P(), P(), P()),
        out_specs=(P(rows, "feat"), P(rows, "feat")),
        check_vma=False,
    )
```

profile of v0, /device:TPU:1, one launch (start us, length us, event | category | flops | bytes accessed | tf_op | source)
XLA Modules:
  0.0 112.5 jit_solution(5581549751252305917)
XLA Ops:
  0.6 0.9 pad_maximum_fusion
  1.6 3.8 %collective-permute-start = (bf16[96,768]{1,0:T(8,128)(2,1)S(1)}, bf16[96,768]{1,0:T(8,128)(2,1)S(1)}, u32[]{:S(2)}, u32[]{:S(2)}) collective-permute-start(bf16[96,768]{1,0:T(8,128)(2,1)S(1)} %pad_maximum_fusion), channel_id=1, source_target_pairs={{0,1},{1,0},{2,3},{3,2},{4,5},{5,4},{6,7},{7,6},{8,9},{9,8},{10,11... | collective-permute-start | bytes 442376 | tf_op jit(solution)/shard_map/ppermute | solution.py:352
  5.4 0.0 copy-start
  5.4 0.9 copy-done
  6.3 0.0 copy-start.1
  6.3 0.8 copy-done.1
  7.1 0.0 copy-start.3
  7.1 1.0 copy-done.3
  8.1 0.0 copy-start.4
  8.1 0.7 shard_map.77
  8.8 0.0 collective-permute-done.other_ref
  8.8 0.2 copy-done.4
  9.1 0.0 copy-start.2
  9.1 2.8 %shard_map.78 = (f32[4,96,192]{2,1,0:T(8,128)S(1)}, bf16[4,144,128]{2,1,0:T(8,128)(2,1)S(1)}) custom-call(bf16[96,768]{1,0:T(8,128)(2,1)S(1)} %collective-permute-done.other_ref, bf16[4,192,192]{2,1,0:T(8,128)(2,1)S(1)} %copy-done.4, f32[4,96,192]{2,1,0:T(8,128)S(1)} %get-tuple-element.20.cells_ref, bf16[384,192]{1,0:T(8,128)(2,1)S(1)} %get-tuple-element.21.query_ref, ...), custom_call_target="tpu_custom_call" | custom-call | flops 1000000000 | bytes 1048576 | tf_op jit(solution)/shard_map/pallas_call | solution.py:60
  11.9 7.6 %all_to_all.10.own_ref = bf16[4,144,128]{2,1,0:T(8,128)(2,1)S(1)} all-to-all(bf16[4,144,128]{2,1,0:T(8,128)(2,1)S(1)} %get-tuple-element.24), channel_id=1, replica_groups=mesh['y_lo'=2,'x'=4,'z_hi'=4,'z_lo'=2,'core'=2,'feat'=2] {'y_lo','z_lo'}, dimensions={0} | all-to-all | bytes 294912 | tf_op jit(solution)/shard_map/all_to_all | solution.py:370
  19.5 3.0 %collective-permute-start.4 = (bf16[4,144,128]{2,1,0:T(8,128)(2,1)S(1)}, bf16[4,144,128]{2,1,0:T(8,128)(2,1)S(1)}, u32[]{:S(2)}, u32[]{:S(2)}) collective-permute-start(bf16[4,144,128]{2,1,0:T(8,128)(2,1)S(1)} %all_to_all.10.own_ref), channel_id=1, source_target_pairs={{0,2},{2,0},{1,3},{3,1},{4,6},{6,4},{5,7},{7,5},{8,10},{10,8},{9,1... | collective-permute-start | bytes 442376 | tf_op jit(solution)/shard_map/ppermute | solution.py:375
  22.5 3.1 %collective-permute-start.1 = (bf16[384,128]{1,0:T(8,128)(2,1)S(1)}, bf16[384,128]{1,0:T(8,128)(2,1)S(1)}, u32[]{:S(2)}, u32[]{:S(2)}) collective-permute-start(bf16[384,128]{1,0:T(8,128)(2,1)S(1)} %bitcast.3), channel_id=1, source_target_pairs={{0,8},{8,16},{16,24},{24,0},{1,9},{9,17},{17,25},{25,1},{2,10},{10... | collective-permute-start | bytes 294920 | tf_op jit(solution)/shard_map/ppermute | solution.py:374
  25.5 2.2 %collective-permute-start.2 = (bf16[384,128]{1,0:T(8,128)(2,1)S(1)}, bf16[384,128]{1,0:T(8,128)(2,1)S(1)}, u32[]{:S(2)}, u32[]{:S(2)}) collective-permute-start(bf16[384,128]{1,0:T(8,128)(2,1)S(1)} %bitcast.4), channel_id=1, source_target_pairs={{0,24},{8,0},{16,8},{24,16},{1,25},{9,1},{17,9},{25,17},{2,26},{10... | collective-permute-start | bytes 294920 | tf_op jit(solution)/shard_map/ppermute | solution.py:374
  27.7 4.4 %collective-permute-start.3 = (bf16[384,128]{1,0:T(8,128)(2,1)S(1)}, bf16[384,128]{1,0:T(8,128)(2,1)S(1)}, u32[]{:S(2)}, u32[]{:S(2)}) collective-permute-start(bf16[384,128]{1,0:T(8,128)(2,1)S(1)} %bitcast.5), channel_id=1, source_target_pairs={{0,16},{8,24},{16,0},{24,8},{1,17},{9,25},{17,1},{25,9},{2,18},{10... | collective-permute-start | bytes 294920 | tf_op jit(solution)/shard_map/ppermute | solution.py:374
  32.1 0.0 collective-permute-done.4.other_ref
  32.1 0.0 copy-done.2
  32.1 1.9 %shard_map.79 = (bf16[6,208,768]{2,1,0:T(8,128)(2,1)S(1)}, bf16[192,192]{1,0:T(8,128)(2,1)S(1)}) custom-call(bf16[4,144,128]{2,1,0:T(8,128)(2,1)S(1)} %all_to_all.10.own_ref, bf16[4,144,128]{2,1,0:T(8,128)(2,1)S(1)} %collective-permute-done.4.other_ref, bf16[4,192,192]{2,1,0:T(8,128)(2,1)S(1)} %copy-done.2), custom_call_target="tpu_custom_call" | custom-call | flops 1000000000 | bytes 1048576 | tf_op jit(solution)/shard_map/pallas_call | solution.py:60
  34.0 0.0 collective-permute-done.1.refs_1_
  34.0 2.5 %collective-permute-done.2.refs_2_ = bf16[384,128]{1,0:T(8,128)(2,1)S(1)} collective-permute-done((bf16[384,128]{1,0:T(8,128)(2,1)S(1)}, bf16[384,128]{1,0:T(8,128)(2,1)S(1)}, u32[]{:S(2)}, u32[]{:S(2)}) %collective-permute-start.2) | collective-permute-done | bytes 98336 | tf_op jit(solution)/shard_map/ppermute | solution.py:374
  36.5 2.4 %collective-permute-done.3.refs_3_ = bf16[384,128]{1,0:T(8,128)(2,1)S(1)} collective-permute-done((bf16[384,128]{1,0:T(8,128)(2,1)S(1)}, bf16[384,128]{1,0:T(8,128)(2,1)S(1)}, u32[]{:S(2)}, u32[]{:S(2)}) %collective-permute-start.3) | collective-permute-done | bytes 98336 | tf_op jit(solution)/shard_map/ppermute | solution.py:374
  39.0 1.3 %collective-permute-start.5 = (bf16[1536,128]{1,0:T(8,128)(2,1)S(1)}, bf16[1536,128]{1,0:T(8,128)(2,1)S(1)}, u32[]{:S(2)}, u32[]{:S(2)}) collective-permute-start(bf16[1536,128]{1,0:T(8,128)(2,1)S(1)} %shard_map.80.refs_0_.first_ref), channel_id=1, source_target_pairs={{0,32},{32,64},{64,96},{96,0},{1,33},{33,65},{65,97},{97,1},{2,34}... | collective-permute-start | bytes 1179656 | tf_op jit(solution)/shard_map/ppermute | solution.py:393
  40.3 1.5 %collective-permute-start.6 = (bf16[1536,128]{1,0:T(8,128)(2,1)S(1)}, bf16[1536,128]{1,0:T(8,128)(2,1)S(1)}, u32[]{:S(2)}, u32[]{:S(2)}) collective-permute-start(bf16[1536,128]{1,0:T(8,128)(2,1)S(1)} %shard_map.80.refs_0_.first_ref), channel_id=1, source_target_pairs={{0,96},{32,0},{64,32},{96,64},{1,97},{33,1},{65,33},{97,65},{2,98}... | collective-permute-start | bytes 1179656 | tf_op jit(solution)/shard_map/ppermute | solution.py:394
  41.8 4.2 %shard_map.81.refs_3_ = f32[6,48,768]{2,1,0:T(8,128)S(1)} custom-call(bf16[1536,128]{1,0:T(8,128)(2,1)S(1)} %shard_map.80.refs_0_.first_ref, bf16[192,192]{1,0:T(8,128)(2,1)S(1)} %get-tuple-element.30.refs_1_.wv_ref, bf16[6,208,768]{2,1,0:T(8,128)(2,1)S(1)} %get-tuple-element.31.refs_2_.folded_ref), custom_call_target="tpu_custom_call" | custom-call | flops 3623878656 | bytes 1048576 | tf_op jit(solution)/shard_map/pallas_call | solution.py:60
  46.1 4.0 %collective-permute-done.5.refs_0_.second_ref = bf16[1536,128]{1,0:T(8,128)(2,1)S(1)} collective-permute-done((bf16[1536,128]{1,0:T(8,128)(2,1)S(1)}, bf16[1536,128]{1,0:T(8,128)(2,1)S(1)}, u32[]{:S(2)}, u32[]{:S(2)}) %collective-permute-start.5) | collective-permute-done | bytes 393248 | tf_op jit(solution)/shard_map/ppermute | solution.py:393
  50.1 0.0 collective-permute-done.6.refs_0_.third_ref
  50.1 4.2 %shard_map.82.refs_3_ = f32[6,48,768]{2,1,0:T(8,128)S(1)} custom-call(bf16[1536,128]{1,0:T(8,128)(2,1)S(1)} %collective-permute-done.5.refs_0_.second_ref, bf16[192,192]{1,0:T(8,128)(2,1)S(1)} %get-tuple-element.30.refs_1_.wv_ref, bf16[6,208,768]{2,1,0:T(8,128)(2,1)S(1)} %get-tuple-element.31.refs_2_.folded_ref, f32[6,48,768]{2,1,0:T(8,128)S(1)} %shard_map.81.refs_3_), custom_call_target="tpu_custom_call" | custom-call | flops 3623878656 | bytes 1048576 | tf_op jit(solution)/shard_map/pallas_call | solution.py:60
  54.4 1.0 collective-permute-start.7
  55.4 2.0 %collective-permute-start.8 = (bf16[768,128]{1,0:T(8,128)(2,1)S(1)}, bf16[768,128]{1,0:T(8,128)(2,1)S(1)}, u32[]{:S(2)}, u32[]{:S(2)}) collective-permute-start(bf16[768,128]{1,0:T(8,128)(2,1)S(1)} %slice.14), channel_id=1, source_target_pairs={{0,96},{32,0},{64,32},{96,64},{1,97},{33,1},{65,33},{97,65},{2,98}... | collective-permute-start | bytes 589832 | tf_op jit(solution)/shard_map/ppermute | solution.py:398
  57.4 4.2 %shard_map.83.mix_ref = f32[6,48,768]{2,1,0:T(8,128)S(1)} custom-call(bf16[1536,128]{1,0:T(8,128)(2,1)S(1)} %collective-permute-done.6.refs_0_.third_ref, bf16[192,192]{1,0:T(8,128)(2,1)S(1)} %get-tuple-element.30.refs_1_.wv_ref, bf16[6,208,768]{2,1,0:T(8,128)(2,1)S(1)} %get-tuple-element.31.refs_2_.folded_ref, f32[6,48,768]{2,1,0:T(8,128)S(1)} %shard_map.82.refs_3_), custom_call_target="tpu_custom_call" | custom-call | flops 3623878656 | bytes 1048576 | tf_op jit(solution)/shard_map/pallas_call | solution.py:60
  61.7 0.0 copy-start.6
  61.7 0.0 collective-permute-done.7.left_ref
  61.7 0.0 collective-permute-done.8.right_ref
  61.7 36.5 %shard_map.84 = (f32[6,40,384]{2,1,0:T(8,128)S(1)}, f32[6,40,384]{2,1,0:T(8,128)S(1)}) custom-call(bf16[768,128]{1,0:T(8,128)(2,1)S(1)} %collective-permute-done.7.left_ref, bf16[768,128]{1,0:T(8,128)(2,1)S(1)} %collective-permute-done.8.right_ref, bf16[192,192]{1,0:T(8,128)(2,1)S(1)} %get-tuple-element.30.refs_1_.wv_ref, ...), custom_call_target="tpu_custom_call" | custom-call | flops 3623878656 | bytes 1048576 | tf_op jit(solution)/shard_map/pallas_call | solution.py:60
  98.2 0.0 copy-start.5
  98.2 2.4 %collective-permute-start.9 = (f32[6,40,384]{2,1,0:T(8,128)S(1)}, f32[6,40,384]{2,1,0:T(8,128)S(1)}, u32[]{:S(2)}, u32[]{:S(2)}) collective-permute-start(f32[6,40,384]{2,1,0:T(8,128)S(1)} %get-tuple-element.36), channel_id=1, source_target_pairs={{0,2},{2,0},{1,3},{3,1},{4,6},{6,4},{5,7},{7,5},{8,10},{10,8},{9,1... | collective-permute-start | bytes 1105928 | tf_op jit(solution)/shard_map/ppermute | solution.py:404
  100.6 0.0 copy-done.6
  100.6 0.2 copy.8.down_ref
  100.8 1.1 %collective-permute-done.9.came_ref = f32[6,40,384]{2,1,0:T(8,128)S(1)} collective-permute-done((f32[6,40,384]{2,1,0:T(8,128)S(1)}, f32[6,40,384]{2,1,0:T(8,128)S(1)}, u32[]{:S(2)}, u32[]{:S(2)}) %collective-permute-start.9) | collective-permute-done | bytes 368672 | tf_op jit(solution)/shard_map/ppermute | solution.py:404
  101.9 0.9 shard_map.85
  102.8 3.7 %all-to-all-start.1 = ((bf16[4,144,128]{2,1,0:T(8,128)(2,1)}), bf16[4,144,128]{2,1,0:T(8,128)(2,1)S(1)}, u32[]{:S(2)}, u32[]{:S(2)}) async-start(bf16[4,144,128]{2,1,0:T(8,128)(2,1)} %shard_map.85), calls=%async_computation.1 | async-start | bytes 294912 | tf_op jit(solution)/shard_map/all_to_all | solution.py:408
  106.5 4.3 %all-to-all-done.1.came_ref = bf16[4,144,128]{2,1,0:T(8,128)(2,1)S(1)} async-done(((bf16[4,144,128]{2,1,0:T(8,128)(2,1)}), bf16[4,144,128]{2,1,0:T(8,128)(2,1)S(1)}, u32[]{:S(2)}, u32[]{:S(2)}) %all-to-all-start.1) | async-done | bytes 147488 | tf_op jit(solution)/shard_map/all_to_all | solution.py:408
  110.8 0.0 copy-done.5
  110.8 1.7 %shard_map.86 = (bf16[64,768]{1,0:T(8,128)(2,1)}, bf16[32,768]{1,0:T(8,128)(2,1)}) custom-call(bf16[4,144,128]{2,1,0:T(8,128)(2,1)S(1)} %all-to-all-done.1.came_ref, f32[4,96,192]{2,1,0:T(8,128)S(1)} %get-tuple-element.37.after_ref, bf16[192,192]{1,0:T(8,128)(2,1)S(1)} %slice_bitcast_fusion.wo_ref, bf16[192,768]{1,0:T(8,128)(2,1)S(1)} %copy-done.5, ...), custom_call_target="tpu_custom_call" | custom-call | flops 1000000000 | bytes 1048576 | tf_op jit(solution)/shard_map/pallas_call | solution.py:60
  (5 shorter events, 0.1 us)
Async XLA Ops:
  1.6 7.3 %collective-permute-start = (bf16[96,768]{1,0:T(8,128)(2,1)S(1)}, bf16[96,768]{1,0:T(8,128)(2,1)S(1)}, u32[]{:S(2)}, u32[]{:S(2)}) collective-permute-start(bf16[96,768]{1,0:T(8,128)(2,1)S(1)} %pad_maximum_fusion), channel_id=1, source_target_pairs={{0,1},{1,0},{2,3},{3,2},{4,5},{5,4},{6,7},{7,6},{8,9},{9,8},{10,11... | collective-permute-start | bytes 442376 | tf_op jit(solution)/shard_map/ppermute | solution.py:352
  5.4 0.9 copy-start
  6.3 0.8 copy-start.1
  7.1 1.0 copy-start.3
  8.1 1.0 copy-start.4
  9.1 23.0 %copy-start.2 = (bf16[4,192,192]{2,1,0:T(8,128)(2,1)S(1)}, bf16[4,192,192]{2,1,0:T(8,128)(2,1)}, u32[]{:S(2)}) copy-start(bf16[4,192,192]{2,1,0:T(8,128)(2,1)} %weights_ref.5) | copy-start | bytes 884740
  19.5 12.6 %collective-permute-start.4 = (bf16[4,144,128]{2,1,0:T(8,128)(2,1)S(1)}, bf16[4,144,128]{2,1,0:T(8,128)(2,1)S(1)}, u32[]{:S(2)}, u32[]{:S(2)}) collective-permute-start(bf16[4,144,128]{2,1,0:T(8,128)(2,1)S(1)} %all_to_all.10.own_ref), channel_id=1, source_target_pairs={{0,2},{2,0},{1,3},{3,1},{4,6},{6,4},{5,7},{7,5},{8,10},{10,8},{9,1... | collective-permute-start | bytes 442376 | tf_op jit(solution)/shard_map/ppermute | solution.py:375
  22.5 11.6 %collective-permute-start.1 = (bf16[384,128]{1,0:T(8,128)(2,1)S(1)}, bf16[384,128]{1,0:T(8,128)(2,1)S(1)}, u32[]{:S(2)}, u32[]{:S(2)}) collective-permute-start(bf16[384,128]{1,0:T(8,128)(2,1)S(1)} %bitcast.3), channel_id=1, source_target_pairs={{0,8},{8,16},{16,24},{24,0},{1,9},{9,17},{17,25},{25,1},{2,10},{10... | collective-permute-start | bytes 294920 | tf_op jit(solution)/shard_map/ppermute | solution.py:374
  25.5 11.0 %collective-permute-start.2 = (bf16[384,128]{1,0:T(8,128)(2,1)S(1)}, bf16[384,128]{1,0:T(8,128)(2,1)S(1)}, u32[]{:S(2)}, u32[]{:S(2)}) collective-permute-start(bf16[384,128]{1,0:T(8,128)(2,1)S(1)} %bitcast.4), channel_id=1, source_target_pairs={{0,24},{8,0},{16,8},{24,16},{1,25},{9,1},{17,9},{25,17},{2,26},{10... | collective-permute-start | bytes 294920 | tf_op jit(solution)/shard_map/ppermute | solution.py:374
  27.7 11.2 %collective-permute-start.3 = (bf16[384,128]{1,0:T(8,128)(2,1)S(1)}, bf16[384,128]{1,0:T(8,128)(2,1)S(1)}, u32[]{:S(2)}, u32[]{:S(2)}) collective-permute-start(bf16[384,128]{1,0:T(8,128)(2,1)S(1)} %bitcast.5), channel_id=1, source_target_pairs={{0,16},{8,24},{16,0},{24,8},{1,17},{9,25},{17,1},{25,9},{2,18},{10... | collective-permute-start | bytes 294920 | tf_op jit(solution)/shard_map/ppermute | solution.py:374
  39.0 11.1 %collective-permute-start.5 = (bf16[1536,128]{1,0:T(8,128)(2,1)S(1)}, bf16[1536,128]{1,0:T(8,128)(2,1)S(1)}, u32[]{:S(2)}, u32[]{:S(2)}) collective-permute-start(bf16[1536,128]{1,0:T(8,128)(2,1)S(1)} %shard_map.80.refs_0_.first_ref), channel_id=1, source_target_pairs={{0,32},{32,64},{64,96},{96,0},{1,33},{33,65},{65,97},{97,1},{2,34}... | collective-permute-start | bytes 1179656 | tf_op jit(solution)/shard_map/ppermute | solution.py:393
  40.3 9.8 %collective-permute-start.6 = (bf16[1536,128]{1,0:T(8,128)(2,1)S(1)}, bf16[1536,128]{1,0:T(8,128)(2,1)S(1)}, u32[]{:S(2)}, u32[]{:S(2)}) collective-permute-start(bf16[1536,128]{1,0:T(8,128)(2,1)S(1)} %shard_map.80.refs_0_.first_ref), channel_id=1, source_target_pairs={{0,96},{32,0},{64,32},{96,64},{1,97},{33,1},{65,33},{97,65},{2,98}... | collective-permute-start | bytes 1179656 | tf_op jit(solution)/shard_map/ppermute | solution.py:394
  54.4 7.3 %collective-permute-start.7 = (bf16[768,128]{1,0:T(8,128)(2,1)S(1)}, bf16[768,128]{1,0:T(8,128)(2,1)S(1)}, u32[]{:S(2)}, u32[]{:S(2)}) collective-permute-start(bf16[768,128]{1,0:T(8,128)(2,1)S(1)} %slice.13), channel_id=1, source_target_pairs={{0,32},{32,64},{64,96},{96,0},{1,33},{33,65},{65,97},{97,1},{2,34}... | collective-permute-start | bytes 589832 | tf_op jit(solution)/shard_map/ppermute | solution.py:397
  55.4 6.3 %collective-permute-start.8 = (bf16[768,128]{1,0:T(8,128)(2,1)S(1)}, bf16[768,128]{1,0:T(8,128)(2,1)S(1)}, u32[]{:S(2)}, u32[]{:S(2)}) collective-permute-start(bf16[768,128]{1,0:T(8,128)(2,1)S(1)} %slice.14), channel_id=1, source_target_pairs={{0,96},{32,0},{64,32},{96,64},{1,97},{33,1},{65,33},{97,65},{2,98}... | collective-permute-start | bytes 589832 | tf_op jit(solution)/shard_map/ppermute | solution.py:398
  61.7 39.0 %copy-start.6 = (bf16[768,192]{0,1:T(8,128)(2,1)S(1)}, bf16[768,192]{0,1:T(8,128)(2,1)}, u32[]{:S(2)}) copy-start(bf16[768,192]{0,1:T(8,128)(2,1)} %param.11) | copy-start | bytes 884740
  98.2 12.5 %copy-start.5 = (bf16[192,768]{1,0:T(8,128)(2,1)S(1)}, bf16[192,768]{1,0:T(8,128)(2,1)}, u32[]{:S(2)}) copy-start(bf16[192,768]{1,0:T(8,128)(2,1)} %up_ref.1) | copy-start | bytes 884740
  98.2 3.7 %collective-permute-start.9 = (f32[6,40,384]{2,1,0:T(8,128)S(1)}, f32[6,40,384]{2,1,0:T(8,128)S(1)}, u32[]{:S(2)}, u32[]{:S(2)}) collective-permute-start(f32[6,40,384]{2,1,0:T(8,128)S(1)} %get-tuple-element.36), channel_id=1, source_target_pairs={{0,2},{2,0},{1,3},{3,1},{4,6},{6,4},{5,7},{7,5},{8,10},{10,8},{9,1... | collective-permute-start | bytes 1105928 | tf_op jit(solution)/shard_map/ppermute | solution.py:404
  102.8 8.0 %all-to-all-start.1 = ((bf16[4,144,128]{2,1,0:T(8,128)(2,1)}), bf16[4,144,128]{2,1,0:T(8,128)(2,1)S(1)}, u32[]{:S(2)}, u32[]{:S(2)}) async-start(bf16[4,144,128]{2,1,0:T(8,128)(2,1)} %shard_map.85), calls=%async_computation.1 | async-start | bytes 294912 | tf_op jit(solution)/shard_map/all_to_all | solution.py:408
where the time goes:
time: 113 us; the launch traced here: 112 us
  Pallas kernels  57.2 us (51%)
  starting transfers between devices  28.4 us (25%)
  waiting for transfers between devices  14.4 us (13%)
  blocking collectives  7.62 us (7%)
  local copies, waits for them, and re-layouts  3.15 us (3%)
    pallas_call x10, Pallas kernels, call(): pl.pallas_call(kernel, out_shape=outs, in_specs=[in_vmem] * len(args), ou...  57.2 us
    ppermute x3, starting transfers between devices, layer(): column.append(lax.ppermute(keys, 'z_hi', shift(SIDE, by)))  9.65 us
    all_to_all x1, blocking collectives, layer(): lax.all_to_all(pieces, classes, split_axis=0, concat_axis=0, tiled=True)  7.62 us
    ppermute x3, waiting for transfers between devices, layer(): column.append(lax.ppermute(keys, 'z_hi', shift(SIDE, by)))  4.93 us
    all_to_all x1, waiting for transfers between devices, layer(): lax.all_to_all(mixed, classes, split_axis=0, concat_axis=0, tiled=True)  4.3 us
    ppermute x1, waiting for transfers between devices, layer(): above = lax.ppermute(keys, 'x', shift(4, 1))  4.03 us
    ppermute x1, starting transfers between devices, layer(): other = lax.ppermute(joined, 'feat', swap)  3.82 us
    all_to_all x1, starting transfers between devices, layer(): lax.all_to_all(mixed, classes, split_axis=0, concat_axis=0, tiled=True)  3.66 us
  transfers between devices with their start and end apart: 11, of which 5 were waited for; matrix products, arithmetic and copies ran while one was open for 0% of the time, Pallas kernels for 10%

commit v1 on v0

--- a/solution.py
+++ b/solution.py
@@ -169,10 +169,19 @@
         folded_ref[head, E:, :] = jnp.where(row == 0, -peak, 0.0).astype(bf16)
 
 
-def stack_kernel(*refs):
-    height = GROUPS * TRAIN_PACK
-    for index in range(SIDE):
-        refs[-1][index * height : (index + 1) * height, :] = refs[index][...]
+def stack_kernel(upper_ref, lower_ref, both_ref):
+    both_ref[: BLOCK // 4, :] = upper_ref[...]
+    both_ref[BLOCK // 4 :, :] = lower_ref[...]
+
+
+def stack(upper, lower):
+    return call(
+        stack_kernel,
+        [jax.ShapeDtypeStruct((BLOCK // 2, LANES), bf16)],
+        (upper, lower),
+        10**6,
+        limit=4,
+    )[0]
 
 
 def unpack_keys(packed_refs, keys_ref):
@@ -213,27 +222,13 @@
         work(head)
 
 
-def attend_last_kernel(
-    left_ref,
-    right_ref,
-    wv_ref,
-    folded_ref,
-    mix_ref,
-    first_ref,
-    second_ref,
-    third_ref,
-    stay_ref,
-    leave_ref,
-    keys_ref,
-    values_ref,
-    total_ref,
-    peak_ref,
-    blocks_ref,
-    scores_ref,
-):
+def attend_last_kernel(*refs):
+    packed_refs = refs[: 2 * SIDE]
+    wv_ref, folded_ref, mix_ref, stay_ref, leave_ref = refs[2 * SIDE : 2 * SIDE + 5]
+    keys_ref, values_ref, total_ref, peak_ref, blocks_ref, scores_ref = refs[2 * SIDE + 5 :]
     attend_kernel(
         False,
-        (left_ref, right_ref),
+        packed_refs[:2],
         (wv_ref, folded_ref, mix_ref, total_ref, keys_ref, values_ref),
     )
     for head in range(HEADS):
@@ -242,10 +237,9 @@
 
     @pl.when(jnp.max(over) > 0.0)
     def _():
-        for index, one_ref in enumerate((first_ref, second_ref, third_ref)):
-            blocks_ref[index] = one_ref[...]
-        blocks_ref[SIDE - 1, : BLOCK // 2] = left_ref[...]
-        blocks_ref[SIDE - 1, BLOCK // 2 :] = right_ref[...]
+        for index, one_ref in enumerate(packed_refs):
+            span = slice(index % 2 * BLOCK // 2, (index % 2 + 1) * BLOCK // 2)
+            blocks_ref[index // 2, span] = one_ref[...]
         peak_ref[...] = jnp.full(peak_ref.shape, far_below, f32)
         total_ref[...] = jnp.zeros(total_ref.shape, f32)
 
@@ -283,9 +277,9 @@
 
 
 def attend(args):
-    first = len(args) == 3
+    first = len(args) == 4
     return call(
-        lambda *refs: attend_kernel(first, refs[:1], refs[1:]),
+        lambda *refs: attend_kernel(first, refs[:2], refs[2:]),
         [mix_shape],
         args,
         attend_flops,
@@ -373,6 +367,9 @@
     for by in (1, 3, 2):
         column.append(lax.ppermute(keys, "z_hi", shift(SIDE, by)))
     received_other = lax.ppermute(received, "core", swap)
+    early = stack(*column[:2])
+    early_above = lax.ppermute(early, "x", shift(4, 1))
+    early_below = lax.ppermute(early, "x", shift(4, 3))
     folded, value_turned = call(
         fold_kernel,
         [
@@ -382,25 +379,18 @@
         (received, received_other, row_weights),
         10**9,
     )
-    column, folded = lax.optimization_barrier((column, folded))
-    keys = call(
-        stack_kernel,
-        [jax.ShapeDtypeStruct((SIDE * GROUPS * TRAIN_PACK, LANES), bf16)],
-        column,
-        10**6,
-        limit=4,
-    )[0]
-    above = lax.ppermute(keys, "x", shift(4, 1))
-    below = lax.ppermute(keys, "x", shift(4, 3))
-    mix = attend((keys, value_turned, folded))
-    mix, above, below = lax.optimization_barrier((mix, above, below))
-    far_above = lax.ppermute(above[: BLOCK // 2], "x", shift(4, 1))
-    far_below_keys = lax.ppermute(below[BLOCK // 2 :], "x", shift(4, 3))
-    mix = attend((above, value_turned, folded, mix))
-    mix = attend((below, value_turned, folded, mix))
-    stay, leave = attend_last(
-        (far_above, far_below_keys, value_turned, folded, mix, keys, above, below)
-    )
+    column, folded = lax.optimization_barrier((column[2:], folded))
+    late = stack(*column)
+    late_above = lax.ppermute(late, "x", shift(4, 1))
+    late_below = lax.ppermute(late, "x", shift(4, 3))
+    mix = attend((early, late, value_turned, folded))
+    mix, early_above, late_below = lax.optimization_barrier((mix, early_above, late_below))
+    far_early = lax.ppermute(early_above, "x", shift(4, 1))
+    far_late = lax.ppermute(late_below, "x", shift(4, 3))
+    mix = attend((early_above, early_below, value_turned, folded, mix))
+    mix = attend((late_above, late_below, value_turned, folded, mix))
+    packed = (far_early, far_late, early, late, early_above, early_below, late_above, late_below)
+    stay, leave = attend_last(packed + (value_turned, folded, mix))
     came = lax.ppermute(leave, "core", swap)
     mixed = call(
         merge_kernel, [jax.ShapeDtypeStruct((GROUPS, PACK, LANES), bf16)], (stay, came), 10**7

time: 113 us -> 108 us (0.956)
  waiting for transfers between devices: 14.4 us -> 7.82 us
  starting transfers between devices: 28.4 us -> 30.3 us
    ppermute x4 -> x6, waiting for transfers between devices: 4.04 us -> 0.02 us  [the longest x1 0.01 us: layer(): early_above = lax.ppermute(early, 'x', shift(4, 1))]
    ppermute x3, waiting for transfers between devices: 4.93 us -> 2.16 us  [layer(): column.append(lax.ppermute(keys, 'z_hi', shift(SIDE, by)))]
    ppermute x4 -> x6, starting transfers between devices: 5.88 us -> 8.15 us  [the longest x1 2.55 us: layer(): late_below = lax.ppermute(late, 'x', shift(4, 3))]
    pallas_call x10 -> x11, Pallas kernels: 57.2 us -> 57.4 us  [call(): pl.pallas_call(kernel, out_shape=outs, in_specs=[in_vmem] * len(args), ou...]
  transfers between devices with their start and end apart: 11 -> 13, of which waited for: 5 -> 3; matrix products, arithmetic and copies ran while one was open for 0% -> 0% of each run, Pallas kernels for 10% -> 14%
where the time goes in v1:
time: 108 us
  Pallas kernels  57.4 us (53%)
  starting transfers between devices  30.3 us (28%)
  waiting for transfers between devices  7.82 us (7%)
  blocking collectives  7.62 us (7%)
  local copies, waits for them, and re-layouts  3.12 us (3%)
    pallas_call x11, Pallas kernels, call(): pl.pallas_call(kernel, out_shape=outs, in_specs=[in_vmem] * len(args), ou...  57.4 us
    ppermute x3, starting transfers between devices, layer(): column.append(lax.ppermute(keys, 'z_hi', shift(SIDE, by)))  9.65 us
    all_to_all x1, blocking collectives, layer(): lax.all_to_all(pieces, classes, split_axis=0, concat_axis=0, tiled=True)  7.62 us
    all_to_all x1, waiting for transfers between devices, layer(): lax.all_to_all(mixed, classes, split_axis=0, concat_axis=0, tiled=True)  4.5 us
    all_to_all x1, starting transfers between devices, layer(): lax.all_to_all(mixed, classes, split_axis=0, concat_axis=0, tiled=True)  3.88 us
    ppermute x1, starting transfers between devices, layer(): other = lax.ppermute(joined, 'feat', swap)  3.82 us
    unnamed x15, local copies, waits for them, and re-layouts  3.11 us
    ppermute x1, starting transfers between devices, layer(): received_other = lax.ppermute(received, 'core', swap)  2.96 us
  transfers between devices with their start and end apart: 13, of which 3 were waited for; matrix products, arithmetic and copies ran while one was open for 0% of the time, Pallas kernels for 14%

profile of v1, /device:TPU:1, one launch (start us, length us, event | category | flops | bytes accessed | tf_op | source)
XLA Modules:
  0.0 108.0 jit_solution(11158804635705948718)
XLA Ops:
  0.6 0.9 pad_maximum_fusion
  1.6 3.8 %collective-permute-start = (bf16[96,768]{1,0:T(8,128)(2,1)S(1)}, bf16[96,768]{1,0:T(8,128)(2,1)S(1)}, u32[]{:S(2)}, u32[]{:S(2)}) collective-permute-start(bf16[96,768]{1,0:T(8,128)(2,1)S(1)} %pad_maximum_fusion), channel_id=1, source_target_pairs={{0,1},{1,0},{2,3},{3,2},{4,5},{5,4},{6,7},{7,6},{8,9},{9,8},{10,11... | collective-permute-start | bytes 442376 | tf_op jit(solution)/shard_map/ppermute | solution.py:346
  5.4 0.0 copy-start
  5.4 0.9 copy-done
  6.3 0.8 copy-done.1
  7.1 1.0 copy-done.3
  8.1 0.7 shard_map.77
  8.8 0.0 collective-permute-done.other_ref
  8.8 0.2 copy-done.4
  9.1 2.8 %shard_map.78 = (f32[4,96,192]{2,1,0:T(8,128)S(1)}, bf16[4,144,128]{2,1,0:T(8,128)(2,1)S(1)}) custom-call(bf16[96,768]{1,0:T(8,128)(2,1)S(1)} %collective-permute-done.other_ref, bf16[4,192,192]{2,1,0:T(8,128)(2,1)S(1)} %copy-done.4, f32[4,96,192]{2,1,0:T(8,128)S(1)} %get-tuple-element.18.cells_ref, bf16[384,192]{1,0:T(8,128)(2,1)S(1)} %get-tuple-element.19.query_ref, ...), custom_call_target="tpu_custom_call" | custom-call | flops 1000000000 | bytes 1048576 | tf_op jit(solution)/shard_map/pallas_call | solution.py:60
  11.9 7.6 %all_to_all.10.own_ref = bf16[4,144,128]{2,1,0:T(8,128)(2,1)S(1)} all-to-all(bf16[4,144,128]{2,1,0:T(8,128)(2,1)S(1)} %get-tuple-element.22), channel_id=1, replica_groups=mesh['y_lo'=2,'x'=4,'z_hi'=4,'z_lo'=2,'core'=2,'feat'=2] {'y_lo','z_lo'}, dimensions={0} | all-to-all | bytes 294912 | tf_op jit(solution)/shard_map/all_to_all | solution.py:364
  19.5 3.0 %collective-permute-start.4 = (bf16[4,144,128]{2,1,0:T(8,128)(2,1)S(1)}, bf16[4,144,128]{2,1,0:T(8,128)(2,1)S(1)}, u32[]{:S(2)}, u32[]{:S(2)}) collective-permute-start(bf16[4,144,128]{2,1,0:T(8,128)(2,1)S(1)} %all_to_all.10.own_ref), channel_id=1, source_target_pairs={{0,2},{2,0},{1,3},{3,1},{4,6},{6,4},{5,7},{7,5},{8,10},{10,8},{9,1... | collective-permute-start | bytes 442376 | tf_op jit(solution)/shard_map/ppermute | solution.py:369
  22.5 3.1 %collective-permute-start.1 = (bf16[384,128]{1,0:T(8,128)(2,1)S(1)}, bf16[384,128]{1,0:T(8,128)(2,1)S(1)}, u32[]{:S(2)}, u32[]{:S(2)}) collective-permute-start(bf16[384,128]{1,0:T(8,128)(2,1)S(1)} %bitcast.3), channel_id=1, source_target_pairs={{0,8},{8,16},{16,24},{24,0},{1,9},{9,17},{17,25},{25,1},{2,10},{10... | collective-permute-start | bytes 294920 | tf_op jit(solution)/shard_map/ppermute | solution.py:368
  25.5 2.2 %collective-permute-start.2 = (bf16[384,128]{1,0:T(8,128)(2,1)S(1)}, bf16[384,128]{1,0:T(8,128)(2,1)S(1)}, u32[]{:S(2)}, u32[]{:S(2)}) collective-permute-start(bf16[384,128]{1,0:T(8,128)(2,1)S(1)} %bitcast.4), channel_id=1, source_target_pairs={{0,24},{8,0},{16,8},{24,16},{1,25},{9,1},{17,9},{25,17},{2,26},{10... | collective-permute-start | bytes 294920 | tf_op jit(solution)/shard_map/ppermute | solution.py:368
  27.7 4.4 %collective-permute-start.3 = (bf16[384,128]{1,0:T(8,128)(2,1)S(1)}, bf16[384,128]{1,0:T(8,128)(2,1)S(1)}, u32[]{:S(2)}, u32[]{:S(2)}) collective-permute-start(bf16[384,128]{1,0:T(8,128)(2,1)S(1)} %bitcast.5), channel_id=1, source_target_pairs={{0,16},{8,24},{16,0},{24,8},{1,17},{9,25},{17,1},{25,9},{2,18},{10... | collective-permute-start | bytes 294920 | tf_op jit(solution)/shard_map/ppermute | solution.py:368
  32.1 0.0 collective-permute-done.1.lower_ref
  32.1 1.3 %collective-permute-start.5 = (bf16[768,128]{1,0:T(8,128)(2,1)S(1)}, bf16[768,128]{1,0:T(8,128)(2,1)S(1)}, u32[]{:S(2)}, u32[]{:S(2)}) collective-permute-start(bf16[768,128]{1,0:T(8,128)(2,1)S(1)} %shard_map.79.refs_0_.refs_2_), channel_id=1, source_target_pairs={{0,32},{32,64},{64,96},{96,0},{1,33},{33,65},{65,97},{97,1},{2,34}... | collective-permute-start | bytes 589832 | tf_op jit(solution)/shard_map/ppermute | solution.py:371
  33.4 1.5 %collective-permute-start.9 = (bf16[768,128]{1,0:T(8,128)(2,1)S(1)}, bf16[768,128]{1,0:T(8,128)(2,1)S(1)}, u32[]{:S(2)}, u32[]{:S(2)}) collective-permute-start(bf16[768,128]{1,0:T(8,128)(2,1)S(1)} %shard_map.79.refs_0_.refs_2_), channel_id=1, source_target_pairs={{0,96},{32,0},{64,32},{96,64},{1,97},{33,1},{65,33},{97,65},{2,98}... | collective-permute-start | bytes 589832 | tf_op jit(solution)/shard_map/ppermute | solution.py:372
  34.9 0.0 collective-permute-done.4.other_ref
  34.9 0.0 copy-done.2
  34.9 1.9 %shard_map.80 = (bf16[6,208,768]{2,1,0:T(8,128)(2,1)S(1)}, bf16[192,192]{1,0:T(8,128)(2,1)S(1)}) custom-call(bf16[4,144,128]{2,1,0:T(8,128)(2,1)S(1)} %all_to_all.10.own_ref, bf16[4,144,128]{2,1,0:T(8,128)(2,1)S(1)} %collective-permute-done.4.other_ref, bf16[4,192,192]{2,1,0:T(8,128)(2,1)S(1)} %copy-done.2), custom_call_target="tpu_custom_call" | custom-call | flops 1000000000 | bytes 1048576 | tf_op jit(solution)/shard_map/pallas_call | solution.py:60
  36.8 0.0 collective-permute-done.2.upper_ref
  36.8 2.2 %collective-permute-done.3.lower_ref = bf16[384,128]{1,0:T(8,128)(2,1)S(1)} collective-permute-done((bf16[384,128]{1,0:T(8,128)(2,1)S(1)}, bf16[384,128]{1,0:T(8,128)(2,1)S(1)}, u32[]{:S(2)}, u32[]{:S(2)}) %collective-permute-start.3) | collective-permute-done | bytes 98336 | tf_op jit(solution)/shard_map/ppermute | solution.py:368
  39.0 2.6 %collective-permute-start.6 = (bf16[768,128]{1,0:T(8,128)(2,1)S(1)}, bf16[768,128]{1,0:T(8,128)(2,1)S(1)}, u32[]{:S(2)}, u32[]{:S(2)}) collective-permute-start(bf16[768,128]{1,0:T(8,128)(2,1)S(1)} %shard_map.81.refs_1_.refs_3_), channel_id=1, source_target_pairs={{0,96},{32,0},{64,32},{96,64},{1,97},{33,1},{65,33},{97,65},{2,98}... | collective-permute-start | bytes 589832 | tf_op jit(solution)/shard_map/ppermute | solution.py:385
  41.5 0.0 collective-permute-start.10
  41.5 4.2 %shard_map.82.refs_4_ = f32[6,48,768]{2,1,0:T(8,128)S(1)} custom-call(bf16[768,128]{1,0:T(8,128)(2,1)S(1)} %shard_map.79.refs_0_.refs_2_, bf16[768,128]{1,0:T(8,128)(2,1)S(1)} %shard_map.81.refs_1_.refs_3_, bf16[192,192]{1,0:T(8,128)(2,1)S(1)} %get-tuple-element.26.refs_2_.refs_8_, bf16[6,208,768]{2,1,0:T(8,128)(2,1)S(1)} %get-tuple-element.27.refs_3_.refs_9_), custom_call_target="tpu_custom_call" | custom-call | flops 3623878656 | bytes 1048576 | tf_op jit(solution)/shard_map/pallas_call | solution.py:60
  45.8 0.0 collective-permute-done.5.refs_0_.refs_4_
  45.8 0.0 collective-permute-done.6.refs_1_.refs_7_
  45.8 0.3 collective-permute-start.7
  46.1 2.5 %collective-permute-start.8 = (bf16[768,128]{1,0:T(8,128)(2,1)S(1)}, bf16[768,128]{1,0:T(8,128)(2,1)S(1)}, u32[]{:S(2)}, u32[]{:S(2)}) collective-permute-start(bf16[768,128]{1,0:T(8,128)(2,1)S(1)} %collective-permute-done.6.refs_1_.refs_7_), channel_id=1, source_target_pairs={{0,96},{32,0},{64,32},{96,64},{1,97},{33,1},{65,33},{97,65},{2,98}... | collective-permute-start | bytes 589832 | tf_op jit(solution)/shard_map/ppermute | solution.py:389
  48.6 0.0 collective-permute-done.9.refs_1_.refs_5_
  48.6 4.2 %shard_map.83.refs_4_ = f32[6,48,768]{2,1,0:T(8,128)S(1)} custom-call(bf16[768,128]{1,0:T(8,128)(2,1)S(1)} %collective-permute-done.5.refs_0_.refs_4_, bf16[768,128]{1,0:T(8,128)(2,1)S(1)} %collective-permute-done.9.refs_1_.refs_5_, bf16[192,192]{1,0:T(8,128)(2,1)S(1)} %get-tuple-element.26.refs_2_.refs_8_, ...), custom_call_target="tpu_custom_call" | custom-call | flops 3623878656 | bytes 1048576 | tf_op jit(solution)/shard_map/pallas_call | solution.py:60
  52.9 0.0 collective-permute-done.10.refs_0_.refs_6_
  52.9 4.2 %shard_map.84.refs_10_ = f32[6,48,768]{2,1,0:T(8,128)S(1)} custom-call(bf16[768,128]{1,0:T(8,128)(2,1)S(1)} %collective-permute-done.10.refs_0_.refs_6_, bf16[768,128]{1,0:T(8,128)(2,1)S(1)} %collective-permute-done.6.refs_1_.refs_7_, bf16[192,192]{1,0:T(8,128)(2,1)S(1)} %get-tuple-element.26.refs_2_.refs_8_, ...), custom_call_target="tpu_custom_call" | custom-call | flops 3623878656 | bytes 1048576 | tf_op jit(solution)/shard_map/pallas_call | solution.py:60
  57.1 0.0 copy-start.6
  57.1 0.0 collective-permute-done.7.refs_0_
  57.2 0.0 collective-permute-done.8.refs_1_
  57.2 36.7 %shard_map.85 = (f32[6,40,384]{2,1,0:T(8,128)S(1)}, f32[6,40,384]{2,1,0:T(8,128)S(1)}) custom-call(bf16[768,128]{1,0:T(8,128)(2,1)S(1)} %collective-permute-done.7.refs_0_, bf16[768,128]{1,0:T(8,128)(2,1)S(1)} %collective-permute-done.8.refs_1_, bf16[768,128]{1,0:T(8,128)(2,1)S(1)} %shard_map.79.refs_0_.refs_2_, ...), custom_call_target="tpu_custom_call" | custom-call | flops 3623878656 | bytes 1048576 | tf_op jit(solution)/shard_map/pallas_call | solution.py:60
  93.9 0.0 copy-start.5
  93.9 1.8 %collective-permute-start.11 = (f32[6,40,384]{2,1,0:T(8,128)S(1)}, f32[6,40,384]{2,1,0:T(8,128)S(1)}, u32[]{:S(2)}, u32[]{:S(2)}) collective-permute-start(f32[6,40,384]{2,1,0:T(8,128)S(1)} %get-tuple-element.32), channel_id=1, source_target_pairs={{0,2},{2,0},{1,3},{3,1},{4,6},{6,4},{5,7},{7,5},{8,10},{10,8},{9,1... | collective-permute-start | bytes 1105928 | tf_op jit(solution)/shard_map/ppermute | solution.py:394
  95.7 0.0 copy-done.6
  95.7 0.2 copy.8.down_ref
  95.9 1.1 %collective-permute-done.11.came_ref = f32[6,40,384]{2,1,0:T(8,128)S(1)} collective-permute-done((f32[6,40,384]{2,1,0:T(8,128)S(1)}, f32[6,40,384]{2,1,0:T(8,128)S(1)}, u32[]{:S(2)}, u32[]{:S(2)}) %collective-permute-start.11) | collective-permute-done | bytes 368672 | tf_op jit(solution)/shard_map/ppermute | solution.py:394
  97.0 0.9 shard_map.86
  97.9 3.9 %all-to-all-start.1 = ((bf16[4,144,128]{2,1,0:T(8,128)(2,1)}), bf16[4,144,128]{2,1,0:T(8,128)(2,1)S(1)}, u32[]{:S(2)}, u32[]{:S(2)}) async-start(bf16[4,144,128]{2,1,0:T(8,128)(2,1)} %shard_map.86), calls=%async_computation.1 | async-start | bytes 294912 | tf_op jit(solution)/shard_map/all_to_all | solution.py:398
  101.8 4.5 %all-to-all-done.1.came_ref = bf16[4,144,128]{2,1,0:T(8,128)(2,1)S(1)} async-done(((bf16[4,144,128]{2,1,0:T(8,128)(2,1)}), bf16[4,144,128]{2,1,0:T(8,128)(2,1)S(1)}, u32[]{:S(2)}, u32[]{:S(2)}) %all-to-all-start.1) | async-done | bytes 147488 | tf_op jit(solution)/shard_map/all_to_all | solution.py:398
  106.3 0.0 copy-done.5
  106.3 1.7 %shard_map.87 = (bf16[64,768]{1,0:T(8,128)(2,1)}, bf16[32,768]{1,0:T(8,128)(2,1)}) custom-call(bf16[4,144,128]{2,1,0:T(8,128)(2,1)S(1)} %all-to-all-done.1.came_ref, f32[4,96,192]{2,1,0:T(8,128)S(1)} %get-tuple-element.33.after_ref, bf16[192,192]{1,0:T(8,128)(2,1)S(1)} %slice_bitcast_fusion.wo_ref, bf16[192,768]{1,0:T(8,128)(2,1)S(1)} %copy-done.5, ...), custom_call_target="tpu_custom_call" | custom-call | flops 1000000000 | bytes 1048576 | tf_op jit(solution)/shard_map/pallas_call | solution.py:60
  (8 shorter events, 0.0 us)
Async XLA Ops:
  1.6 7.3 %collective-permute-start = (bf16[96,768]{1,0:T(8,128)(2,1)S(1)}, bf16[96,768]{1,0:T(8,128)(2,1)S(1)}, u32[]{:S(2)}, u32[]{:S(2)}) collective-permute-start(bf16[96,768]{1,0:T(8,128)(2,1)S(1)} %pad_maximum_fusion), channel_id=1, source_target_pairs={{0,1},{1,0},{2,3},{3,2},{4,5},{5,4},{6,7},{7,6},{8,9},{9,8},{10,11... | collective-permute-start | bytes 442376 | tf_op jit(solution)/shard_map/ppermute | solution.py:346
  5.4 0.9 copy-start
  6.3 0.8 copy-start.1
  7.1 1.0 copy-start.3
  8.1 1.0 copy-start.4
  9.1 25.8 %copy-start.2 = (bf16[4,192,192]{2,1,0:T(8,128)(2,1)S(1)}, bf16[4,192,192]{2,1,0:T(8,128)(2,1)}, u32[]{:S(2)}) copy-start(bf16[4,192,192]{2,1,0:T(8,128)(2,1)} %weights_ref.5) | copy-start | bytes 884740
  19.5 15.4 %collective-permute-start.4 = (bf16[4,144,128]{2,1,0:T(8,128)(2,1)S(1)}, bf16[4,144,128]{2,1,0:T(8,128)(2,1)S(1)}, u32[]{:S(2)}, u32[]{:S(2)}) collective-permute-start(bf16[4,144,128]{2,1,0:T(8,128)(2,1)S(1)} %all_to_all.10.own_ref), channel_id=1, source_target_pairs={{0,2},{2,0},{1,3},{3,1},{4,6},{6,4},{5,7},{7,5},{8,10},{10,8},{9,1... | collective-permute-start | bytes 442376 | tf_op jit(solution)/shard_map/ppermute | solution.py:369
  22.5 9.7 %collective-permute-start.1 = (bf16[384,128]{1,0:T(8,128)(2,1)S(1)}, bf16[384,128]{1,0:T(8,128)(2,1)S(1)}, u32[]{:S(2)}, u32[]{:S(2)}) collective-permute-start(bf16[384,128]{1,0:T(8,128)(2,1)S(1)} %bitcast.3), channel_id=1, source_target_pairs={{0,8},{8,16},{16,24},{24,0},{1,9},{9,17},{17,25},{25,1},{2,10},{10... | collective-permute-start | bytes 294920 | tf_op jit(solution)/shard_map/ppermute | solution.py:368
  25.5 11.3 %collective-permute-start.2 = (bf16[384,128]{1,0:T(8,128)(2,1)S(1)}, bf16[384,128]{1,0:T(8,128)(2,1)S(1)}, u32[]{:S(2)}, u32[]{:S(2)}) collective-permute-start(bf16[384,128]{1,0:T(8,128)(2,1)S(1)} %bitcast.4), channel_id=1, source_target_pairs={{0,24},{8,0},{16,8},{24,16},{1,25},{9,1},{17,9},{25,17},{2,26},{10... | collective-permute-start | bytes 294920 | tf_op jit(solution)/shard_map/ppermute | solution.py:368
  27.7 11.2 %collective-permute-start.3 = (bf16[384,128]{1,0:T(8,128)(2,1)S(1)}, bf16[384,128]{1,0:T(8,128)(2,1)S(1)}, u32[]{:S(2)}, u32[]{:S(2)}) collective-permute-start(bf16[384,128]{1,0:T(8,128)(2,1)S(1)} %bitcast.5), channel_id=1, source_target_pairs={{0,16},{8,24},{16,0},{24,8},{1,17},{9,25},{17,1},{25,9},{2,18},{10... | collective-permute-start | bytes 294920 | tf_op jit(solution)/shard_map/ppermute | solution.py:368
  32.1 13.7 %collective-permute-start.5 = (bf16[768,128]{1,0:T(8,128)(2,1)S(1)}, bf16[768,128]{1,0:T(8,128)(2,1)S(1)}, u32[]{:S(2)}, u32[]{:S(2)}) collective-permute-start(bf16[768,128]{1,0:T(8,128)(2,1)S(1)} %shard_map.79.refs_0_.refs_2_), channel_id=1, source_target_pairs={{0,32},{32,64},{64,96},{96,0},{1,33},{33,65},{65,97},{97,1},{2,34}... | collective-permute-start | bytes 589832 | tf_op jit(solution)/shard_map/ppermute | solution.py:371
  33.4 15.2 %collective-permute-start.9 = (bf16[768,128]{1,0:T(8,128)(2,1)S(1)}, bf16[768,128]{1,0:T(8,128)(2,1)S(1)}, u32[]{:S(2)}, u32[]{:S(2)}) collective-permute-start(bf16[768,128]{1,0:T(8,128)(2,1)S(1)} %shard_map.79.refs_0_.refs_2_), channel_id=1, source_target_pairs={{0,96},{32,0},{64,32},{96,64},{1,97},{33,1},{65,33},{97,65},{2,98}... | collective-permute-start | bytes 589832 | tf_op jit(solution)/shard_map/ppermute | solution.py:372
  39.0 6.8 %collective-permute-start.6 = (bf16[768,128]{1,0:T(8,128)(2,1)S(1)}, bf16[768,128]{1,0:T(8,128)(2,1)S(1)}, u32[]{:S(2)}, u32[]{:S(2)}) collective-permute-start(bf16[768,128]{1,0:T(8,128)(2,1)S(1)} %shard_map.81.refs_1_.refs_3_), channel_id=1, source_target_pairs={{0,96},{32,0},{64,32},{96,64},{1,97},{33,1},{65,33},{97,65},{2,98}... | collective-permute-start | bytes 589832 | tf_op jit(solution)/shard_map/ppermute | solution.py:385
  41.5 11.3 %collective-permute-start.10 = (bf16[768,128]{1,0:T(8,128)(2,1)S(1)}, bf16[768,128]{1,0:T(8,128)(2,1)S(1)}, u32[]{:S(2)}, u32[]{:S(2)}) collective-permute-start(bf16[768,128]{1,0:T(8,128)(2,1)S(1)} %shard_map.81.refs_1_.refs_3_), channel_id=1, source_target_pairs={{0,32},{32,64},{64,96},{96,0},{1,33},{33,65},{65,97},{97,1},{2,34}... | collective-permute-start | bytes 589832 | tf_op jit(solution)/shard_map/ppermute | solution.py:384
  45.8 11.4 %collective-permute-start.7 = (bf16[768,128]{1,0:T(8,128)(2,1)S(1)}, bf16[768,128]{1,0:T(8,128)(2,1)S(1)}, u32[]{:S(2)}, u32[]{:S(2)}) collective-permute-start(bf16[768,128]{1,0:T(8,128)(2,1)S(1)} %collective-permute-done.5.refs_0_.refs_4_), channel_id=1, source_target_pairs={{0,32},{32,64},{64,96},{96,0},{1,33},{33,65},{65,97},{97,1},{2,34}... | collective-permute-start | bytes 589832 | tf_op jit(solution)/shard_map/ppermute | solution.py:388
  46.1 11.1 %collective-permute-start.8 = (bf16[768,128]{1,0:T(8,128)(2,1)S(1)}, bf16[768,128]{1,0:T(8,128)(2,1)S(1)}, u32[]{:S(2)}, u32[]{:S(2)}) collective-permute-start(bf16[768,128]{1,0:T(8,128)(2,1)S(1)} %collective-permute-done.6.refs_1_.refs_7_), channel_id=1, source_target_pairs={{0,96},{32,0},{64,32},{96,64},{1,97},{33,1},{65,33},{97,65},{2,98}... | collective-permute-start | bytes 589832 | tf_op jit(solution)/shard_map/ppermute | solution.py:389
  57.1 38.6 %copy-start.6 = (bf16[768,192]{0,1:T(8,128)(2,1)S(1)}, bf16[768,192]{0,1:T(8,128)(2,1)}, u32[]{:S(2)}) copy-start(bf16[768,192]{0,1:T(8,128)(2,1)} %param.11) | copy-start | bytes 884740
  93.9 12.4 %copy-start.5 = (bf16[192,768]{1,0:T(8,128)(2,1)S(1)}, bf16[192,768]{1,0:T(8,128)(2,1)}, u32[]{:S(2)}) copy-start(bf16[192,768]{1,0:T(8,128)(2,1)} %up_ref.1) | copy-start | bytes 884740
  93.9 3.1 %collective-permute-start.11 = (f32[6,40,384]{2,1,0:T(8,128)S(1)}, f32[6,40,384]{2,1,0:T(8,128)S(1)}, u32[]{:S(2)}, u32[]{:S(2)}) collective-permute-start(f32[6,40,384]{2,1,0:T(8,128)S(1)} %get-tuple-element.32), channel_id=1, source_target_pairs={{0,2},{2,0},{1,3},{3,1},{4,6},{6,4},{5,7},{7,5},{8,10},{10,8},{9,1... | collective-permute-start | bytes 1105928 | tf_op jit(solution)/shard_map/ppermute | solution.py:394
  97.9 8.4 %all-to-all-start.1 = ((bf16[4,144,128]{2,1,0:T(8,128)(2,1)}), bf16[4,144,128]{2,1,0:T(8,128)(2,1)S(1)}, u32[]{:S(2)}, u32[]{:S(2)}) async-start(bf16[4,144,128]{2,1,0:T(8,128)(2,1)} %shard_map.86), calls=%async_computation.1 | async-start | bytes 294912 | tf_op jit(solution)/shard_map/all_to_all | solution.py:398

commit v2 on v1

--- a/solution.py
+++ b/solution.py
@@ -41,6 +41,10 @@
 f32 = jnp.float32
 
 
+classes = ("y_lo", "z_lo")
+piece_shape = jax.ShapeDtypeStruct((PACK, LANES), bf16)
+
+
 def mm(left, right):
     return jnp.dot(left, right, preferred_element_type=f32)
 
@@ -106,9 +110,14 @@
     value_ref[...] = mm(normed, weights_ref[2]).astype(bf16)
 
 
+def own_class():
+    return lax.axis_index(classes)
+
+
 def before_kernel(
-    other_ref, weights_ref, cells_ref, query_ref, key_ref, value_ref, after_ref, send_ref
+    other_ref, weights_ref, cells_ref, query_ref, key_ref, value_ref, after_ref, *refs
 ):
+    send_refs, pieces_ref = refs[:GROUPS], refs[GROUPS]
     parts = []
     for index in range(GROUPS):
         cell = other_ref[:, index * E : (index + 1) * E].astype(f32)
@@ -150,7 +159,25 @@
     for index in range(GROUPS):
         after = cells_ref[index] + moved[index * ROWS : (index + 1) * ROWS]
         after_ref[index] = after
-        send_ref[index] = pack(layer_norm(after))
+        pieces_ref[index] = pack(layer_norm(after))
+    for turn in range(GROUPS):
+        send_refs[turn][...] = pieces_ref[own_class() ^ turn]
+
+
+def gather_kernel(*refs):
+    received_ref, keys_ref = refs[GROUPS:]
+    for turn in range(GROUPS):
+        piece = refs[turn][...]
+        received_ref[turn] = piece
+        keys_ref[turn * TRAIN_PACK : (turn + 1) * TRAIN_PACK, :] = piece[:TRAIN_PACK]
+
+
+def exchange(pieces):
+    came = [pieces[0]]
+    for turn in range(1, GROUPS):
+        pairs = [(one, one ^ turn) for one in range(GROUPS)]
+        came.append(lax.ppermute(pieces[turn], classes, pairs))
+    return came
 
 
 def fold_kernel(own_ref, other_ref, weights_ref, folded_ref, turned_ref):
@@ -305,7 +332,7 @@
     )
 
 
-def merge_kernel(stay_ref, came_ref, send_ref):
+def merge_kernel(stay_ref, came_ref, *send_refs):
     parts = []
     for head in range(HEADS):
         stay = stay_ref[head]
@@ -318,11 +345,15 @@
         parts.append(mixed / total)
     turned = jnp.concatenate(parts, axis=0).T
     for peer in range(GROUPS):
-        send_ref[peer] = pack(turned[peer * ROWS : (peer + 1) * ROWS])
-
-
-def after_kernel(came_ref, after_ref, wo_ref, up_ref, down_ref, train_ref, test_ref):
-    mixes = [unpack(came_ref[index]) for index in range(GROUPS)]
+        send_refs[peer][...] = pack(turned[peer * ROWS : (peer + 1) * ROWS])
+
+
+def after_kernel(*refs):
+    came_refs = refs[:GROUPS]
+    after_ref, wo_ref, up_ref, down_ref, train_ref, test_ref, pieces_ref = refs[GROUPS:]
+    for turn in range(GROUPS):
+        pieces_ref[own_class() ^ turn] = came_refs[turn][...]
+    mixes = [unpack(pieces_ref[index]) for index in range(GROUPS)]
     row_mix = jnp.concatenate(mixes, axis=0).astype(bf16)
     after_row = after_ref[...].reshape(GROUPS * ROWS, E) + mm(row_mix, wo_ref[...])
     third = layer_norm(after_row).astype(bf16)
@@ -351,18 +382,23 @@
         (train_cells, test_cells, feat_weights),
         10**9,
     )
-    after_feat, pieces = call(
+    after_feat, *pieces = call(
         before_kernel,
-        [
-            jax.ShapeDtypeStruct((GROUPS, ROWS, E), f32),
-            jax.ShapeDtypeStruct((GROUPS, PACK, LANES), bf16),
-        ],
+        [jax.ShapeDtypeStruct((GROUPS, ROWS, E), f32)] + [piece_shape] * GROUPS,
         (other, feat_weights, *near),
         10**9,
-    )
-    classes = ("y_lo", "z_lo")
-    received = lax.all_to_all(pieces, classes, split_axis=0, concat_axis=0, tiled=True)
-    keys = received[:, :TRAIN_PACK].reshape(GROUPS * TRAIN_PACK, LANES)
+        scratch=[pltpu.VMEM((GROUPS, PACK, LANES), bf16)],
+    )
+    received, keys = call(
+        gather_kernel,
+        [
+            jax.ShapeDtypeStruct((GROUPS, PACK, LANES), bf16),
+            jax.ShapeDtypeStruct((GROUPS * TRAIN_PACK, LANES), bf16),
+        ],
+        exchange(pieces),
+        10**6,
+        limit=4,
+    )
     column = [keys]
     for by in (1, 3, 2):
         column.append(lax.ppermute(keys, "z_hi", shift(SIDE, by)))
@@ -392,18 +428,16 @@
     packed = (far_early, far_late, early, late, early_above, early_below, late_above, late_below)
     stay, leave = attend_last(packed + (value_turned, folded, mix))
     came = lax.ppermute(leave, "core", swap)
-    mixed = call(
-        merge_kernel, [jax.ShapeDtypeStruct((GROUPS, PACK, LANES), bf16)], (stay, came), 10**7
-    )[0]
-    returned = lax.all_to_all(mixed, classes, split_axis=0, concat_axis=0, tiled=True)
+    mixed = call(merge_kernel, [piece_shape] * GROUPS, (stay, came), 10**7)
     train_out, test_out = call(
         after_kernel,
         [
             jax.ShapeDtypeStruct((TRAIN_ROWS, GROUPS * E), bf16),
             jax.ShapeDtypeStruct((TEST_ROWS, GROUPS * E), bf16),
         ],
-        (returned, after_feat, row_weights[3], mlp_up, mlp_down),
+        (*exchange(mixed), after_feat, row_weights[3], mlp_up, mlp_down),
         10**9,
+        scratch=[pltpu.VMEM((GROUPS, PACK, LANES), bf16)],
     )
     return (train_out, test_out)
 

time: 108 us -> 106 us (0.981); the launches traced: 108 us -> 105 us
  blocking collectives: 7.62 us -> 0 us
  starting transfers between devices: 30.3 us -> 35.9 us
    all_to_all x1 -> x0, blocking collectives: 7.62 us -> none  [layer(): lax.all_to_all(pieces, classes, split_axis=0, concat_axis=0, tiled=True)]
    ppermute x0 -> x6, starting transfers between devices: none -> 7.16 us  [exchange(): came.append(lax.ppermute(pieces[turn], classes, pairs))]
    ppermute x0 -> x6, waiting for transfers between devices: none -> 5.83 us  [exchange(): came.append(lax.ppermute(pieces[turn], classes, pairs))]
    all_to_all x1 -> x0, waiting for transfers between devices: 4.5 us -> none  [layer(): lax.all_to_all(mixed, classes, split_axis=0, concat_axis=0, tiled=True)]
    all_to_all x1 -> x0, starting transfers between devices: 3.88 us -> none  [layer(): lax.all_to_all(mixed, classes, split_axis=0, concat_axis=0, tiled=True)]
    ppermute x1, starting transfers between devices: 1.81 us -> 4.88 us  [layer(): came = lax.ppermute(leave, 'core', swap)]
    ppermute x3, waiting for transfers between devices: 2.16 us -> 0.01 us  [layer(): column.append(lax.ppermute(keys, 'z_hi', shift(SIDE, by)))]
    ppermute x1, starting transfers between devices: 2.55 us -> 1.34 us  [layer(): late_below = lax.ppermute(late, 'x', shift(4, 3))]
  transfers between devices with their start and end apart: 13 -> 18, of which waited for: 3 -> 6; matrix products, arithmetic and copies ran while one was open for 0% -> 0% of each run, Pallas kernels for 14% -> 15%
where the time goes in v2:
time: 106 us; the launch traced here: 105 us
  Pallas kernels  56.9 us (54%)
  starting transfers between devices  35.9 us (34%)
  waiting for transfers between devices  7.17 us (7%)
  local copies, waits for them, and re-layouts  3.12 us (3%)
    pallas_call x12, Pallas kernels, call(): pl.pallas_call(kernel, out_shape=outs, in_specs=[in_vmem] * len(args), ou...  56.9 us
    ppermute x3, starting transfers between devices, layer(): column.append(lax.ppermute(keys, 'z_hi', shift(SIDE, by)))  9.58 us
    ppermute x6, starting transfers between devices, exchange(): came.append(lax.ppermute(pieces[turn], classes, pairs))  7.16 us
    ppermute x6, waiting for transfers between devices, exchange(): came.append(lax.ppermute(pieces[turn], classes, pairs))  5.83 us
    ppermute x1, starting transfers between devices, layer(): came = lax.ppermute(leave, 'core', swap)  4.88 us
    ppermute x1, starting transfers between devices, layer(): other = lax.ppermute(joined, 'feat', swap)  3.82 us
    ppermute x1, starting transfers between devices, layer(): received_other = lax.ppermute(received, 'core', swap)  3.29 us
    unnamed x15, local copies, waits for them, and re-layouts  3.11 us
  transfers between devices with their start and end apart: 18, of which 6 were waited for; matrix products, arithmetic and copies ran while one was open for 0% of the time, Pallas kernels for 15%

profile of v2, /device:TPU:1, one launch (start us, length us, event | category | flops | bytes accessed | tf_op | source)
XLA Modules:
  0.0 104.8 jit_solution(8974322744852661480)
XLA Ops:
  0.6 0.9 pad_maximum_fusion
  1.6 3.8 %collective-permute-start = (bf16[96,768]{1,0:T(8,128)(2,1)S(1)}, bf16[96,768]{1,0:T(8,128)(2,1)S(1)}, u32[]{:S(2)}, u32[]{:S(2)}) collective-permute-start(bf16[96,768]{1,0:T(8,128)(2,1)S(1)} %pad_maximum_fusion), channel_id=1, source_target_pairs={{0,1},{1,0},{2,3},{3,2},{4,5},{5,4},{6,7},{7,6},{8,9},{9,8},{10,11... | collective-permute-start | bytes 442376 | tf_op jit(solution)/shard_map/ppermute | solution.py:377
  5.4 0.9 copy-done
  6.3 0.8 copy-done.1
  7.1 1.0 copy-done.3
  8.1 0.7 shard_map.77
  8.8 0.2 copy-done.4
  9.1 2.8 %shard_map.78 = (f32[4,96,192]{2,1,0:T(8,128)S(1)}, bf16[144,128]{1,0:T(8,128)(2,1)S(1)}, bf16[144,128]{1,0:T(8,128)(2,1)S(1)}, bf16[144,128]{1,0:T(8,128)(2,1)S(1)}, bf16[144,128]{1,0:T(8,128)(2,1)S(1)}) custom-call(bf16[96,768]{1,0:T(8,128)(2,1)S(1)} %collective-permute-done.other_ref, bf16[4,192,192]{2,1,0:T(8,128)(2,1)S(1)} %copy-done.4, ...), custom_call_target="tpu_custom_call" | custom-call | flops 1000000000 | bytes 1048576 | tf_op jit(solution)/shard_map/pallas_call | solution.py:64
  11.9 1.7 %collective-permute-start.1 = (bf16[144,128]{1,0:T(8,128)(2,1)S(1)}, bf16[144,128]{1,0:T(8,128)(2,1)S(1)}, u32[]{:S(2)}, u32[]{:S(2)}) collective-permute-start(bf16[144,128]{1,0:T(8,128)(2,1)S(1)} %get-tuple-element.32), channel_id=1, source_target_pairs={{0,4},{4,0},{128,132},{132,128},{1,5},{5,1},{129,133},{133,129},{2... | collective-permute-start | bytes 110600 | tf_op jit(solution)/shard_map/ppermute | solution.py:179
  13.6 0.9 collective-permute-start.2
  14.5 0.3 collective-permute-start.3
  14.9 0.1 collective-permute-done.1.refs_1_
  15.0 1.5 %collective-permute-done.2.refs_2_ = bf16[144,128]{1,0:T(8,128)(2,1)S(1)} collective-permute-done((bf16[144,128]{1,0:T(8,128)(2,1)S(1)}, bf16[144,128]{1,0:T(8,128)(2,1)S(1)}, u32[]{:S(2)}, u32[]{:S(2)}) %collective-permute-start.2) | collective-permute-done | bytes 36896 | tf_op jit(solution)/shard_map/ppermute | solution.py:179
  16.4 1.9 %collective-permute-done.3.refs_3_ = bf16[144,128]{1,0:T(8,128)(2,1)S(1)} collective-permute-done((bf16[144,128]{1,0:T(8,128)(2,1)S(1)}, bf16[144,128]{1,0:T(8,128)(2,1)S(1)}, u32[]{:S(2)}, u32[]{:S(2)}) %collective-permute-start.3) | collective-permute-done | bytes 36896 | tf_op jit(solution)/shard_map/ppermute | solution.py:179
  18.3 3.3 %collective-permute-start.7 = (bf16[4,144,128]{2,1,0:T(8,128)(2,1)S(1)}, bf16[4,144,128]{2,1,0:T(8,128)(2,1)S(1)}, u32[]{:S(2)}, u32[]{:S(2)}) collective-permute-start(bf16[4,144,128]{2,1,0:T(8,128)(2,1)S(1)} %get-tuple-element.36.own_ref), channel_id=1, source_target_pairs={{0,2},{2,0},{1,3},{3,1},{4,6},{6,4},{5,7},{7,5},{8,10},{10,8},{9,1... | collective-permute-start | bytes 442376 | tf_op jit(solution)/shard_map/ppermute | solution.py:405
  21.6 3.0 %collective-permute-start.4 = (bf16[384,128]{1,0:T(8,128)(2,1)S(1)}, bf16[384,128]{1,0:T(8,128)(2,1)S(1)}, u32[]{:S(2)}, u32[]{:S(2)}) collective-permute-start(bf16[384,128]{1,0:T(8,128)(2,1)S(1)} %get-tuple-element.35.upper_ref), channel_id=1, source_target_pairs={{0,8},{8,16},{16,24},{24,0},{1,9},{9,17},{17,25},{25,1},{2,10},{10... | collective-permute-start | bytes 294920 | tf_op jit(solution)/shard_map/ppermute | solution.py:404
  24.6 2.1 %collective-permute-start.5 = (bf16[384,128]{1,0:T(8,128)(2,1)S(1)}, bf16[384,128]{1,0:T(8,128)(2,1)S(1)}, u32[]{:S(2)}, u32[]{:S(2)}) collective-permute-start(bf16[384,128]{1,0:T(8,128)(2,1)S(1)} %get-tuple-element.35.upper_ref), channel_id=1, source_target_pairs={{0,24},{8,0},{16,8},{24,16},{1,25},{9,1},{17,9},{25,17},{2,26},{10... | collective-permute-start | bytes 294920 | tf_op jit(solution)/shard_map/ppermute | solution.py:404
  26.7 4.5 %collective-permute-start.6 = (bf16[384,128]{1,0:T(8,128)(2,1)S(1)}, bf16[384,128]{1,0:T(8,128)(2,1)S(1)}, u32[]{:S(2)}, u32[]{:S(2)}) collective-permute-start(bf16[384,128]{1,0:T(8,128)(2,1)S(1)} %get-tuple-element.35.upper_ref), channel_id=1, source_target_pairs={{0,16},{8,24},{16,0},{24,8},{1,17},{9,25},{17,1},{25,9},{2,18},{10... | collective-permute-start | bytes 294920 | tf_op jit(solution)/shard_map/ppermute | solution.py:404
  31.2 1.3 %collective-permute-start.8 = (bf16[768,128]{1,0:T(8,128)(2,1)S(1)}, bf16[768,128]{1,0:T(8,128)(2,1)S(1)}, u32[]{:S(2)}, u32[]{:S(2)}) collective-permute-start(bf16[768,128]{1,0:T(8,128)(2,1)S(1)} %shard_map.80.refs_0_.refs_2_), channel_id=1, source_target_pairs={{0,32},{32,64},{64,96},{96,0},{1,33},{33,65},{65,97},{97,1},{2,34}... | collective-permute-start | bytes 589832 | tf_op jit(solution)/shard_map/ppermute | solution.py:407
  32.5 1.5 %collective-permute-start.12 = (bf16[768,128]{1,0:T(8,128)(2,1)S(1)}, bf16[768,128]{1,0:T(8,128)(2,1)S(1)}, u32[]{:S(2)}, u32[]{:S(2)}) collective-permute-start(bf16[768,128]{1,0:T(8,128)(2,1)S(1)} %shard_map.80.refs_0_.refs_2_), channel_id=1, source_target_pairs={{0,96},{32,0},{64,32},{96,64},{1,97},{33,1},{65,33},{97,65},{2,98}... | collective-permute-start | bytes 589832 | tf_op jit(solution)/shard_map/ppermute | solution.py:408
  34.0 0.0 collective-permute-done.7.other_ref
  34.0 1.9 %shard_map.81 = (bf16[6,208,768]{2,1,0:T(8,128)(2,1)S(1)}, bf16[192,192]{1,0:T(8,128)(2,1)S(1)}) custom-call(bf16[4,144,128]{2,1,0:T(8,128)(2,1)S(1)} %get-tuple-element.36.own_ref, bf16[4,144,128]{2,1,0:T(8,128)(2,1)S(1)} %collective-permute-done.7.other_ref, bf16[4,192,192]{2,1,0:T(8,128)(2,1)S(1)} %copy-done.2), custom_call_target="tpu_custom_call" | custom-call | flops 1000000000 | bytes 1048576 | tf_op jit(solution)/shard_map/pallas_call | solution.py:64
  35.9 0.0 collective-permute-done.5.upper_ref
  35.9 0.0 collective-permute-done.6.lower_ref
  35.9 1.3 %collective-permute-start.9 = (bf16[768,128]{1,0:T(8,128)(2,1)S(1)}, bf16[768,128]{1,0:T(8,128)(2,1)S(1)}, u32[]{:S(2)}, u32[]{:S(2)}) collective-permute-start(bf16[768,128]{1,0:T(8,128)(2,1)S(1)} %shard_map.82.refs_1_.refs_3_), channel_id=1, source_target_pairs={{0,96},{32,0},{64,32},{96,64},{1,97},{33,1},{65,33},{97,65},{2,98}... | collective-permute-start | bytes 589832 | tf_op jit(solution)/shard_map/ppermute | solution.py:421
  37.3 0.2 collective-permute-start.13
  37.5 4.2 %shard_map.83.refs_4_ = f32[6,48,768]{2,1,0:T(8,128)S(1)} custom-call(bf16[768,128]{1,0:T(8,128)(2,1)S(1)} %shard_map.80.refs_0_.refs_2_, bf16[768,128]{1,0:T(8,128)(2,1)S(1)} %shard_map.82.refs_1_.refs_3_, bf16[192,192]{1,0:T(8,128)(2,1)S(1)} %get-tuple-element.40.refs_2_.refs_8_, bf16[6,208,768]{2,1,0:T(8,128)(2,1)S(1)} %get-tuple-element.41.refs_3_.refs_9_), custom_call_target="tpu_custom_call" | custom-call | flops 3623878656 | bytes 1048576 | tf_op jit(solution)/shard_map/pallas_call | solution.py:64
  41.7 0.0 collective-permute-done.8.refs_0_.refs_4_
  41.7 0.0 collective-permute-done.9.refs_1_.refs_7_
  41.7 0.7 collective-permute-start.10
  42.5 2.1 %collective-permute-start.11 = (bf16[768,128]{1,0:T(8,128)(2,1)S(1)}, bf16[768,128]{1,0:T(8,128)(2,1)S(1)}, u32[]{:S(2)}, u32[]{:S(2)}) collective-permute-start(bf16[768,128]{1,0:T(8,128)(2,1)S(1)} %collective-permute-done.9.refs_1_.refs_7_), channel_id=1, source_target_pairs={{0,96},{32,0},{64,32},{96,64},{1,97},{33,1},{65,33},{97,65},{2,98}... | collective-permute-start | bytes 589832 | tf_op jit(solution)/shard_map/ppermute | solution.py:425
  44.6 4.2 %shard_map.84.refs_4_ = f32[6,48,768]{2,1,0:T(8,128)S(1)} custom-call(bf16[768,128]{1,0:T(8,128)(2,1)S(1)} %collective-permute-done.8.refs_0_.refs_4_, bf16[768,128]{1,0:T(8,128)(2,1)S(1)} %collective-permute-done.12.refs_1_.refs_5_, bf16[192,192]{1,0:T(8,128)(2,1)S(1)} %get-tuple-element.40.refs_2_.refs_8_, ...), custom_call_target="tpu_custom_call" | custom-call | flops 3623878656 | bytes 1048576 | tf_op jit(solution)/shard_map/pallas_call | solution.py:64
  48.9 4.2 %shard_map.85.refs_10_ = f32[6,48,768]{2,1,0:T(8,128)S(1)} custom-call(bf16[768,128]{1,0:T(8,128)(2,1)S(1)} %collective-permute-done.13.refs_0_.refs_6_, bf16[768,128]{1,0:T(8,128)(2,1)S(1)} %collective-permute-done.9.refs_1_.refs_7_, bf16[192,192]{1,0:T(8,128)(2,1)S(1)} %get-tuple-element.40.refs_2_.refs_8_, ...), custom_call_target="tpu_custom_call" | custom-call | flops 3623878656 | bytes 1048576 | tf_op jit(solution)/shard_map/pallas_call | solution.py:64
  53.1 0.0 copy-start.6
  53.1 0.0 copy-start.5
  53.1 0.0 collective-permute-done.11.refs_1_
  53.1 36.8 %shard_map.86 = (f32[6,40,384]{2,1,0:T(8,128)S(1)}, f32[6,40,384]{2,1,0:T(8,128)S(1)}) custom-call(bf16[768,128]{1,0:T(8,128)(2,1)S(1)} %collective-permute-done.10.refs_0_, bf16[768,128]{1,0:T(8,128)(2,1)S(1)} %collective-permute-done.11.refs_1_, bf16[768,128]{1,0:T(8,128)(2,1)S(1)} %shard_map.80.refs_0_.refs_2_, ...), custom_call_target="tpu_custom_call" | custom-call | flops 3623878656 | bytes 1048576 | tf_op jit(solution)/shard_map/pallas_call | solution.py:64
  89.9 4.9 %collective-permute-start.14 = (f32[6,40,384]{2,1,0:T(8,128)S(1)}, f32[6,40,384]{2,1,0:T(8,128)S(1)}, u32[]{:S(2)}, u32[]{:S(2)}) collective-permute-start(f32[6,40,384]{2,1,0:T(8,128)S(1)} %get-tuple-element.46), channel_id=1, source_target_pairs={{0,2},{2,0},{1,3},{3,1},{4,6},{6,4},{5,7},{7,5},{8,10},{10,8},{9,1... | collective-permute-start | bytes 1105928 | tf_op jit(solution)/shard_map/ppermute | solution.py:430
  94.8 1.3 %collective-permute-done.14.came_ref = f32[6,40,384]{2,1,0:T(8,128)S(1)} collective-permute-done((f32[6,40,384]{2,1,0:T(8,128)S(1)}, f32[6,40,384]{2,1,0:T(8,128)S(1)}, u32[]{:S(2)}, u32[]{:S(2)}) %collective-permute-start.14) | collective-permute-done | bytes 368672 | tf_op jit(solution)/shard_map/ppermute | solution.py:430
  96.1 0.2 shard_map.87
  96.3 2.9 %collective-permute-start.15 = (bf16[144,128]{1,0:T(8,128)(2,1)S(1)}, bf16[144,128]{1,0:T(8,128)(2,1)S(1)}, u32[]{:S(2)}, u32[]{:S(2)}) collective-permute-start(bf16[144,128]{1,0:T(8,128)(2,1)S(1)} %get-tuple-element.48), channel_id=1, source_target_pairs={{0,4},{4,0},{128,132},{132,128},{1,5},{5,1},{129,133},{133,129},{2... | collective-permute-start | bytes 110600 | tf_op jit(solution)/shard_map/ppermute | solution.py:179
  99.2 0.2 collective-permute-start.16
  99.4 1.1 %collective-permute-start.17 = (bf16[144,128]{1,0:T(8,128)(2,1)S(1)}, bf16[144,128]{1,0:T(8,128)(2,1)S(1)}, u32[]{:S(2)}, u32[]{:S(2)}) collective-permute-start(bf16[144,128]{1,0:T(8,128)(2,1)S(1)} %get-tuple-element.50), channel_id=1, source_target_pairs={{0,132},{4,128},{128,4},{132,0},{1,133},{5,129},{129,5},{133,1},{2... | collective-permute-start | bytes 110600 | tf_op jit(solution)/shard_map/ppermute | solution.py:179
  100.5 0.2 copy.8.refs_7_
  100.7 0.0 collective-permute-done.15.refs_1_
  100.7 1.3 %collective-permute-done.16.refs_2_ = bf16[144,128]{1,0:T(8,128)(2,1)S(1)} collective-permute-done((bf16[144,128]{1,0:T(8,128)(2,1)S(1)}, bf16[144,128]{1,0:T(8,128)(2,1)S(1)}, u32[]{:S(2)}, u32[]{:S(2)}) %collective-permute-start.16) | collective-permute-done | bytes 36896 | tf_op jit(solution)/shard_map/ppermute | solution.py:179
  102.0 1.1 %collective-permute-done.17.refs_3_ = bf16[144,128]{1,0:T(8,128)(2,1)S(1)} collective-permute-done((bf16[144,128]{1,0:T(8,128)(2,1)S(1)}, bf16[144,128]{1,0:T(8,128)(2,1)S(1)}, u32[]{:S(2)}, u32[]{:S(2)}) %collective-permute-start.17) | collective-permute-done | bytes 36896 | tf_op jit(solution)/shard_map/ppermute | solution.py:179
  103.1 1.7 %shard_map.88 = (bf16[64,768]{1,0:T(8,128)(2,1)}, bf16[32,768]{1,0:T(8,128)(2,1)}) custom-call(bf16[144,128]{1,0:T(8,128)(2,1)S(1)} %get-tuple-element.47.refs_0_, bf16[144,128]{1,0:T(8,128)(2,1)S(1)} %collective-permute-done.15.refs_1_, bf16[144,128]{1,0:T(8,128)(2,1)S(1)} %collective-permute-done.16.refs_2_, ...), custom_call_target="tpu_custom_call" | custom-call | flops 1000000000 | bytes 1048576 | tf_op jit(solution)/shard_map/pallas_call | solution.py:64
  (17 shorter events, 0.1 us)
Async XLA Ops:
  1.6 7.3 %collective-permute-start = (bf16[96,768]{1,0:T(8,128)(2,1)S(1)}, bf16[96,768]{1,0:T(8,128)(2,1)S(1)}, u32[]{:S(2)}, u32[]{:S(2)}) collective-permute-start(bf16[96,768]{1,0:T(8,128)(2,1)S(1)} %pad_maximum_fusion), channel_id=1, source_target_pairs={{0,1},{1,0},{2,3},{3,2},{4,5},{5,4},{6,7},{7,6},{8,9},{9,8},{10,11... | collective-permute-start | bytes 442376 | tf_op jit(solution)/shard_map/ppermute | solution.py:377
  5.4 0.9 copy-start
  6.3 0.8 copy-start.1
  7.1 1.0 copy-start.3
  8.1 1.0 copy-start.4
  9.1 24.9 %copy-start.2 = (bf16[4,192,192]{2,1,0:T(8,128)(2,1)S(1)}, bf16[4,192,192]{2,1,0:T(8,128)(2,1)}, u32[]{:S(2)}) copy-start(bf16[4,192,192]{2,1,0:T(8,128)(2,1)} %weights_ref.5) | copy-start | bytes 884740
  11.9 3.1 %collective-permute-start.1 = (bf16[144,128]{1,0:T(8,128)(2,1)S(1)}, bf16[144,128]{1,0:T(8,128)(2,1)S(1)}, u32[]{:S(2)}, u32[]{:S(2)}) collective-permute-start(bf16[144,128]{1,0:T(8,128)(2,1)S(1)} %get-tuple-element.32), channel_id=1, source_target_pairs={{0,4},{4,0},{128,132},{132,128},{1,5},{5,1},{129,133},{133,129},{2... | collective-permute-start | bytes 110600 | tf_op jit(solution)/shard_map/ppermute | solution.py:179
  13.6 2.8 %collective-permute-start.2 = (bf16[144,128]{1,0:T(8,128)(2,1)S(1)}, bf16[144,128]{1,0:T(8,128)(2,1)S(1)}, u32[]{:S(2)}, u32[]{:S(2)}) collective-permute-start(bf16[144,128]{1,0:T(8,128)(2,1)S(1)} %get-tuple-element.33), channel_id=1, source_target_pairs={{0,128},{4,132},{128,0},{132,4},{1,129},{5,133},{129,1},{133,5},{2... | collective-permute-start | bytes 110600 | tf_op jit(solution)/shard_map/ppermute | solution.py:179
  14.5 3.7 %collective-permute-start.3 = (bf16[144,128]{1,0:T(8,128)(2,1)S(1)}, bf16[144,128]{1,0:T(8,128)(2,1)S(1)}, u32[]{:S(2)}, u32[]{:S(2)}) collective-permute-start(bf16[144,128]{1,0:T(8,128)(2,1)S(1)} %get-tuple-element.34), channel_id=1, source_target_pairs={{0,132},{4,128},{128,4},{132,0},{1,133},{5,129},{129,5},{133,1},{2... | collective-permute-start | bytes 110600 | tf_op jit(solution)/shard_map/ppermute | solution.py:179
  18.3 15.7 %collective-permute-start.7 = (bf16[4,144,128]{2,1,0:T(8,128)(2,1)S(1)}, bf16[4,144,128]{2,1,0:T(8,128)(2,1)S(1)}, u32[]{:S(2)}, u32[]{:S(2)}) collective-permute-start(bf16[4,144,128]{2,1,0:T(8,128)(2,1)S(1)} %get-tuple-element.36.own_ref), channel_id=1, source_target_pairs={{0,2},{2,0},{1,3},{3,1},{4,6},{6,4},{5,7},{7,5},{8,10},{10,8},{9,1... | collective-permute-start | bytes 442376 | tf_op jit(solution)/shard_map/ppermute | solution.py:405
  21.6 9.6 %collective-permute-start.4 = (bf16[384,128]{1,0:T(8,128)(2,1)S(1)}, bf16[384,128]{1,0:T(8,128)(2,1)S(1)}, u32[]{:S(2)}, u32[]{:S(2)}) collective-permute-start(bf16[384,128]{1,0:T(8,128)(2,1)S(1)} %get-tuple-element.35.upper_ref), channel_id=1, source_target_pairs={{0,8},{8,16},{16,24},{24,0},{1,9},{9,17},{17,25},{25,1},{2,10},{10... | collective-permute-start | bytes 294920 | tf_op jit(solution)/shard_map/ppermute | solution.py:404
  24.6 11.3 %collective-permute-start.5 = (bf16[384,128]{1,0:T(8,128)(2,1)S(1)}, bf16[384,128]{1,0:T(8,128)(2,1)S(1)}, u32[]{:S(2)}, u32[]{:S(2)}) collective-permute-start(bf16[384,128]{1,0:T(8,128)(2,1)S(1)} %get-tuple-element.35.upper_ref), channel_id=1, source_target_pairs={{0,24},{8,0},{16,8},{24,16},{1,25},{9,1},{17,9},{25,17},{2,26},{10... | collective-permute-start | bytes 294920 | tf_op jit(solution)/shard_map/ppermute | solution.py:404
  26.7 9.2 %collective-permute-start.6 = (bf16[384,128]{1,0:T(8,128)(2,1)S(1)}, bf16[384,128]{1,0:T(8,128)(2,1)S(1)}, u32[]{:S(2)}, u32[]{:S(2)}) collective-permute-start(bf16[384,128]{1,0:T(8,128)(2,1)S(1)} %get-tuple-element.35.upper_ref), channel_id=1, source_target_pairs={{0,16},{8,24},{16,0},{24,8},{1,17},{9,25},{17,1},{25,9},{2,18},{10... | collective-permute-start | bytes 294920 | tf_op jit(solution)/shard_map/ppermute | solution.py:404
  31.2 10.5 %collective-permute-start.8 = (bf16[768,128]{1,0:T(8,128)(2,1)S(1)}, bf16[768,128]{1,0:T(8,128)(2,1)S(1)}, u32[]{:S(2)}, u32[]{:S(2)}) collective-permute-start(bf16[768,128]{1,0:T(8,128)(2,1)S(1)} %shard_map.80.refs_0_.refs_2_), channel_id=1, source_target_pairs={{0,32},{32,64},{64,96},{96,0},{1,33},{33,65},{65,97},{97,1},{2,34}... | collective-permute-start | bytes 589832 | tf_op jit(solution)/shard_map/ppermute | solution.py:407
  32.5 12.1 %collective-permute-start.12 = (bf16[768,128]{1,0:T(8,128)(2,1)S(1)}, bf16[768,128]{1,0:T(8,128)(2,1)S(1)}, u32[]{:S(2)}, u32[]{:S(2)}) collective-permute-start(bf16[768,128]{1,0:T(8,128)(2,1)S(1)} %shard_map.80.refs_0_.refs_2_), channel_id=1, source_target_pairs={{0,96},{32,0},{64,32},{96,64},{1,97},{33,1},{65,33},{97,65},{2,98}... | collective-permute-start | bytes 589832 | tf_op jit(solution)/shard_map/ppermute | solution.py:408
  35.9 5.8 %collective-permute-start.9 = (bf16[768,128]{1,0:T(8,128)(2,1)S(1)}, bf16[768,128]{1,0:T(8,128)(2,1)S(1)}, u32[]{:S(2)}, u32[]{:S(2)}) collective-permute-start(bf16[768,128]{1,0:T(8,128)(2,1)S(1)} %shard_map.82.refs_1_.refs_3_), channel_id=1, source_target_pairs={{0,96},{32,0},{64,32},{96,64},{1,97},{33,1},{65,33},{97,65},{2,98}... | collective-permute-start | bytes 589832 | tf_op jit(solution)/shard_map/ppermute | solution.py:421
  37.3 11.6 %collective-permute-start.13 = (bf16[768,128]{1,0:T(8,128)(2,1)S(1)}, bf16[768,128]{1,0:T(8,128)(2,1)S(1)}, u32[]{:S(2)}, u32[]{:S(2)}) collective-permute-start(bf16[768,128]{1,0:T(8,128)(2,1)S(1)} %shard_map.82.refs_1_.refs_3_), channel_id=1, source_target_pairs={{0,32},{32,64},{64,96},{96,0},{1,33},{33,65},{65,97},{97,1},{2,34}... | collective-permute-start | bytes 589832 | tf_op jit(solution)/shard_map/ppermute | solution.py:420
  41.7 11.4 %collective-permute-start.10 = (bf16[768,128]{1,0:T(8,128)(2,1)S(1)}, bf16[768,128]{1,0:T(8,128)(2,1)S(1)}, u32[]{:S(2)}, u32[]{:S(2)}) collective-permute-start(bf16[768,128]{1,0:T(8,128)(2,1)S(1)} %collective-permute-done.8.refs_0_.refs_4_), channel_id=1, source_target_pairs={{0,32},{32,64},{64,96},{96,0},{1,33},{33,65},{65,97},{97,1},{2,34}... | collective-permute-start | bytes 589832 | tf_op jit(solution)/shard_map/ppermute | solution.py:424
  42.5 10.7 %collective-permute-start.11 = (bf16[768,128]{1,0:T(8,128)(2,1)S(1)}, bf16[768,128]{1,0:T(8,128)(2,1)S(1)}, u32[]{:S(2)}, u32[]{:S(2)}) collective-permute-start(bf16[768,128]{1,0:T(8,128)(2,1)S(1)} %collective-permute-done.9.refs_1_.refs_7_), channel_id=1, source_target_pairs={{0,96},{32,0},{64,32},{96,64},{1,97},{33,1},{65,33},{97,65},{2,98}... | collective-permute-start | bytes 589832 | tf_op jit(solution)/shard_map/ppermute | solution.py:425
  53.1 47.4 %copy-start.6 = (bf16[768,192]{0,1:T(8,128)(2,1)S(1)}, bf16[768,192]{0,1:T(8,128)(2,1)}, u32[]{:S(2)}) copy-start(bf16[768,192]{0,1:T(8,128)(2,1)} %param.11) | copy-start | bytes 884740
  53.1 50.0 %copy-start.5 = (bf16[192,768]{1,0:T(8,128)(2,1)S(1)}, bf16[192,768]{1,0:T(8,128)(2,1)}, u32[]{:S(2)}) copy-start(bf16[192,768]{1,0:T(8,128)(2,1)} %refs_6_.1) | copy-start | bytes 884740
  89.9 6.2 %collective-permute-start.14 = (f32[6,40,384]{2,1,0:T(8,128)S(1)}, f32[6,40,384]{2,1,0:T(8,128)S(1)}, u32[]{:S(2)}, u32[]{:S(2)}) collective-permute-start(f32[6,40,384]{2,1,0:T(8,128)S(1)} %get-tuple-element.46), channel_id=1, source_target_pairs={{0,2},{2,0},{1,3},{3,1},{4,6},{6,4},{5,7},{7,5},{8,10},{10,8},{9,1... | collective-permute-start | bytes 1105928 | tf_op jit(solution)/shard_map/ppermute | solution.py:430
  96.3 4.3 %collective-permute-start.15 = (bf16[144,128]{1,0:T(8,128)(2,1)S(1)}, bf16[144,128]{1,0:T(8,128)(2,1)S(1)}, u32[]{:S(2)}, u32[]{:S(2)}) collective-permute-start(bf16[144,128]{1,0:T(8,128)(2,1)S(1)} %get-tuple-element.48), channel_id=1, source_target_pairs={{0,4},{4,0},{128,132},{132,128},{1,5},{5,1},{129,133},{133,129},{2... | collective-permute-start | bytes 110600 | tf_op jit(solution)/shard_map/ppermute | solution.py:179
  99.2 2.8 %collective-permute-start.16 = (bf16[144,128]{1,0:T(8,128)(2,1)S(1)}, bf16[144,128]{1,0:T(8,128)(2,1)S(1)}, u32[]{:S(2)}, u32[]{:S(2)}) collective-permute-start(bf16[144,128]{1,0:T(8,128)(2,1)S(1)} %get-tuple-element.49), channel_id=1, source_target_pairs={{0,128},{4,132},{128,0},{132,4},{1,129},{5,133},{129,1},{133,5},{2... | collective-permute-start | bytes 110600 | tf_op jit(solution)/shard_map/ppermute | solution.py:179
  99.4 3.7 %collective-permute-start.17 = (bf16[144,128]{1,0:T(8,128)(2,1)S(1)}, bf16[144,128]{1,0:T(8,128)(2,1)S(1)}, u32[]{:S(2)}, u32[]{:S(2)}) collective-permute-start(bf16[144,128]{1,0:T(8,128)(2,1)S(1)} %get-tuple-element.50), channel_id=1, source_target_pairs={{0,132},{4,128},{128,4},{132,0},{1,133},{5,129},{129,5},{133,1},{2... | collective-permute-start | bytes 110600 | tf_op jit(solution)/shard_map/ppermute | solution.py:179

commit v3 on v2

--- a/solution.py
+++ b/solution.py
@@ -12,7 +12,6 @@
 HEADS = 6
 HD = 32
 GROUPS = 4
-FEATS = 8
 TRAIN_ROWS = 64
 TEST_ROWS = 32
 ROWS = TRAIN_ROWS + TEST_ROWS
@@ -27,7 +26,9 @@
 KEYS = SOURCES * TRAIN_ROWS
 SUMS = HD + 16
 FOLD = E + 16
-PROBES = 64
+PROBES = 16
+KEY_STEP = 256
+AHEAD = 2
 BLOCK = SOURCES * TRAIN_PACK
 STATE = HD + 8
 
@@ -96,7 +97,40 @@
     return jnp.concatenate(parts, axis=0)
 
 
-def near_kernel(train_ref, test_ref, weights_ref, cells_ref, query_ref, key_ref, value_ref):
+def head_maps():
+    head_of = lax.broadcasted_iota(jnp.int32, (E, 128), 0) >> 5
+    head_in = lax.broadcasted_iota(jnp.int32, (E, 128), 1)
+    head_to = lax.broadcasted_iota(jnp.int32, (128, E), 1) >> 5
+    head_out = lax.broadcasted_iota(jnp.int32, (128, E), 0)
+    gather = jnp.where(head_of == head_in, 1.0, 0.0).astype(bf16)
+    return gather, jnp.where(head_to == head_out, 1.0, 0.0).astype(bf16)
+
+
+def rows_of(table, index):
+    return table[index * ROWS : (index + 1) * ROWS]
+
+
+def group_scores(asked, keys, gather):
+    products = [asked * rows_of(keys, j) for j in range(GROUPS)]
+    scores = mm(jnp.concatenate(products, axis=0), gather)
+    return [rows_of(scores, j) for j in range(GROUPS)]
+
+
+def halves(total):
+    high = total.astype(bf16)
+    return [high, (total - high.astype(f32)).astype(bf16)]
+
+
+def near_kernel(
+    train_ref,
+    test_ref,
+    weights_ref,
+    cells_ref,
+    query_ref,
+    peak_ref,
+    total_ref,
+    mixed_ref,
+):
     parts = []
     for index in range(GROUPS):
         span = slice(index * E, (index + 1) * E)
@@ -105,9 +139,27 @@
         cells_ref[index] = cell
         parts.append(layer_norm(cell).astype(bf16))
     normed = jnp.concatenate(parts, axis=0)
-    query_ref[...] = (mm(normed, weights_ref[0]) * log2_scale).astype(bf16)
-    key_ref[...] = mm(normed, weights_ref[1]).astype(bf16)
-    value_ref[...] = mm(normed, weights_ref[2]).astype(bf16)
+    queries = (mm(normed, weights_ref[0]) * log2_scale).astype(bf16)
+    query_ref[...] = queries
+    keys = mm(normed, weights_ref[1]).astype(bf16)
+    values = mm(normed, weights_ref[2]).astype(bf16).astype(f32)
+    gather, spread = head_maps()
+    for index in range(GROUPS):
+        scores = group_scores(rows_of(queries, index), keys, gather)
+        peak = scores[0]
+        for one in scores[1:]:
+            peak = jnp.maximum(peak, one)
+        weights = [jnp.exp2(one - peak) for one in scores]
+        total = weights[0]
+        for one in weights[1:]:
+            total = total + one
+        wide = mm(jnp.concatenate([one.astype(bf16) for one in weights], axis=0), spread)
+        mixed = rows_of(wide, 0) * rows_of(values, 0)
+        for j in range(1, GROUPS):
+            mixed = mixed + rows_of(wide, j) * rows_of(values, j)
+        peak_ref[index] = peak
+        total_ref[index] = total
+        mixed_ref[index] = mixed
 
 
 def own_class():
@@ -115,7 +167,7 @@
 
 
 def before_kernel(
-    other_ref, weights_ref, cells_ref, query_ref, key_ref, value_ref, after_ref, *refs
+    other_ref, weights_ref, cells_ref, query_ref, peak_ref, total_ref, mixed_ref, after_ref, *refs
 ):
     send_refs, pieces_ref = refs[:GROUPS], refs[GROUPS]
     parts = []
@@ -123,37 +175,27 @@
         cell = other_ref[:, index * E : (index + 1) * E].astype(f32)
         parts.append(layer_norm(cell).astype(bf16))
     normed = jnp.concatenate(parts, axis=0)
-    far_keys = mm(normed, weights_ref[1]).astype(bf16)
-    far_values = mm(normed, weights_ref[2]).astype(bf16)
-    queries = query_ref[...]
-    keys = jnp.concatenate([key_ref[...], far_keys], axis=0)
-    values = jnp.concatenate([value_ref[...], far_values], axis=0).astype(f32)
-    head_of = lax.broadcasted_iota(jnp.int32, (E, 128), 0) >> 5
-    gather = jnp.where(head_of == lax.broadcasted_iota(jnp.int32, (E, 128), 1), 1.0, 0.0).astype(bf16)
-    head_to = lax.broadcasted_iota(jnp.int32, (128, E), 1) >> 5
-    spread = jnp.where(head_to == lax.broadcasted_iota(jnp.int32, (128, E), 0), 1.0, 0.0).astype(bf16)
+    keys = mm(normed, weights_ref[1]).astype(bf16)
+    values = mm(normed, weights_ref[2]).astype(bf16).astype(f32)
+    gather, spread = head_maps()
     mixtures = []
     for index in range(GROUPS):
-        asked = queries[index * ROWS : (index + 1) * ROWS]
-        products = jnp.concatenate(
-            [asked * keys[j * ROWS : (j + 1) * ROWS] for j in range(FEATS)], axis=0
-        )
-        scores = mm(products, gather)
-        pieces = [scores[j * ROWS : (j + 1) * ROWS] for j in range(FEATS)]
-        peak = pieces[0]
-        for one in pieces[1:]:
+        scores = group_scores(query_ref[index * ROWS : (index + 1) * ROWS, :], keys, gather)
+        near_peak = peak_ref[index]
+        peak = near_peak
+        for one in scores:
             peak = jnp.maximum(peak, one)
-        weights = [jnp.exp2(one - peak) for one in pieces]
-        total = weights[0]
-        for one in weights[1:]:
+        fade = jnp.exp2(near_peak - peak)
+        weights = [jnp.exp2(one - peak) for one in scores]
+        total = total_ref[index] * fade
+        for one in weights:
             total = total + one
-        high = total.astype(bf16)
-        low = (total - high.astype(f32)).astype(bf16)
-        wide = mm(jnp.concatenate([one.astype(bf16) for one in weights] + [high, low], axis=0), spread)
-        mixed = wide[:ROWS] * values[:ROWS]
-        for j in range(1, FEATS):
-            mixed = mixed + wide[j * ROWS : (j + 1) * ROWS] * values[j * ROWS : (j + 1) * ROWS]
-        whole = wide[FEATS * ROWS : (FEATS + 1) * ROWS] + wide[(FEATS + 1) * ROWS :]
+        widened = [one.astype(bf16) for one in weights] + halves(fade) + halves(total)
+        wide = mm(jnp.concatenate(widened, axis=0), spread)
+        mixed = mixed_ref[index] * (rows_of(wide, GROUPS) + rows_of(wide, GROUPS + 1))
+        for j in range(GROUPS):
+            mixed = mixed + rows_of(wide, j) * rows_of(values, j)
+        whole = rows_of(wide, GROUPS + 2) + rows_of(wide, GROUPS + 3)
         mixtures.append((mixed / whole).astype(bf16))
     moved = mm(jnp.concatenate(mixtures, axis=0), weights_ref[3]).astype(bf16).astype(f32)
     for index in range(GROUPS):
@@ -213,8 +255,8 @@
 
 def unpack_keys(packed_refs, keys_ref):
     half = TRAIN_ROWS // 2
-    each = SOURCES // len(packed_refs)
-    for source in range(SOURCES):
+    each = SOURCES // 2
+    for source in range(len(packed_refs) * each):
         packed_ref = packed_refs[source // each]
         low = source * TRAIN_ROWS
         top = source % each * TRAIN_PACK
@@ -222,56 +264,78 @@
         keys_ref[low : low + TRAIN_ROWS, :LANES] = packed_ref[top : top + TRAIN_ROWS, :]
         keys_ref[low : low + half, LANES:E] = rest[:, :REST]
         keys_ref[low + half : low + TRAIN_ROWS, LANES:E] = rest[:, REST:]
-    keys_ref[:, E:] = jnp.ones((KEYS, FOLD - E), bf16)
+    keys_ref[:, E:] = jnp.ones((keys_ref.shape[0], FOLD - E), bf16)
 
 
 def turn_values(wv_ref, keys_ref, values_ref):
     values = mm_nt(wv_ref[...], keys_ref[:, :E]).astype(bf16)
     for head in range(HEADS):
         values_ref[head, 0:HD, :] = values[head * HD : (head + 1) * HD, :]
-        values_ref[head, HD:SUMS, :] = jnp.ones((SUMS - HD, KEYS), bf16)
+        values_ref[head, HD:SUMS, :] = jnp.ones((SUMS - HD, keys_ref.shape[0]), bf16)
+
+
+def attend_heads(packed_refs, wv_ref, folded_ref, keys_ref, values_ref, finish):
+    unpack_keys(packed_refs, keys_ref)
+    turn_values(wv_ref, keys_ref, values_ref)
+    steps = keys_ref.shape[0] // KEY_STEP
+    waiting = []
+    sums = {}
+
+    def drain():
+        head, step, weights = waiting.pop(0)
+        part = mm(values_ref[head, :, step * KEY_STEP : (step + 1) * KEY_STEP], weights)
+        sums[head] = sums[head] + part if step else part
+        if step == steps - 1:
+            finish(head, sums.pop(head))
+
+    for head in range(HEADS):
+        for step in range(steps):
+            scores = mm(keys_ref[step * KEY_STEP : (step + 1) * KEY_STEP, :], folded_ref[head])
+            waiting.append((head, step, jnp.exp2(scores).astype(bf16)))
+            if len(waiting) > AHEAD:
+                drain()
+    while waiting:
+        drain()
 
 
 def attend_kernel(first, packed_refs, refs):
     wv_ref, folded_ref = refs[:2]
     mix_out, keys_ref, values_ref = refs[-3:]
-    unpack_keys(packed_refs, keys_ref)
-    turn_values(wv_ref, keys_ref, values_ref)
-
-    def work(head):
-        weights = jnp.exp2(mm(keys_ref[...], folded_ref[head])).astype(bf16)
-        mixed = mm(values_ref[head], weights)
-        if not first:
-            mixed = mixed + refs[2][head]
-        mix_out[head] = mixed
-
-    for head in range(HEADS):
-        work(head)
+
+    def finish(head, mixed):
+        mix_out[head] = mixed if first else mixed + refs[2][head]
+
+    attend_heads(packed_refs, wv_ref, folded_ref, keys_ref, values_ref, finish)
 
 
 def attend_last_kernel(*refs):
     packed_refs = refs[: 2 * SIDE]
     wv_ref, folded_ref, mix_ref, stay_ref, leave_ref = refs[2 * SIDE : 2 * SIDE + 5]
     keys_ref, values_ref, total_ref, peak_ref, blocks_ref, scores_ref = refs[2 * SIDE + 5 :]
-    attend_kernel(
-        False,
-        packed_refs[:2],
-        (wv_ref, folded_ref, mix_ref, total_ref, keys_ref, values_ref),
-    )
-    for head in range(HEADS):
-        peak_ref[head] = -folded_ref[head, E:, :].astype(f32)[:8]
-    over = jnp.where(jnp.abs(total_ref[...]) < safe_size, 0.0, 1.0)
-
-    @pl.when(jnp.max(over) > 0.0)
+    over = [jnp.zeros((8, ALL_Q), f32)]
+
+    def leave(head, total, peak):
+        joined = jnp.concatenate([total[: HD + 1], peak, total[HD + 2 : STATE]], axis=0)
+        stay_ref[head] = joined[:, :OWN_Q]
+        leave_ref[head] = joined[:, OWN_Q:]
+
+    def finish(head, mixed):
+        total = mixed + mix_ref[head]
+        grown = jnp.where(jnp.abs(total) < safe_size, 0.0, 1.0)
+        over[0] = jnp.maximum(over[0], jnp.max(grown.reshape(SUMS // 8, 8, ALL_Q), axis=0))
+        leave(head, total, -folded_ref[head, E:, :].astype(f32)[:1])
+
+    attend_heads(packed_refs[:2], wv_ref, folded_ref, keys_ref, values_ref, finish)
+
+    @pl.when(jnp.max(over[0]) > 0.0)
     def _():
         for index, one_ref in enumerate(packed_refs):
-            span = slice(index % 2 * BLOCK // 2, (index % 2 + 1) * BLOCK // 2)
-            blocks_ref[index // 2, span] = one_ref[...]
+            blocks_ref[index] = one_ref[...]
         peak_ref[...] = jnp.full(peak_ref.shape, far_below, f32)
         total_ref[...] = jnp.zeros(total_ref.shape, f32)
 
         def one_block(index, carry):
-            unpack_keys((blocks_ref.at[index],), keys_ref)
+            unpack_keys((blocks_ref.at[2 * index], blocks_ref.at[2 * index + 1]), keys_ref)
             turn_values(wv_ref, keys_ref, values_ref)
 
             def work(head, kept):
@@ -288,30 +352,28 @@
             return carry
 
         lax.fori_loop(0, SIDE, one_block, 0)
-
-    for head in range(HEADS):
-        total = total_ref[head]
-        joined = jnp.concatenate(
-            [total[: HD + 1], peak_ref[head][0:1, :], total[HD + 2 : STATE]], axis=0
-        )
-        stay_ref[head] = joined[:, :OWN_Q]
-        leave_ref[head] = joined[:, OWN_Q:]
+        for head in range(HEADS):
+            leave(head, total_ref[head], peak_ref[head][0:1, :])
 
 
 mix_shape = jax.ShapeDtypeStruct((HEADS, SUMS, ALL_Q), f32)
-attend_scratch = [pltpu.VMEM((KEYS, FOLD), bf16), pltpu.VMEM((HEADS, SUMS, KEYS), bf16)]
 attend_flops = 4 * HEADS * KEYS * ALL_Q * E
 
 
-def attend(args):
-    first = len(args) == 4
+def attend_scratch(keys):
+    return [pltpu.VMEM((keys, FOLD), bf16), pltpu.VMEM((HEADS, SUMS, keys), bf16)]
+
+
+def attend(packed, args):
+    count = len(packed)
+    first = len(args) == 2
     return call(
-        lambda *refs: attend_kernel(first, refs[:2], refs[2:]),
+        lambda *refs: attend_kernel(first, refs[:count], refs[count:]),
         [mix_shape],
-        args,
-        attend_flops,
-        scratch=attend_scratch,
-        limit=20,
+        (*packed, *args),
+        attend_flops * count // 2,
+        scratch=attend_scratch(KEYS * count // 2),
+        limit=24,
     )[0]
 
 
@@ -321,11 +383,11 @@
         [jax.ShapeDtypeStruct((HEADS, STATE, OWN_Q), f32)] * 2,
         args,
         attend_flops,
-        scratch=attend_scratch
+        scratch=attend_scratch(KEYS)
         + [
             pltpu.VMEM((HEADS, SUMS, ALL_Q), f32),
             pltpu.VMEM((HEADS, 8, ALL_Q), f32),
-            pltpu.VMEM((SIDE, BLOCK, LANES), bf16),
+            pltpu.VMEM((2 * SIDE, BLOCK // 2, LANES), bf16),
             pltpu.VMEM((KEYS, ALL_Q), f32),
         ],
         limit=20,
@@ -375,10 +437,15 @@
     swap = [(0, 1), (1, 0)]
     joined = jnp.concatenate([train_cells, test_cells], axis=0)
     other = lax.ppermute(joined, "feat", swap)
-    wide = (GROUPS * ROWS, E)
     near = call(
         near_kernel,
-        [jax.ShapeDtypeStruct((GROUPS, ROWS, E), f32)] + [jax.ShapeDtypeStruct(wide, bf16)] * 3,
+        [
+            jax.ShapeDtypeStruct((GROUPS, ROWS, E), f32),
+            jax.ShapeDtypeStruct((GROUPS * ROWS, E), bf16),
+            jax.ShapeDtypeStruct((GROUPS, ROWS, 128), f32),
+            jax.ShapeDtypeStruct((GROUPS, ROWS, 128), f32),
+            jax.ShapeDtypeStruct((GROUPS, ROWS, E), f32),
+        ],
         (train_cells, test_cells, feat_weights),
         10**9,
     )
@@ -419,13 +486,13 @@
     late = stack(*column)
     late_above = lax.ppermute(late, "x", shift(4, 1))
     late_below = lax.ppermute(late, "x", shift(4, 3))
-    mix = attend((early, late, value_turned, folded))
+    mix = attend((early, late), (value_turned, folded))
     mix, early_above, late_below = lax.optimization_barrier((mix, early_above, late_below))
     far_early = lax.ppermute(early_above, "x", shift(4, 1))
     far_late = lax.ppermute(late_below, "x", shift(4, 3))
-    mix = attend((early_above, early_below, value_turned, folded, mix))
-    mix = attend((late_above, late_below, value_turned, folded, mix))
-    packed = (far_early, far_late, early, late, early_above, early_below, late_above, late_below)
+    middle = (early_above, early_below, late_above, late_below)
+    mix = attend(middle, (value_turned, folded, mix))
+    packed = (far_early, far_late, early, late) + middle
     stay, leave = attend_last(packed + (value_turned, folded, mix))
     came = lax.ppermute(leave, "core", swap)
     mixed = call(merge_kernel, [piece_shape] * GROUPS, (stay, came), 10**7)

time: 106 us -> 104 us (0.981); the launches traced: 105 us -> 104 us
    pallas_call x12 -> x11, Pallas kernels: 56.9 us -> 56.5 us  [call(): pl.pallas_call(kernel, out_shape=outs, in_specs=[in_vmem] * len(args), ou...]
where the time goes in v3:
time: 104 us
  Pallas kernels  56.5 us (54%)
  starting transfers between devices  35.8 us (34%)
  waiting for transfers between devices  7.04 us (7%)
  local copies, waits for them, and re-layouts  2.89 us (3%)
    pallas_call x11, Pallas kernels, call(): pl.pallas_call(kernel, out_shape=outs, in_specs=[in_vmem] * len(args), ou...  56.5 us
    ppermute x3, starting transfers between devices, layer(): column.append(lax.ppermute(keys, 'z_hi', shift(SIDE, by)))  9.59 us
    ppermute x6, starting transfers between devices, exchange(): came.append(lax.ppermute(pieces[turn], classes, pairs))  6.31 us
    ppermute x1, starting transfers between devices, layer(): came = lax.ppermute(leave, 'core', swap)  5.82 us
    ppermute x6, waiting for transfers between devices, exchange(): came.append(lax.ppermute(pieces[turn], classes, pairs))  5.7 us
    ppermute x1, starting transfers between devices, layer(): other = lax.ppermute(joined, 'feat', swap)  3.82 us
    ppermute x1, starting transfers between devices, layer(): received_other = lax.ppermute(received, 'core', swap)  3.14 us
    unnamed x15, local copies, waits for them, and re-layouts  2.88 us
  transfers between devices with their start and end apart: 18, of which 6 were waited for; matrix products, arithmetic and copies ran while one was open for 0% of the time, Pallas kernels for 15%

profile of v3, /device:TPU:1, one launch (start us, length us, event | category | flops | bytes accessed | tf_op | source)
XLA Modules:
  0.0 104.0 jit_solution(1398355927291124665)
XLA Ops:
  0.6 0.9 pad_maximum_fusion
  1.6 3.8 %collective-permute-start = (bf16[96,768]{1,0:T(8,128)(2,1)S(1)}, bf16[96,768]{1,0:T(8,128)(2,1)S(1)}, u32[]{:S(2)}, u32[]{:S(2)}) collective-permute-start(bf16[96,768]{1,0:T(8,128)(2,1)S(1)} %pad_maximum_fusion), channel_id=1, source_target_pairs={{0,1},{1,0},{2,3},{3,2},{4,5},{5,4},{6,7},{7,6},{8,9},{9,8},{10,11... | collective-permute-start | bytes 442376 | tf_op jit(solution)/shard_map/ppermute | solution.py:439
  5.4 0.9 copy-done
  6.3 0.8 copy-done.1
  7.1 1.0 copy-done.3
  8.1 1.7 %shard_map.77 = (f32[4,96,192]{2,1,0:T(8,128)S(1)}, bf16[384,192]{1,0:T(8,128)(2,1)S(1)}, f32[4,96,128]{2,1,0:T(8,128)S(1)}, f32[4,96,128]{2,1,0:T(8,128)S(1)}, f32[4,96,192]{2,1,0:T(8,128)S(1)}) custom-call(bf16[64,768]{1,0:T(8,128)(2,1)S(1)} %copy-done, bf16[32,768]{1,0:T(8,128)(2,1)S(1)} %copy-done.1, bf16[4,192,192]{2,1,0:T(8,128)(2,1)S(1)} %copy-done.3), custom_call_target="tpu_custom_call" | custom-call | flops 1000000000 | bytes 1048576 | tf_op jit(solution)/shard_map/pallas_call | solution.py:65
  9.8 0.0 collective-permute-done.other_ref
  9.8 0.0 copy-start.2
  9.8 2.3 %shard_map.78 = (f32[4,96,192]{2,1,0:T(8,128)S(1)}, bf16[144,128]{1,0:T(8,128)(2,1)S(1)}, bf16[144,128]{1,0:T(8,128)(2,1)S(1)}, bf16[144,128]{1,0:T(8,128)(2,1)S(1)}, bf16[144,128]{1,0:T(8,128)(2,1)S(1)}) custom-call(bf16[96,768]{1,0:T(8,128)(2,1)S(1)} %collective-permute-done.other_ref, bf16[4,192,192]{2,1,0:T(8,128)(2,1)S(1)} %copy-done.4, ...), custom_call_target="tpu_custom_call" | custom-call | flops 1000000000 | bytes 1048576 | tf_op jit(solution)/shard_map/pallas_call | solution.py:65
  12.1 1.7 %collective-permute-start.1 = (bf16[144,128]{1,0:T(8,128)(2,1)S(1)}, bf16[144,128]{1,0:T(8,128)(2,1)S(1)}, u32[]{:S(2)}, u32[]{:S(2)}) collective-permute-start(bf16[144,128]{1,0:T(8,128)(2,1)S(1)} %get-tuple-element.34), channel_id=1, source_target_pairs={{0,4},{4,0},{128,132},{132,128},{1,5},{5,1},{129,133},{133,129},{2... | collective-permute-start | bytes 110600 | tf_op jit(solution)/shard_map/ppermute | solution.py:221
  13.9 0.4 collective-permute-start.2
  14.3 0.9 collective-permute-start.3
  15.2 0.1 collective-permute-done.1.refs_1_
  15.2 1.5 %collective-permute-done.2.refs_2_ = bf16[144,128]{1,0:T(8,128)(2,1)S(1)} collective-permute-done((bf16[144,128]{1,0:T(8,128)(2,1)S(1)}, bf16[144,128]{1,0:T(8,128)(2,1)S(1)}, u32[]{:S(2)}, u32[]{:S(2)}) %collective-permute-start.2) | collective-permute-done | bytes 36896 | tf_op jit(solution)/shard_map/ppermute | solution.py:221
  16.7 1.3 %collective-permute-done.3.refs_3_ = bf16[144,128]{1,0:T(8,128)(2,1)S(1)} collective-permute-done((bf16[144,128]{1,0:T(8,128)(2,1)S(1)}, bf16[144,128]{1,0:T(8,128)(2,1)S(1)}, u32[]{:S(2)}, u32[]{:S(2)}) %collective-permute-start.3) | collective-permute-done | bytes 36896 | tf_op jit(solution)/shard_map/ppermute | solution.py:221
  18.0 3.1 %collective-permute-start.7 = (bf16[4,144,128]{2,1,0:T(8,128)(2,1)S(1)}, bf16[4,144,128]{2,1,0:T(8,128)(2,1)S(1)}, u32[]{:S(2)}, u32[]{:S(2)}) collective-permute-start(bf16[4,144,128]{2,1,0:T(8,128)(2,1)S(1)} %get-tuple-element.38.own_ref), channel_id=1, source_target_pairs={{0,2},{2,0},{1,3},{3,1},{4,6},{6,4},{5,7},{7,5},{8,10},{10,8},{9,1... | collective-permute-start | bytes 442376 | tf_op jit(solution)/shard_map/ppermute | solution.py:472
  21.2 3.0 %collective-permute-start.4 = (bf16[384,128]{1,0:T(8,128)(2,1)S(1)}, bf16[384,128]{1,0:T(8,128)(2,1)S(1)}, u32[]{:S(2)}, u32[]{:S(2)}) collective-permute-start(bf16[384,128]{1,0:T(8,128)(2,1)S(1)} %get-tuple-element.37.upper_ref), channel_id=1, source_target_pairs={{0,8},{8,16},{16,24},{24,0},{1,9},{9,17},{17,25},{25,1},{2,10},{10... | collective-permute-start | bytes 294920 | tf_op jit(solution)/shard_map/ppermute | solution.py:471
  24.2 2.1 %collective-permute-start.5 = (bf16[384,128]{1,0:T(8,128)(2,1)S(1)}, bf16[384,128]{1,0:T(8,128)(2,1)S(1)}, u32[]{:S(2)}, u32[]{:S(2)}) collective-permute-start(bf16[384,128]{1,0:T(8,128)(2,1)S(1)} %get-tuple-element.37.upper_ref), channel_id=1, source_target_pairs={{0,24},{8,0},{16,8},{24,16},{1,25},{9,1},{17,9},{25,17},{2,26},{10... | collective-permute-start | bytes 294920 | tf_op jit(solution)/shard_map/ppermute | solution.py:471
  26.3 4.5 %collective-permute-start.6 = (bf16[384,128]{1,0:T(8,128)(2,1)S(1)}, bf16[384,128]{1,0:T(8,128)(2,1)S(1)}, u32[]{:S(2)}, u32[]{:S(2)}) collective-permute-start(bf16[384,128]{1,0:T(8,128)(2,1)S(1)} %get-tuple-element.37.upper_ref), channel_id=1, source_target_pairs={{0,16},{8,24},{16,0},{24,8},{1,17},{9,25},{17,1},{25,9},{2,18},{10... | collective-permute-start | bytes 294920 | tf_op jit(solution)/shard_map/ppermute | solution.py:471
  30.7 0.0 collective-permute-done.4.lower_ref
  30.8 1.3 %collective-permute-start.8 = (bf16[768,128]{1,0:T(8,128)(2,1)S(1)}, bf16[768,128]{1,0:T(8,128)(2,1)S(1)}, u32[]{:S(2)}, u32[]{:S(2)}) collective-permute-start(bf16[768,128]{1,0:T(8,128)(2,1)S(1)} %shard_map.80.refs_0_.refs_2_), channel_id=1, source_target_pairs={{0,32},{32,64},{64,96},{96,0},{1,33},{33,65},{65,97},{97,1},{2,34}... | collective-permute-start | bytes 589832 | tf_op jit(solution)/shard_map/ppermute | solution.py:474
  32.1 1.5 %collective-permute-start.12 = (bf16[768,128]{1,0:T(8,128)(2,1)S(1)}, bf16[768,128]{1,0:T(8,128)(2,1)S(1)}, u32[]{:S(2)}, u32[]{:S(2)}) collective-permute-start(bf16[768,128]{1,0:T(8,128)(2,1)S(1)} %shard_map.80.refs_0_.refs_2_), channel_id=1, source_target_pairs={{0,96},{32,0},{64,32},{96,64},{1,97},{33,1},{65,33},{97,65},{2,98}... | collective-permute-start | bytes 589832 | tf_op jit(solution)/shard_map/ppermute | solution.py:475
  33.5 1.8 %shard_map.81 = (bf16[6,208,768]{2,1,0:T(8,128)(2,1)S(1)}, bf16[192,192]{1,0:T(8,128)(2,1)S(1)}) custom-call(bf16[4,144,128]{2,1,0:T(8,128)(2,1)S(1)} %get-tuple-element.38.own_ref, bf16[4,144,128]{2,1,0:T(8,128)(2,1)S(1)} %collective-permute-done.7.other_ref, bf16[4,192,192]{2,1,0:T(8,128)(2,1)S(1)} %copy-done.2), custom_call_target="tpu_custom_call" | custom-call | flops 1000000000 | bytes 1048576 | tf_op jit(solution)/shard_map/pallas_call | solution.py:65
  35.4 0.0 collective-permute-done.5.upper_ref
  35.4 0.0 collective-permute-done.6.lower_ref
  35.4 1.3 %collective-permute-start.9 = (bf16[768,128]{1,0:T(8,128)(2,1)S(1)}, bf16[768,128]{1,0:T(8,128)(2,1)S(1)}, u32[]{:S(2)}, u32[]{:S(2)}) collective-permute-start(bf16[768,128]{1,0:T(8,128)(2,1)S(1)} %shard_map.82.refs_1_.refs_3_), channel_id=1, source_target_pairs={{0,96},{32,0},{64,32},{96,64},{1,97},{33,1},{65,33},{97,65},{2,98}... | collective-permute-start | bytes 589832 | tf_op jit(solution)/shard_map/ppermute | solution.py:488
  36.8 0.2 collective-permute-start.13
  37.0 4.1 %shard_map.83.refs_6_ = f32[6,48,768]{2,1,0:T(8,128)S(1)} custom-call(bf16[768,128]{1,0:T(8,128)(2,1)S(1)} %shard_map.80.refs_0_.refs_2_, bf16[768,128]{1,0:T(8,128)(2,1)S(1)} %shard_map.82.refs_1_.refs_3_, bf16[192,192]{1,0:T(8,128)(2,1)S(1)} %get-tuple-element.42.refs_2_.refs_4_.refs_8_, bf16[6,208,768]{2,1,0:T(8,128)(2,1)S(1)} %get-tuple-element.43.refs_3_.refs_5_.refs_9_), custom_call_target="tpu_custom_call" | custom-call | flops 3623878656 | bytes 1048576 | tf_op jit(solution)/shard_map/pallas_call | solution.py:65
  41.1 0.0 collective-permute-done.8.refs_0_.refs_4_
  41.1 0.0 collective-permute-done.9.refs_3_.refs_7_
  41.1 0.9 collective-permute-start.10
  42.0 1.9 %collective-permute-start.11 = (bf16[768,128]{1,0:T(8,128)(2,1)S(1)}, bf16[768,128]{1,0:T(8,128)(2,1)S(1)}, u32[]{:S(2)}, u32[]{:S(2)}) collective-permute-start(bf16[768,128]{1,0:T(8,128)(2,1)S(1)} %collective-permute-done.9.refs_3_.refs_7_), channel_id=1, source_target_pairs={{0,96},{32,0},{64,32},{96,64},{1,97},{33,1},{65,33},{97,65},{2,98}... | collective-permute-start | bytes 589832 | tf_op jit(solution)/shard_map/ppermute | solution.py:492
  43.9 0.0 collective-permute-done.12.refs_1_.refs_5_
  44.0 0.0 collective-permute-done.13.refs_2_.refs_6_
  44.0 8.0 %shard_map.84.refs_10_ = f32[6,48,768]{2,1,0:T(8,128)S(1)} custom-call(bf16[768,128]{1,0:T(8,128)(2,1)S(1)} %collective-permute-done.8.refs_0_.refs_4_, bf16[768,128]{1,0:T(8,128)(2,1)S(1)} %collective-permute-done.12.refs_1_.refs_5_, bf16[768,128]{1,0:T(8,128)(2,1)S(1)} %collective-permute-done.13.refs_2_.refs_6_, ...), custom_call_target="tpu_custom_call" | custom-call | flops 7247757312 | bytes 1048576 | tf_op jit(solution)/shard_map/pallas_call | solution.py:65
  51.9 0.0 copy-start.6
  51.9 0.0 copy-start.5
  52.0 36.6 %shard_map.85 = (f32[6,40,384]{2,1,0:T(8,128)S(1)}, f32[6,40,384]{2,1,0:T(8,128)S(1)}) custom-call(bf16[768,128]{1,0:T(8,128)(2,1)S(1)} %collective-permute-done.10.refs_0_, bf16[768,128]{1,0:T(8,128)(2,1)S(1)} %collective-permute-done.11.refs_1_, bf16[768,128]{1,0:T(8,128)(2,1)S(1)} %shard_map.80.refs_0_.refs_2_, ...), custom_call_target="tpu_custom_call" | custom-call | flops 3623878656 | bytes 1048576 | tf_op jit(solution)/shard_map/pallas_call | solution.py:65
  88.6 5.8 %collective-permute-start.14 = (f32[6,40,384]{2,1,0:T(8,128)S(1)}, f32[6,40,384]{2,1,0:T(8,128)S(1)}, u32[]{:S(2)}, u32[]{:S(2)}) collective-permute-start(f32[6,40,384]{2,1,0:T(8,128)S(1)} %get-tuple-element.48), channel_id=1, source_target_pairs={{0,2},{2,0},{1,3},{3,1},{4,6},{6,4},{5,7},{7,5},{8,10},{10,8},{9,1... | collective-permute-start | bytes 1105928 | tf_op jit(solution)/shard_map/ppermute | solution.py:497
  94.4 1.3 %collective-permute-done.14.came_ref = f32[6,40,384]{2,1,0:T(8,128)S(1)} collective-permute-done((f32[6,40,384]{2,1,0:T(8,128)S(1)}, f32[6,40,384]{2,1,0:T(8,128)S(1)}, u32[]{:S(2)}, u32[]{:S(2)}) %collective-permute-start.14) | collective-permute-done | bytes 368672 | tf_op jit(solution)/shard_map/ppermute | solution.py:497
  95.7 0.2 shard_map.86
  95.9 2.0 %collective-permute-start.15 = (bf16[144,128]{1,0:T(8,128)(2,1)S(1)}, bf16[144,128]{1,0:T(8,128)(2,1)S(1)}, u32[]{:S(2)}, u32[]{:S(2)}) collective-permute-start(bf16[144,128]{1,0:T(8,128)(2,1)S(1)} %get-tuple-element.50), channel_id=1, source_target_pairs={{0,4},{4,0},{128,132},{132,128},{1,5},{5,1},{129,133},{133,129},{2... | collective-permute-start | bytes 110600 | tf_op jit(solution)/shard_map/ppermute | solution.py:221
  97.9 0.6 collective-permute-start.16
  98.6 0.6 collective-permute-start.17
  99.2 0.2 copy.8.refs_7_
  99.4 1.3 %collective-permute-done.16.refs_2_ = bf16[144,128]{1,0:T(8,128)(2,1)S(1)} collective-permute-done((bf16[144,128]{1,0:T(8,128)(2,1)S(1)}, bf16[144,128]{1,0:T(8,128)(2,1)S(1)}, u32[]{:S(2)}, u32[]{:S(2)}) %collective-permute-start.16) | collective-permute-done | bytes 36896 | tf_op jit(solution)/shard_map/ppermute | solution.py:221
  100.8 1.5 %collective-permute-done.17.refs_3_ = bf16[144,128]{1,0:T(8,128)(2,1)S(1)} collective-permute-done((bf16[144,128]{1,0:T(8,128)(2,1)S(1)}, bf16[144,128]{1,0:T(8,128)(2,1)S(1)}, u32[]{:S(2)}, u32[]{:S(2)}) %collective-permute-start.17) | collective-permute-done | bytes 36896 | tf_op jit(solution)/shard_map/ppermute | solution.py:221
  102.3 1.7 %shard_map.87 = (bf16[64,768]{1,0:T(8,128)(2,1)}, bf16[32,768]{1,0:T(8,128)(2,1)}) custom-call(bf16[144,128]{1,0:T(8,128)(2,1)S(1)} %get-tuple-element.49.refs_0_, bf16[144,128]{1,0:T(8,128)(2,1)S(1)} %collective-permute-done.15.refs_1_, bf16[144,128]{1,0:T(8,128)(2,1)S(1)} %collective-permute-done.16.refs_2_, ...), custom_call_target="tpu_custom_call" | custom-call | flops 1000000000 | bytes 1048576 | tf_op jit(solution)/shard_map/pallas_call | solution.py:65
  (16 shorter events, 0.1 us)
Async XLA Ops:
  1.6 8.2 %collective-permute-start = (bf16[96,768]{1,0:T(8,128)(2,1)S(1)}, bf16[96,768]{1,0:T(8,128)(2,1)S(1)}, u32[]{:S(2)}, u32[]{:S(2)}) collective-permute-start(bf16[96,768]{1,0:T(8,128)(2,1)S(1)} %pad_maximum_fusion), channel_id=1, source_target_pairs={{0,1},{1,0},{2,3},{3,2},{4,5},{5,4},{6,7},{7,6},{8,9},{9,8},{10,11... | collective-permute-start | bytes 442376 | tf_op jit(solution)/shard_map/ppermute | solution.py:439
  5.4 0.9 copy-start
  6.3 0.8 copy-start.1
  7.1 1.0 copy-start.3
  8.1 1.7 %copy-start.4 = (bf16[4,192,192]{2,1,0:T(8,128)(2,1)S(1)}, bf16[4,192,192]{2,1,0:T(8,128)(2,1)}, u32[]{:S(2)}) copy-start(bf16[4,192,192]{2,1,0:T(8,128)(2,1)} %weights_ref.4) | copy-start | bytes 884740
  9.8 23.8 %copy-start.2 = (bf16[4,192,192]{2,1,0:T(8,128)(2,1)S(1)}, bf16[4,192,192]{2,1,0:T(8,128)(2,1)}, u32[]{:S(2)}) copy-start(bf16[4,192,192]{2,1,0:T(8,128)(2,1)} %weights_ref.5) | copy-start | bytes 884740
  12.1 3.1 %collective-permute-start.1 = (bf16[144,128]{1,0:T(8,128)(2,1)S(1)}, bf16[144,128]{1,0:T(8,128)(2,1)S(1)}, u32[]{:S(2)}, u32[]{:S(2)}) collective-permute-start(bf16[144,128]{1,0:T(8,128)(2,1)S(1)} %get-tuple-element.34), channel_id=1, source_target_pairs={{0,4},{4,0},{128,132},{132,128},{1,5},{5,1},{129,133},{133,129},{2... | collective-permute-start | bytes 110600 | tf_op jit(solution)/shard_map/ppermute | solution.py:221
  13.9 2.8 %collective-permute-start.2 = (bf16[144,128]{1,0:T(8,128)(2,1)S(1)}, bf16[144,128]{1,0:T(8,128)(2,1)S(1)}, u32[]{:S(2)}, u32[]{:S(2)}) collective-permute-start(bf16[144,128]{1,0:T(8,128)(2,1)S(1)} %get-tuple-element.35), channel_id=1, source_target_pairs={{0,128},{4,132},{128,0},{132,4},{1,129},{5,133},{129,1},{133,5},{2... | collective-permute-start | bytes 110600 | tf_op jit(solution)/shard_map/ppermute | solution.py:221
  14.3 3.7 %collective-permute-start.3 = (bf16[144,128]{1,0:T(8,128)(2,1)S(1)}, bf16[144,128]{1,0:T(8,128)(2,1)S(1)}, u32[]{:S(2)}, u32[]{:S(2)}) collective-permute-start(bf16[144,128]{1,0:T(8,128)(2,1)S(1)} %get-tuple-element.36), channel_id=1, source_target_pairs={{0,132},{4,128},{128,4},{132,0},{1,133},{5,129},{129,5},{133,1},{2... | collective-permute-start | bytes 110600 | tf_op jit(solution)/shard_map/ppermute | solution.py:221
  18.0 15.5 %collective-permute-start.7 = (bf16[4,144,128]{2,1,0:T(8,128)(2,1)S(1)}, bf16[4,144,128]{2,1,0:T(8,128)(2,1)S(1)}, u32[]{:S(2)}, u32[]{:S(2)}) collective-permute-start(bf16[4,144,128]{2,1,0:T(8,128)(2,1)S(1)} %get-tuple-element.38.own_ref), channel_id=1, source_target_pairs={{0,2},{2,0},{1,3},{3,1},{4,6},{6,4},{5,7},{7,5},{8,10},{10,8},{9,1... | collective-permute-start | bytes 442376 | tf_op jit(solution)/shard_map/ppermute | solution.py:472
  21.2 9.6 %collective-permute-start.4 = (bf16[384,128]{1,0:T(8,128)(2,1)S(1)}, bf16[384,128]{1,0:T(8,128)(2,1)S(1)}, u32[]{:S(2)}, u32[]{:S(2)}) collective-permute-start(bf16[384,128]{1,0:T(8,128)(2,1)S(1)} %get-tuple-element.37.upper_ref), channel_id=1, source_target_pairs={{0,8},{8,16},{16,24},{24,0},{1,9},{9,17},{17,25},{25,1},{2,10},{10... | collective-permute-start | bytes 294920 | tf_op jit(solution)/shard_map/ppermute | solution.py:471
  24.2 11.2 %collective-permute-start.5 = (bf16[384,128]{1,0:T(8,128)(2,1)S(1)}, bf16[384,128]{1,0:T(8,128)(2,1)S(1)}, u32[]{:S(2)}, u32[]{:S(2)}) collective-permute-start(bf16[384,128]{1,0:T(8,128)(2,1)S(1)} %get-tuple-element.37.upper_ref), channel_id=1, source_target_pairs={{0,24},{8,0},{16,8},{24,16},{1,25},{9,1},{17,9},{25,17},{2,26},{10... | collective-permute-start | bytes 294920 | tf_op jit(solution)/shard_map/ppermute | solution.py:471
  26.3 9.1 %collective-permute-start.6 = (bf16[384,128]{1,0:T(8,128)(2,1)S(1)}, bf16[384,128]{1,0:T(8,128)(2,1)S(1)}, u32[]{:S(2)}, u32[]{:S(2)}) collective-permute-start(bf16[384,128]{1,0:T(8,128)(2,1)S(1)} %get-tuple-element.37.upper_ref), channel_id=1, source_target_pairs={{0,16},{8,24},{16,0},{24,8},{1,17},{9,25},{17,1},{25,9},{2,18},{10... | collective-permute-start | bytes 294920 | tf_op jit(solution)/shard_map/ppermute | solution.py:471
  30.8 10.3 %collective-permute-start.8 = (bf16[768,128]{1,0:T(8,128)(2,1)S(1)}, bf16[768,128]{1,0:T(8,128)(2,1)S(1)}, u32[]{:S(2)}, u32[]{:S(2)}) collective-permute-start(bf16[768,128]{1,0:T(8,128)(2,1)S(1)} %shard_map.80.refs_0_.refs_2_), channel_id=1, source_target_pairs={{0,32},{32,64},{64,96},{96,0},{1,33},{33,65},{65,97},{97,1},{2,34}... | collective-permute-start | bytes 589832 | tf_op jit(solution)/shard_map/ppermute | solution.py:474
  32.1 11.9 %collective-permute-start.12 = (bf16[768,128]{1,0:T(8,128)(2,1)S(1)}, bf16[768,128]{1,0:T(8,128)(2,1)S(1)}, u32[]{:S(2)}, u32[]{:S(2)}) collective-permute-start(bf16[768,128]{1,0:T(8,128)(2,1)S(1)} %shard_map.80.refs_0_.refs_2_), channel_id=1, source_target_pairs={{0,96},{32,0},{64,32},{96,64},{1,97},{33,1},{65,33},{97,65},{2,98}... | collective-permute-start | bytes 589832 | tf_op jit(solution)/shard_map/ppermute | solution.py:475
  35.4 5.6 %collective-permute-start.9 = (bf16[768,128]{1,0:T(8,128)(2,1)S(1)}, bf16[768,128]{1,0:T(8,128)(2,1)S(1)}, u32[]{:S(2)}, u32[]{:S(2)}) collective-permute-start(bf16[768,128]{1,0:T(8,128)(2,1)S(1)} %shard_map.82.refs_1_.refs_3_), channel_id=1, source_target_pairs={{0,96},{32,0},{64,32},{96,64},{1,97},{33,1},{65,33},{97,65},{2,98}... | collective-permute-start | bytes 589832 | tf_op jit(solution)/shard_map/ppermute | solution.py:488
  36.8 7.2 %collective-permute-start.13 = (bf16[768,128]{1,0:T(8,128)(2,1)S(1)}, bf16[768,128]{1,0:T(8,128)(2,1)S(1)}, u32[]{:S(2)}, u32[]{:S(2)}) collective-permute-start(bf16[768,128]{1,0:T(8,128)(2,1)S(1)} %shard_map.82.refs_1_.refs_3_), channel_id=1, source_target_pairs={{0,32},{32,64},{64,96},{96,0},{1,33},{33,65},{65,97},{97,1},{2,34}... | collective-permute-start | bytes 589832 | tf_op jit(solution)/shard_map/ppermute | solution.py:487
  41.1 10.9 %collective-permute-start.10 = (bf16[768,128]{1,0:T(8,128)(2,1)S(1)}, bf16[768,128]{1,0:T(8,128)(2,1)S(1)}, u32[]{:S(2)}, u32[]{:S(2)}) collective-permute-start(bf16[768,128]{1,0:T(8,128)(2,1)S(1)} %collective-permute-done.8.refs_0_.refs_4_), channel_id=1, source_target_pairs={{0,32},{32,64},{64,96},{96,0},{1,33},{33,65},{65,97},{97,1},{2,34}... | collective-permute-start | bytes 589832 | tf_op jit(solution)/shard_map/ppermute | solution.py:491
  42.0 10.0 %collective-permute-start.11 = (bf16[768,128]{1,0:T(8,128)(2,1)S(1)}, bf16[768,128]{1,0:T(8,128)(2,1)S(1)}, u32[]{:S(2)}, u32[]{:S(2)}) collective-permute-start(bf16[768,128]{1,0:T(8,128)(2,1)S(1)} %collective-permute-done.9.refs_3_.refs_7_), channel_id=1, source_target_pairs={{0,96},{32,0},{64,32},{96,64},{1,97},{33,1},{65,33},{97,65},{2,98}... | collective-permute-start | bytes 589832 | tf_op jit(solution)/shard_map/ppermute | solution.py:492
  51.9 47.3 %copy-start.6 = (bf16[768,192]{0,1:T(8,128)(2,1)S(1)}, bf16[768,192]{0,1:T(8,128)(2,1)}, u32[]{:S(2)}) copy-start(bf16[768,192]{0,1:T(8,128)(2,1)} %param.11) | copy-start | bytes 884740
  51.9 50.4 %copy-start.5 = (bf16[192,768]{1,0:T(8,128)(2,1)S(1)}, bf16[192,768]{1,0:T(8,128)(2,1)}, u32[]{:S(2)}) copy-start(bf16[192,768]{1,0:T(8,128)(2,1)} %refs_6_.1) | copy-start | bytes 884740
  88.6 7.1 %collective-permute-start.14 = (f32[6,40,384]{2,1,0:T(8,128)S(1)}, f32[6,40,384]{2,1,0:T(8,128)S(1)}, u32[]{:S(2)}, u32[]{:S(2)}) collective-permute-start(f32[6,40,384]{2,1,0:T(8,128)S(1)} %get-tuple-element.48), channel_id=1, source_target_pairs={{0,2},{2,0},{1,3},{3,1},{4,6},{6,4},{5,7},{7,5},{8,10},{10,8},{9,1... | collective-permute-start | bytes 1105928 | tf_op jit(solution)/shard_map/ppermute | solution.py:497
  95.9 3.5 %collective-permute-start.15 = (bf16[144,128]{1,0:T(8,128)(2,1)S(1)}, bf16[144,128]{1,0:T(8,128)(2,1)S(1)}, u32[]{:S(2)}, u32[]{:S(2)}) collective-permute-start(bf16[144,128]{1,0:T(8,128)(2,1)S(1)} %get-tuple-element.50), channel_id=1, source_target_pairs={{0,4},{4,0},{128,132},{132,128},{1,5},{5,1},{129,133},{133,129},{2... | collective-permute-start | bytes 110600 | tf_op jit(solution)/shard_map/ppermute | solution.py:221
  97.9 2.8 %collective-permute-start.16 = (bf16[144,128]{1,0:T(8,128)(2,1)S(1)}, bf16[144,128]{1,0:T(8,128)(2,1)S(1)}, u32[]{:S(2)}, u32[]{:S(2)}) collective-permute-start(bf16[144,128]{1,0:T(8,128)(2,1)S(1)} %get-tuple-element.51), channel_id=1, source_target_pairs={{0,128},{4,132},{128,0},{132,4},{1,129},{5,133},{129,1},{133,5},{2... | collective-permute-start | bytes 110600 | tf_op jit(solution)/shard_map/ppermute | solution.py:221
  98.6 3.7 %collective-permute-start.17 = (bf16[144,128]{1,0:T(8,128)(2,1)S(1)}, bf16[144,128]{1,0:T(8,128)(2,1)S(1)}, u32[]{:S(2)}, u32[]{:S(2)}) collective-permute-start(bf16[144,128]{1,0:T(8,128)(2,1)S(1)} %get-tuple-element.52), channel_id=1, source_target_pairs={{0,132},{4,128},{128,4},{132,0},{1,133},{5,129},{129,5},{133,1},{2... | collective-permute-start | bytes 110600 | tf_op jit(solution)/shard_map/ppermute | solution.py:221

commit v4 on v3

--- a/solution.py
+++ b/solution.py
@@ -122,8 +122,7 @@
 
 
 def near_kernel(
-    train_ref,
-    test_ref,
+    joined_ref,
     weights_ref,
     cells_ref,
     query_ref,
@@ -133,9 +132,7 @@
 ):
     parts = []
     for index in range(GROUPS):
-        span = slice(index * E, (index + 1) * E)
-        cell = [one_ref[:, span].astype(f32) for one_ref in (train_ref, test_ref)]
-        cell = jnp.concatenate(cell, axis=0)
+        cell = joined_ref[:, index * E : (index + 1) * E].astype(f32)
         cells_ref[index] = cell
         parts.append(layer_norm(cell).astype(bf16))
     normed = jnp.concatenate(parts, axis=0)
@@ -227,14 +224,19 @@
     parts = [unpack(one_ref[index]) for one_ref in (own_ref, other_ref) for index in range(GROUPS)]
     asked = jnp.concatenate(parts, axis=0).astype(bf16)
     probes = jnp.concatenate([parts[0][:PROBES], parts[GROUPS][:PROBES]], axis=0).astype(bf16)
-    queries = (mm(asked, weights_ref[0]) * log2_scale).astype(bf16)
-    weight = weights_ref[1]
+    turned = weights_ref[0].astype(f32).T.astype(bf16)
+    queries = (mm_nt(turned, asked) * log2_scale).astype(bf16)
+    weight = weights_ref[1].astype(f32)
+    probed = mm(probes, weights_ref[1])
+    head_of = lax.broadcasted_iota(jnp.int32, (1, E), 1) >> 5
+    masks = [jnp.where(head_of == head, 1.0, 0.0) for head in range(HEADS)]
+    stacked = [weight * mask for mask in masks] + [probed * mask for mask in masks]
+    folded = mm(jnp.concatenate(stacked, axis=0).astype(bf16), queries)
     row = lax.broadcasted_iota(jnp.int32, (FOLD - E, ALL_Q), 0)
     for head in range(HEADS):
-        part = slice(head * HD, (head + 1) * HD)
-        folded = mm_nt(weight[:, part], queries[:, part]).astype(bf16)
-        peak = jnp.max(mm(probes, folded), axis=0, keepdims=True)
-        folded_ref[head, :E, :] = folded
+        folded_ref[head, :E, :] = folded[head * E : (head + 1) * E].astype(bf16)
+        low = HEADS * E + head * 2 * PROBES
+        peak = jnp.max(folded[low : low + 2 * PROBES], axis=0, keepdims=True)
         folded_ref[head, E:, :] = jnp.where(row == 0, -peak, 0.0).astype(bf16)
 
 
@@ -435,7 +437,9 @@
 
 def layer(train_cells, test_cells, feat_weights, row_weights, mlp_up, mlp_down):
     swap = [(0, 1), (1, 0)]
-    joined = jnp.concatenate([train_cells, test_cells], axis=0)
+    low = jnp.array(-jnp.inf, bf16)
+    upper = lax.pad(train_cells, low, ((0, TEST_ROWS, 0), (0, 0, 0)))
+    joined = jnp.maximum(upper, lax.pad(test_cells, low, ((TRAIN_ROWS, 0, 0), (0, 0, 0))))
     other = lax.ppermute(joined, "feat", swap)
     near = call(
         near_kernel,
@@ -446,7 +450,7 @@
             jax.ShapeDtypeStruct((GROUPS, ROWS, 128), f32),
             jax.ShapeDtypeStruct((GROUPS, ROWS, E), f32),
         ],
-        (train_cells, test_cells, feat_weights),
+        (joined, feat_weights),
         10**9,
     )
     after_feat, *pieces = call(
@@ -487,7 +491,8 @@
     late_above = lax.ppermute(late, "x", shift(4, 1))
     late_below = lax.ppermute(late, "x", shift(4, 3))
     mix = attend((early, late), (value_turned, folded))
-    mix, early_above, late_below = lax.optimization_barrier((mix, early_above, late_below))
+    mix, early_above = lax.optimization_barrier((mix, early_above))
+    mix, late_below = lax.optimization_barrier((mix, late_below))
     far_early = lax.ppermute(early_above, "x", shift(4, 1))
     far_late = lax.ppermute(late_below, "x", shift(4, 3))
     middle = (early_above, early_below, late_above, late_below)

time: 104 us -> 104 us (level)
  local copies, waits for them, and re-layouts: 2.89 us -> 1.19 us
  starting transfers between devices: 35.8 us -> 37.3 us
    unnamed x15 -> x9, local copies, waits for them, and re-layouts: 2.88 us -> 1.18 us
  transfers between devices with their start and end apart: 18 -> 18, of which waited for: 6 -> 5; matrix products, arithmetic and copies ran while one was open for 0% -> 0% of each run, Pallas kernels for 15% -> 14%
where the time goes in v4:
time: 104 us; the launch traced here: 103 us
  Pallas kernels  55.6 us (53%)
  starting transfers between devices  37.3 us (36%)
  waiting for transfers between devices  7.51 us (7%)
  local copies, waits for them, and re-layouts  1.19 us (1%)
    pallas_call x11, Pallas kernels, call(): pl.pallas_call(kernel, out_shape=outs, in_specs=[in_vmem] * len(args), ou...  55.6 us
    ppermute x3, starting transfers between devices, layer(): column.append(lax.ppermute(keys, 'z_hi', shift(SIDE, by)))  9.59 us
    ppermute x6, starting transfers between devices, exchange(): came.append(lax.ppermute(pieces[turn], classes, pairs))  7.02 us
    ppermute x6, waiting for transfers between devices, exchange(): came.append(lax.ppermute(pieces[turn], classes, pairs))  6.17 us
    ppermute x1, starting transfers between devices, layer(): came = lax.ppermute(leave, 'core', swap)  5.84 us
    ppermute x1, starting transfers between devices, layer(): other = lax.ppermute(joined, 'feat', swap)  3.82 us
    ppermute x1, starting transfers between devices, layer(): received_other = lax.ppermute(received, 'core', swap)  3.29 us
    ppermute x1, starting transfers between devices, layer(): far_late = lax.ppermute(late_below, 'x', shift(4, 3))  2.61 us
  transfers between devices with their start and end apart: 18, of which 5 were waited for; matrix products, arithmetic and copies ran while one was open for 0% of the time, Pallas kernels for 14%

profile of v4, /device:TPU:1, one launch (start us, length us, event | category | flops | bytes accessed | tf_op | source)
XLA Modules:
  0.0 103.4 jit_solution(11208516974604016101)
XLA Ops:
  0.6 0.9 pad_maximum_fusion.joined_ref
  1.6 3.8 %collective-permute-start = (bf16[96,768]{1,0:T(8,128)(2,1)S(1)}, bf16[96,768]{1,0:T(8,128)(2,1)S(1)}, u32[]{:S(2)}, u32[]{:S(2)}) collective-permute-start(bf16[96,768]{1,0:T(8,128)(2,1)S(1)} %pad_maximum_fusion.joined_ref), channel_id=1, source_target_pairs={{0,1},{1,0},{2,3},{3,2},{4,5},{5,4},{6,7},{7,6},{8,9},{9,8},{10,11... | collective-permute-start | bytes 442376 | tf_op jit(solution)/shard_map/ppermute | solution.py:443
  5.4 1.0 copy-done.1
  6.4 1.7 %shard_map.77 = (f32[4,96,192]{2,1,0:T(8,128)S(1)}, bf16[384,192]{1,0:T(8,128)(2,1)S(1)}, f32[4,96,128]{2,1,0:T(8,128)S(1)}, f32[4,96,128]{2,1,0:T(8,128)S(1)}, f32[4,96,192]{2,1,0:T(8,128)S(1)}) custom-call(bf16[96,768]{1,0:T(8,128)(2,1)S(1)} %pad_maximum_fusion.joined_ref, bf16[4,192,192]{2,1,0:T(8,128)(2,1)S(1)} %copy-done.1), custom_call_target="tpu_custom_call" | custom-call | flops 1000000000 | bytes 1048576 | tf_op jit(solution)/shard_map/pallas_call | solution.py:65
  8.1 0.0 collective-permute-done.other_ref
  8.1 0.0 copy-start
  8.1 2.3 %shard_map.78 = (f32[4,96,192]{2,1,0:T(8,128)S(1)}, bf16[144,128]{1,0:T(8,128)(2,1)S(1)}, bf16[144,128]{1,0:T(8,128)(2,1)S(1)}, bf16[144,128]{1,0:T(8,128)(2,1)S(1)}, bf16[144,128]{1,0:T(8,128)(2,1)S(1)}) custom-call(bf16[96,768]{1,0:T(8,128)(2,1)S(1)} %collective-permute-done.other_ref, bf16[4,192,192]{2,1,0:T(8,128)(2,1)S(1)} %copy-done.1, ...), custom_call_target="tpu_custom_call" | custom-call | flops 1000000000 | bytes 1048576 | tf_op jit(solution)/shard_map/pallas_call | solution.py:65
  10.4 2.3 %collective-permute-start.1 = (bf16[144,128]{1,0:T(8,128)(2,1)S(1)}, bf16[144,128]{1,0:T(8,128)(2,1)S(1)}, u32[]{:S(2)}, u32[]{:S(2)}) collective-permute-start(bf16[144,128]{1,0:T(8,128)(2,1)S(1)} %get-tuple-element.35), channel_id=1, source_target_pairs={{0,4},{4,0},{128,132},{132,128},{1,5},{5,1},{129,133},{133,129},{2... | collective-permute-start | bytes 110600 | tf_op jit(solution)/shard_map/ppermute | solution.py:218
  12.8 1.3 %collective-permute-start.2 = (bf16[144,128]{1,0:T(8,128)(2,1)S(1)}, bf16[144,128]{1,0:T(8,128)(2,1)S(1)}, u32[]{:S(2)}, u32[]{:S(2)}) collective-permute-start(bf16[144,128]{1,0:T(8,128)(2,1)S(1)} %get-tuple-element.36), channel_id=1, source_target_pairs={{0,128},{4,132},{128,0},{132,4},{1,129},{5,133},{129,1},{133,5},{2... | collective-permute-start | bytes 110600 | tf_op jit(solution)/shard_map/ppermute | solution.py:218
  14.1 0.0 collective-permute-start.3
  14.1 0.0 collective-permute-done.1.refs_1_
  14.1 1.5 %collective-permute-done.2.refs_2_ = bf16[144,128]{1,0:T(8,128)(2,1)S(1)} collective-permute-done((bf16[144,128]{1,0:T(8,128)(2,1)S(1)}, bf16[144,128]{1,0:T(8,128)(2,1)S(1)}, u32[]{:S(2)}, u32[]{:S(2)}) %collective-permute-start.2) | collective-permute-done | bytes 36896 | tf_op jit(solution)/shard_map/ppermute | solution.py:218
  15.6 2.2 %collective-permute-done.3.refs_3_ = bf16[144,128]{1,0:T(8,128)(2,1)S(1)} collective-permute-done((bf16[144,128]{1,0:T(8,128)(2,1)S(1)}, bf16[144,128]{1,0:T(8,128)(2,1)S(1)}, u32[]{:S(2)}, u32[]{:S(2)}) %collective-permute-start.3) | collective-permute-done | bytes 36896 | tf_op jit(solution)/shard_map/ppermute | solution.py:218
  17.9 3.3 %collective-permute-start.7 = (bf16[4,144,128]{2,1,0:T(8,128)(2,1)S(1)}, bf16[4,144,128]{2,1,0:T(8,128)(2,1)S(1)}, u32[]{:S(2)}, u32[]{:S(2)}) collective-permute-start(bf16[4,144,128]{2,1,0:T(8,128)(2,1)S(1)} %get-tuple-element.39.own_ref), channel_id=1, source_target_pairs={{0,2},{2,0},{1,3},{3,1},{4,6},{6,4},{5,7},{7,5},{8,10},{10,8},{9,1... | collective-permute-start | bytes 442376 | tf_op jit(solution)/shard_map/ppermute | solution.py:476
  21.2 3.0 %collective-permute-start.4 = (bf16[384,128]{1,0:T(8,128)(2,1)S(1)}, bf16[384,128]{1,0:T(8,128)(2,1)S(1)}, u32[]{:S(2)}, u32[]{:S(2)}) collective-permute-start(bf16[384,128]{1,0:T(8,128)(2,1)S(1)} %get-tuple-element.38.upper_ref), channel_id=1, source_target_pairs={{0,8},{8,16},{16,24},{24,0},{1,9},{9,17},{17,25},{25,1},{2,10},{10... | collective-permute-start | bytes 294920 | tf_op jit(solution)/shard_map/ppermute | solution.py:475
  24.1 2.1 %collective-permute-start.5 = (bf16[384,128]{1,0:T(8,128)(2,1)S(1)}, bf16[384,128]{1,0:T(8,128)(2,1)S(1)}, u32[]{:S(2)}, u32[]{:S(2)}) collective-permute-start(bf16[384,128]{1,0:T(8,128)(2,1)S(1)} %get-tuple-element.38.upper_ref), channel_id=1, source_target_pairs={{0,24},{8,0},{16,8},{24,16},{1,25},{9,1},{17,9},{25,17},{2,26},{10... | collective-permute-start | bytes 294920 | tf_op jit(solution)/shard_map/ppermute | solution.py:475
  26.3 4.5 %collective-permute-start.6 = (bf16[384,128]{1,0:T(8,128)(2,1)S(1)}, bf16[384,128]{1,0:T(8,128)(2,1)S(1)}, u32[]{:S(2)}, u32[]{:S(2)}) collective-permute-start(bf16[384,128]{1,0:T(8,128)(2,1)S(1)} %get-tuple-element.38.upper_ref), channel_id=1, source_target_pairs={{0,16},{8,24},{16,0},{24,8},{1,17},{9,25},{17,1},{25,9},{2,18},{10... | collective-permute-start | bytes 294920 | tf_op jit(solution)/shard_map/ppermute | solution.py:475
  30.7 0.0 collective-permute-done.4.lower_ref
  30.8 1.3 %collective-permute-start.8 = (bf16[768,128]{1,0:T(8,128)(2,1)S(1)}, bf16[768,128]{1,0:T(8,128)(2,1)S(1)}, u32[]{:S(2)}, u32[]{:S(2)}) collective-permute-start(bf16[768,128]{1,0:T(8,128)(2,1)S(1)} %shard_map.80.refs_0_.refs_2_), channel_id=1, source_target_pairs={{0,32},{32,64},{64,96},{96,0},{1,33},{33,65},{65,97},{97,1},{2,34}... | collective-permute-start | bytes 589832 | tf_op jit(solution)/shard_map/ppermute | solution.py:478
  32.1 1.5 %collective-permute-start.12 = (bf16[768,128]{1,0:T(8,128)(2,1)S(1)}, bf16[768,128]{1,0:T(8,128)(2,1)S(1)}, u32[]{:S(2)}, u32[]{:S(2)}) collective-permute-start(bf16[768,128]{1,0:T(8,128)(2,1)S(1)} %shard_map.80.refs_0_.refs_2_), channel_id=1, source_target_pairs={{0,96},{32,0},{64,32},{96,64},{1,97},{33,1},{65,33},{97,65},{2,98}... | collective-permute-start | bytes 589832 | tf_op jit(solution)/shard_map/ppermute | solution.py:479
  33.5 0.0 collective-permute-done.7.other_ref
  33.5 1.0 shard_map.81
  34.5 0.0 collective-permute-done.5.upper_ref
  34.6 0.0 collective-permute-done.6.lower_ref
  34.6 2.2 %collective-permute-start.10 = (bf16[768,128]{1,0:T(8,128)(2,1)S(1)}, bf16[768,128]{1,0:T(8,128)(2,1)S(1)}, u32[]{:S(2)}, u32[]{:S(2)}) collective-permute-start(bf16[768,128]{1,0:T(8,128)(2,1)S(1)} %shard_map.82.refs_1_.refs_3_), channel_id=1, source_target_pairs={{0,96},{32,0},{64,32},{96,64},{1,97},{33,1},{65,33},{97,65},{2,98}... | collective-permute-start | bytes 589832 | tf_op jit(solution)/shard_map/ppermute | solution.py:492
  36.8 0.0 collective-permute-start.13
  36.8 4.1 %shard_map.83.refs_6_ = f32[6,48,768]{2,1,0:T(8,128)S(1)} custom-call(bf16[768,128]{1,0:T(8,128)(2,1)S(1)} %shard_map.80.refs_0_.refs_2_, bf16[768,128]{1,0:T(8,128)(2,1)S(1)} %shard_map.82.refs_1_.refs_3_, bf16[192,192]{1,0:T(8,128)(2,1)S(1)} %get-tuple-element.43.refs_2_.refs_4_.refs_8_, bf16[6,208,768]{2,1,0:T(8,128)(2,1)S(1)} %get-tuple-element.44.refs_3_.refs_5_.refs_9_), custom_call_target="tpu_custom_call" | custom-call | flops 3623878656 | bytes 1048576 | tf_op jit(solution)/shard_map/pallas_call | solution.py:65
  40.9 0.0 collective-permute-done.8.refs_0_.refs_4_
  40.9 0.2 collective-permute-start.9
  41.1 0.0 collective-permute-done.10.refs_3_.refs_7_
  41.1 2.6 %collective-permute-start.11 = (bf16[768,128]{1,0:T(8,128)(2,1)S(1)}, bf16[768,128]{1,0:T(8,128)(2,1)S(1)}, u32[]{:S(2)}, u32[]{:S(2)}) collective-permute-start(bf16[768,128]{1,0:T(8,128)(2,1)S(1)} %collective-permute-done.10.refs_3_.refs_7_), channel_id=1, source_target_pairs={{0,96},{32,0},{64,32},{96,64},{1,97},{33,1},{65,33},{97,65},{2,98}... | collective-permute-start | bytes 589832 | tf_op jit(solution)/shard_map/ppermute | solution.py:497
  43.7 0.0 collective-permute-done.12.refs_1_.refs_5_
  43.7 8.0 %shard_map.84.refs_10_ = f32[6,48,768]{2,1,0:T(8,128)S(1)} custom-call(bf16[768,128]{1,0:T(8,128)(2,1)S(1)} %collective-permute-done.8.refs_0_.refs_4_, bf16[768,128]{1,0:T(8,128)(2,1)S(1)} %collective-permute-done.12.refs_1_.refs_5_, bf16[768,128]{1,0:T(8,128)(2,1)S(1)} %collective-permute-done.13.refs_2_.refs_6_, ...), custom_call_target="tpu_custom_call" | custom-call | flops 7247757312 | bytes 1048576 | tf_op jit(solution)/shard_map/pallas_call | solution.py:65
  51.7 0.0 copy-start.3
  51.7 0.0 copy-start.2
  51.7 0.0 collective-permute-done.11.refs_1_
  51.8 36.6 %shard_map.85 = (f32[6,40,384]{2,1,0:T(8,128)S(1)}, f32[6,40,384]{2,1,0:T(8,128)S(1)}) custom-call(bf16[768,128]{1,0:T(8,128)(2,1)S(1)} %collective-permute-done.9.refs_0_, bf16[768,128]{1,0:T(8,128)(2,1)S(1)} %collective-permute-done.11.refs_1_, bf16[768,128]{1,0:T(8,128)(2,1)S(1)} %shard_map.80.refs_0_.refs_2_, ...), custom_call_target="tpu_custom_call" | custom-call | flops 3623878656 | bytes 1048576 | tf_op jit(solution)/shard_map/pallas_call | solution.py:65
  88.3 5.8 %collective-permute-start.14 = (f32[6,40,384]{2,1,0:T(8,128)S(1)}, f32[6,40,384]{2,1,0:T(8,128)S(1)}, u32[]{:S(2)}, u32[]{:S(2)}) collective-permute-start(f32[6,40,384]{2,1,0:T(8,128)S(1)} %get-tuple-element.50), channel_id=1, source_target_pairs={{0,2},{2,0},{1,3},{3,1},{4,6},{6,4},{5,7},{7,5},{8,10},{10,8},{9,1... | collective-permute-start | bytes 1105928 | tf_op jit(solution)/shard_map/ppermute | solution.py:502
  94.2 1.3 %collective-permute-done.14.came_ref = f32[6,40,384]{2,1,0:T(8,128)S(1)} collective-permute-done((f32[6,40,384]{2,1,0:T(8,128)S(1)}, f32[6,40,384]{2,1,0:T(8,128)S(1)}, u32[]{:S(2)}, u32[]{:S(2)}) %collective-permute-start.14) | collective-permute-done | bytes 368672 | tf_op jit(solution)/shard_map/ppermute | solution.py:502
  95.5 0.2 shard_map.86
  95.7 2.1 %collective-permute-start.15 = (bf16[144,128]{1,0:T(8,128)(2,1)S(1)}, bf16[144,128]{1,0:T(8,128)(2,1)S(1)}, u32[]{:S(2)}, u32[]{:S(2)}) collective-permute-start(bf16[144,128]{1,0:T(8,128)(2,1)S(1)} %get-tuple-element.52), channel_id=1, source_target_pairs={{0,4},{4,0},{128,132},{132,128},{1,5},{5,1},{129,133},{133,129},{2... | collective-permute-start | bytes 110600 | tf_op jit(solution)/shard_map/ppermute | solution.py:218
  97.8 0.2 collective-permute-start.16
  98.0 1.1 %collective-permute-start.17 = (bf16[144,128]{1,0:T(8,128)(2,1)S(1)}, bf16[144,128]{1,0:T(8,128)(2,1)S(1)}, u32[]{:S(2)}, u32[]{:S(2)}) collective-permute-start(bf16[144,128]{1,0:T(8,128)(2,1)S(1)} %get-tuple-element.54), channel_id=1, source_target_pairs={{0,132},{4,128},{128,4},{132,0},{1,133},{5,129},{129,5},{133,1},{2... | collective-permute-start | bytes 110600 | tf_op jit(solution)/shard_map/ppermute | solution.py:218
  99.1 0.2 copy.8.refs_7_
  99.3 0.0 collective-permute-done.15.refs_1_
  99.3 1.3 %collective-permute-done.16.refs_2_ = bf16[144,128]{1,0:T(8,128)(2,1)S(1)} collective-permute-done((bf16[144,128]{1,0:T(8,128)(2,1)S(1)}, bf16[144,128]{1,0:T(8,128)(2,1)S(1)}, u32[]{:S(2)}, u32[]{:S(2)}) %collective-permute-start.16) | collective-permute-done | bytes 36896 | tf_op jit(solution)/shard_map/ppermute | solution.py:218
  100.6 1.1 %collective-permute-done.17.refs_3_ = bf16[144,128]{1,0:T(8,128)(2,1)S(1)} collective-permute-done((bf16[144,128]{1,0:T(8,128)(2,1)S(1)}, bf16[144,128]{1,0:T(8,128)(2,1)S(1)}, u32[]{:S(2)}, u32[]{:S(2)}) %collective-permute-start.17) | collective-permute-done | bytes 36896 | tf_op jit(solution)/shard_map/ppermute | solution.py:218
  101.7 1.7 %shard_map.87 = (bf16[64,768]{1,0:T(8,128)(2,1)}, bf16[32,768]{1,0:T(8,128)(2,1)}) custom-call(bf16[144,128]{1,0:T(8,128)(2,1)S(1)} %get-tuple-element.51.refs_0_, bf16[144,128]{1,0:T(8,128)(2,1)S(1)} %collective-permute-done.15.refs_1_, bf16[144,128]{1,0:T(8,128)(2,1)S(1)} %collective-permute-done.16.refs_2_, ...), custom_call_target="tpu_custom_call" | custom-call | flops 1000000000 | bytes 1048576 | tf_op jit(solution)/shard_map/pallas_call | solution.py:65
  (10 shorter events, 0.1 us)
Async XLA Ops:
  1.6 6.5 %collective-permute-start = (bf16[96,768]{1,0:T(8,128)(2,1)S(1)}, bf16[96,768]{1,0:T(8,128)(2,1)S(1)}, u32[]{:S(2)}, u32[]{:S(2)}) collective-permute-start(bf16[96,768]{1,0:T(8,128)(2,1)S(1)} %pad_maximum_fusion.joined_ref), channel_id=1, source_target_pairs={{0,1},{1,0},{2,3},{3,2},{4,5},{5,4},{6,7},{7,6},{8,9},{9,8},{10,11... | collective-permute-start | bytes 442376 | tf_op jit(solution)/shard_map/ppermute | solution.py:443
  5.4 1.0 copy-start.1
  8.1 25.4 %copy-start = (bf16[4,192,192]{2,1,0:T(8,128)(2,1)S(1)}, bf16[4,192,192]{2,1,0:T(8,128)(2,1)}, u32[]{:S(2)}) copy-start(bf16[4,192,192]{2,1,0:T(8,128)(2,1)} %weights_ref.5) | copy-start | bytes 884740
  10.4 3.7 %collective-permute-start.1 = (bf16[144,128]{1,0:T(8,128)(2,1)S(1)}, bf16[144,128]{1,0:T(8,128)(2,1)S(1)}, u32[]{:S(2)}, u32[]{:S(2)}) collective-permute-start(bf16[144,128]{1,0:T(8,128)(2,1)S(1)} %get-tuple-element.35), channel_id=1, source_target_pairs={{0,4},{4,0},{128,132},{132,128},{1,5},{5,1},{129,133},{133,129},{2... | collective-permute-start | bytes 110600 | tf_op jit(solution)/shard_map/ppermute | solution.py:218
  12.8 2.8 %collective-permute-start.2 = (bf16[144,128]{1,0:T(8,128)(2,1)S(1)}, bf16[144,128]{1,0:T(8,128)(2,1)S(1)}, u32[]{:S(2)}, u32[]{:S(2)}) collective-permute-start(bf16[144,128]{1,0:T(8,128)(2,1)S(1)} %get-tuple-element.36), channel_id=1, source_target_pairs={{0,128},{4,132},{128,0},{132,4},{1,129},{5,133},{129,1},{133,5},{2... | collective-permute-start | bytes 110600 | tf_op jit(solution)/shard_map/ppermute | solution.py:218
  14.1 3.7 %collective-permute-start.3 = (bf16[144,128]{1,0:T(8,128)(2,1)S(1)}, bf16[144,128]{1,0:T(8,128)(2,1)S(1)}, u32[]{:S(2)}, u32[]{:S(2)}) collective-permute-start(bf16[144,128]{1,0:T(8,128)(2,1)S(1)} %get-tuple-element.37), channel_id=1, source_target_pairs={{0,132},{4,128},{128,4},{132,0},{1,133},{5,129},{129,5},{133,1},{2... | collective-permute-start | bytes 110600 | tf_op jit(solution)/shard_map/ppermute | solution.py:218
  17.9 15.7 %collective-permute-start.7 = (bf16[4,144,128]{2,1,0:T(8,128)(2,1)S(1)}, bf16[4,144,128]{2,1,0:T(8,128)(2,1)S(1)}, u32[]{:S(2)}, u32[]{:S(2)}) collective-permute-start(bf16[4,144,128]{2,1,0:T(8,128)(2,1)S(1)} %get-tuple-element.39.own_ref), channel_id=1, source_target_pairs={{0,2},{2,0},{1,3},{3,1},{4,6},{6,4},{5,7},{7,5},{8,10},{10,8},{9,1... | collective-permute-start | bytes 442376 | tf_op jit(solution)/shard_map/ppermute | solution.py:476
  21.2 9.6 %collective-permute-start.4 = (bf16[384,128]{1,0:T(8,128)(2,1)S(1)}, bf16[384,128]{1,0:T(8,128)(2,1)S(1)}, u32[]{:S(2)}, u32[]{:S(2)}) collective-permute-start(bf16[384,128]{1,0:T(8,128)(2,1)S(1)} %get-tuple-element.38.upper_ref), channel_id=1, source_target_pairs={{0,8},{8,16},{16,24},{24,0},{1,9},{9,17},{17,25},{25,1},{2,10},{10... | collective-permute-start | bytes 294920 | tf_op jit(solution)/shard_map/ppermute | solution.py:475
  24.1 10.4 %collective-permute-start.5 = (bf16[384,128]{1,0:T(8,128)(2,1)S(1)}, bf16[384,128]{1,0:T(8,128)(2,1)S(1)}, u32[]{:S(2)}, u32[]{:S(2)}) collective-permute-start(bf16[384,128]{1,0:T(8,128)(2,1)S(1)} %get-tuple-element.38.upper_ref), channel_id=1, source_target_pairs={{0,24},{8,0},{16,8},{24,16},{1,25},{9,1},{17,9},{25,17},{2,26},{10... | collective-permute-start | bytes 294920 | tf_op jit(solution)/shard_map/ppermute | solution.py:475
  26.3 8.3 %collective-permute-start.6 = (bf16[384,128]{1,0:T(8,128)(2,1)S(1)}, bf16[384,128]{1,0:T(8,128)(2,1)S(1)}, u32[]{:S(2)}, u32[]{:S(2)}) collective-permute-start(bf16[384,128]{1,0:T(8,128)(2,1)S(1)} %get-tuple-element.38.upper_ref), channel_id=1, source_target_pairs={{0,16},{8,24},{16,0},{24,8},{1,17},{9,25},{17,1},{25,9},{2,18},{10... | collective-permute-start | bytes 294920 | tf_op jit(solution)/shard_map/ppermute | solution.py:475
  30.8 10.1 %collective-permute-start.8 = (bf16[768,128]{1,0:T(8,128)(2,1)S(1)}, bf16[768,128]{1,0:T(8,128)(2,1)S(1)}, u32[]{:S(2)}, u32[]{:S(2)}) collective-permute-start(bf16[768,128]{1,0:T(8,128)(2,1)S(1)} %shard_map.80.refs_0_.refs_2_), channel_id=1, source_target_pairs={{0,32},{32,64},{64,96},{96,0},{1,33},{33,65},{65,97},{97,1},{2,34}... | collective-permute-start | bytes 589832 | tf_op jit(solution)/shard_map/ppermute | solution.py:478
  32.1 11.7 %collective-permute-start.12 = (bf16[768,128]{1,0:T(8,128)(2,1)S(1)}, bf16[768,128]{1,0:T(8,128)(2,1)S(1)}, u32[]{:S(2)}, u32[]{:S(2)}) collective-permute-start(bf16[768,128]{1,0:T(8,128)(2,1)S(1)} %shard_map.80.refs_0_.refs_2_), channel_id=1, source_target_pairs={{0,96},{32,0},{64,32},{96,64},{1,97},{33,1},{65,33},{97,65},{2,98}... | collective-permute-start | bytes 589832 | tf_op jit(solution)/shard_map/ppermute | solution.py:479
  34.6 6.5 %collective-permute-start.10 = (bf16[768,128]{1,0:T(8,128)(2,1)S(1)}, bf16[768,128]{1,0:T(8,128)(2,1)S(1)}, u32[]{:S(2)}, u32[]{:S(2)}) collective-permute-start(bf16[768,128]{1,0:T(8,128)(2,1)S(1)} %shard_map.82.refs_1_.refs_3_), channel_id=1, source_target_pairs={{0,96},{32,0},{64,32},{96,64},{1,97},{33,1},{65,33},{97,65},{2,98}... | collective-permute-start | bytes 589832 | tf_op jit(solution)/shard_map/ppermute | solution.py:492
  36.8 7.0 %collective-permute-start.13 = (bf16[768,128]{1,0:T(8,128)(2,1)S(1)}, bf16[768,128]{1,0:T(8,128)(2,1)S(1)}, u32[]{:S(2)}, u32[]{:S(2)}) collective-permute-start(bf16[768,128]{1,0:T(8,128)(2,1)S(1)} %shard_map.82.refs_1_.refs_3_), channel_id=1, source_target_pairs={{0,32},{32,64},{64,96},{96,0},{1,33},{33,65},{65,97},{97,1},{2,34}... | collective-permute-start | bytes 589832 | tf_op jit(solution)/shard_map/ppermute | solution.py:491
  40.9 10.9 %collective-permute-start.9 = (bf16[768,128]{1,0:T(8,128)(2,1)S(1)}, bf16[768,128]{1,0:T(8,128)(2,1)S(1)}, u32[]{:S(2)}, u32[]{:S(2)}) collective-permute-start(bf16[768,128]{1,0:T(8,128)(2,1)S(1)} %collective-permute-done.8.refs_0_.refs_4_), channel_id=1, source_target_pairs={{0,32},{32,64},{64,96},{96,0},{1,33},{33,65},{65,97},{97,1},{2,34}... | collective-permute-start | bytes 589832 | tf_op jit(solution)/shard_map/ppermute | solution.py:496
  41.1 10.6 %collective-permute-start.11 = (bf16[768,128]{1,0:T(8,128)(2,1)S(1)}, bf16[768,128]{1,0:T(8,128)(2,1)S(1)}, u32[]{:S(2)}, u32[]{:S(2)}) collective-permute-start(bf16[768,128]{1,0:T(8,128)(2,1)S(1)} %collective-permute-done.10.refs_3_.refs_7_), channel_id=1, source_target_pairs={{0,96},{32,0},{64,32},{96,64},{1,97},{33,1},{65,33},{97,65},{2,98}... | collective-permute-start | bytes 589832 | tf_op jit(solution)/shard_map/ppermute | solution.py:497
  51.7 47.4 %copy-start.3 = (bf16[768,192]{0,1:T(8,128)(2,1)S(1)}, bf16[768,192]{0,1:T(8,128)(2,1)}, u32[]{:S(2)}) copy-start(bf16[768,192]{0,1:T(8,128)(2,1)} %param.11) | copy-start | bytes 884740
  51.7 50.0 %copy-start.2 = (bf16[192,768]{1,0:T(8,128)(2,1)S(1)}, bf16[192,768]{1,0:T(8,128)(2,1)}, u32[]{:S(2)}) copy-start(bf16[192,768]{1,0:T(8,128)(2,1)} %refs_6_.1) | copy-start | bytes 884740
  88.3 7.2 %collective-permute-start.14 = (f32[6,40,384]{2,1,0:T(8,128)S(1)}, f32[6,40,384]{2,1,0:T(8,128)S(1)}, u32[]{:S(2)}, u32[]{:S(2)}) collective-permute-start(f32[6,40,384]{2,1,0:T(8,128)S(1)} %get-tuple-element.50), channel_id=1, source_target_pairs={{0,2},{2,0},{1,3},{3,1},{4,6},{6,4},{5,7},{7,5},{8,10},{10,8},{9,1... | collective-permute-start | bytes 1105928 | tf_op jit(solution)/shard_map/ppermute | solution.py:502
  95.7 3.6 %collective-permute-start.15 = (bf16[144,128]{1,0:T(8,128)(2,1)S(1)}, bf16[144,128]{1,0:T(8,128)(2,1)S(1)}, u32[]{:S(2)}, u32[]{:S(2)}) collective-permute-start(bf16[144,128]{1,0:T(8,128)(2,1)S(1)} %get-tuple-element.52), channel_id=1, source_target_pairs={{0,4},{4,0},{128,132},{132,128},{1,5},{5,1},{129,133},{133,129},{2... | collective-permute-start | bytes 110600 | tf_op jit(solution)/shard_map/ppermute | solution.py:218
  97.8 2.8 %collective-permute-start.16 = (bf16[144,128]{1,0:T(8,128)(2,1)S(1)}, bf16[144,128]{1,0:T(8,128)(2,1)S(1)}, u32[]{:S(2)}, u32[]{:S(2)}) collective-permute-start(bf16[144,128]{1,0:T(8,128)(2,1)S(1)} %get-tuple-element.53), channel_id=1, source_target_pairs={{0,128},{4,132},{128,0},{132,4},{1,129},{5,133},{129,1},{133,5},{2... | collective-permute-start | bytes 110600 | tf_op jit(solution)/shard_map/ppermute | solution.py:218
  98.0 3.7 %collective-permute-start.17 = (bf16[144,128]{1,0:T(8,128)(2,1)S(1)}, bf16[144,128]{1,0:T(8,128)(2,1)S(1)}, u32[]{:S(2)}, u32[]{:S(2)}) collective-permute-start(bf16[144,128]{1,0:T(8,128)(2,1)S(1)} %get-tuple-element.54), channel_id=1, source_target_pairs={{0,132},{4,128},{128,4},{132,0},{1,133},{5,129},{129,5},{133,1},{2... | collective-permute-start | bytes 110600 | tf_op jit(solution)/shard_map/ppermute | solution.py:218

commit v5 on v4

--- a/solution.py
+++ b/solution.py
@@ -245,6 +245,16 @@
     both_ref[BLOCK // 4 :, :] = lower_ref[...]
 
 
+def choose_kernel(early_above, early_below, late_above, late_below, chosen_ref):
+    core = lax.axis_index("core")
+    for turn, parts in enumerate(((early_above, late_above), (early_below, late_below))):
+
+        @pl.when(core == turn)
+        def _():
+            chosen_ref[: BLOCK // 2, :] = parts[0][...]
+            chosen_ref[BLOCK // 2 :, :] = parts[1][...]
+
+
 def stack(upper, lower):
     return call(
         stack_kernel,
@@ -311,9 +321,10 @@
 
 
 def attend_last_kernel(*refs):
-    packed_refs = refs[: 2 * SIDE]
-    wv_ref, folded_ref, mix_ref, stay_ref, leave_ref = refs[2 * SIDE : 2 * SIDE + 5]
-    keys_ref, values_ref, total_ref, peak_ref, blocks_ref, scores_ref = refs[2 * SIDE + 5 :]
+    far_ref = refs[0]
+    packed_refs = (far_ref.at[: BLOCK // 2], far_ref.at[BLOCK // 2 :]) + refs[1 : 2 * SIDE - 1]
+    wv_ref, folded_ref, mix_ref, stay_ref, leave_ref = refs[2 * SIDE - 1 : 2 * SIDE + 4]
+    keys_ref, values_ref, total_ref, peak_ref, blocks_ref, scores_ref = refs[2 * SIDE + 4 :]
     over = [jnp.zeros((8, ALL_Q), f32)]
 
     def leave(head, total, peak):
@@ -486,18 +497,20 @@
         (received, received_other, row_weights),
         10**9,
     )
-    column, folded = lax.optimization_barrier((column[2:], folded))
-    late = stack(*column)
+    late = stack(*column[2:])
     late_above = lax.ppermute(late, "x", shift(4, 1))
     late_below = lax.ppermute(late, "x", shift(4, 3))
     mix = attend((early, late), (value_turned, folded))
-    mix, early_above = lax.optimization_barrier((mix, early_above))
-    mix, late_below = lax.optimization_barrier((mix, late_below))
-    far_early = lax.ppermute(early_above, "x", shift(4, 1))
-    far_late = lax.ppermute(late_below, "x", shift(4, 3))
     middle = (early_above, early_below, late_above, late_below)
+    mix, middle = lax.optimization_barrier((mix, middle))
+    chosen = call(
+        choose_kernel, [jax.ShapeDtypeStruct((BLOCK, LANES), bf16)], middle, 10**6, limit=4
+    )[0]
+    pairs = [(2 * one, (2 * one + 2) % 8) for one in range(4)]
+    pairs += [(2 * one + 1, (2 * one + 7) % 8) for one in range(4)]
+    far = lax.ppermute(chosen, ("x", "core"), pairs)
     mix = attend(middle, (value_turned, folded, mix))
-    packed = (far_early, far_late, early, late) + middle
+    packed = (far, early, late) + middle
     stay, leave = attend_last(packed + (value_turned, folded, mix))
     came = lax.ppermute(leave, "core", swap)
     mixed = call(merge_kernel, [piece_shape] * GROUPS, (stay, came), 10**7)

time: 104 us -> 106 us (1.019)
  waiting for transfers between devices: 7.51 us -> 13.6 us
  starting transfers between devices: 37.3 us -> 32.8 us
    ppermute x3, waiting for transfers between devices: 0.01 us -> 6.67 us  [layer(): column.append(lax.ppermute(keys, 'z_hi', shift(SIDE, by)))]
    ppermute x1, starting transfers between devices: 5.84 us -> 3.53 us  [layer(): came = lax.ppermute(leave, 'core', swap)]
    ppermute x1, starting transfers between devices: 0.01 us -> 1.22 us  [layer(): late_above = lax.ppermute(late, 'x', shift(4, 1))]
    ppermute x3, starting transfers between devices: 9.59 us -> 8.38 us  [layer(): column.append(lax.ppermute(keys, 'z_hi', shift(SIDE, by)))]
    ppermute x1, starting transfers between devices: 1.29 us -> 0.08 us  [layer(): early_above = lax.ppermute(early, 'x', shift(4, 1))]
    ppermute x1, starting transfers between devices: 1.47 us -> 2.66 us  [layer(): early_below = lax.ppermute(early, 'x', shift(4, 3))]
    ppermute x2 -> x1, starting transfers between devices: 2.85 us -> 1.9 us  [layer(): far = lax.ppermute(chosen, ('x', 'core'), pairs)]
    pallas_call x11 -> x12, Pallas kernels: 55.6 us -> 55.7 us  [call(): pl.pallas_call(kernel, out_shape=outs, in_specs=[in_vmem] * len(args), ou...]
  transfers between devices with their start and end apart: 18 -> 17, of which waited for: 5 -> 6; matrix products, arithmetic and copies ran while one was open for 0% -> 0% of each run, Pallas kernels for 14% -> 14%
where the time goes in v5:
time: 106 us; the launch traced here: 105 us
  Pallas kernels  55.7 us (53%)
  starting transfers between devices  32.8 us (31%)
  waiting for transfers between devices  13.6 us (13%)
  local copies, waits for them, and re-layouts  1.19 us (1%)
    pallas_call x12, Pallas kernels, call(): pl.pallas_call(kernel, out_shape=outs, in_specs=[in_vmem] * len(args), ou...  55.7 us
    ppermute x3, starting transfers between devices, layer(): column.append(lax.ppermute(keys, 'z_hi', shift(SIDE, by)))  8.38 us
    ppermute x3, waiting for transfers between devices, layer(): column.append(lax.ppermute(keys, 'z_hi', shift(SIDE, by)))  6.67 us
    ppermute x6, starting transfers between devices, exchange(): came.append(lax.ppermute(pieces[turn], classes, pairs))  6.39 us
    ppermute x6, waiting for transfers between devices, exchange(): came.append(lax.ppermute(pieces[turn], classes, pairs))  5.6 us
    ppermute x1, starting transfers between devices, layer(): other = lax.ppermute(joined, 'feat', swap)  3.82 us
    ppermute x1, starting transfers between devices, layer(): came = lax.ppermute(leave, 'core', swap)  3.53 us
    ppermute x1, starting transfers between devices, layer(): received_other = lax.ppermute(received, 'core', swap)  3.29 us
  transfers between devices with their start and end apart: 17, of which 6 were waited for; matrix products, arithmetic and copies ran while one was open for 0% of the time, Pallas kernels for 14%

profile of v5, /device:TPU:1, one launch (start us, length us, event | category | flops | bytes accessed | tf_op | source)
XLA Modules:
  0.0 105.0 jit_solution(6438822402708631288)
XLA Ops:
  0.6 0.9 pad_maximum_fusion.joined_ref
  1.6 3.8 %collective-permute-start = (bf16[96,768]{1,0:T(8,128)(2,1)S(1)}, bf16[96,768]{1,0:T(8,128)(2,1)S(1)}, u32[]{:S(2)}, u32[]{:S(2)}) collective-permute-start(bf16[96,768]{1,0:T(8,128)(2,1)S(1)} %pad_maximum_fusion.joined_ref), channel_id=1, source_target_pairs={{0,1},{1,0},{2,3},{3,2},{4,5},{5,4},{6,7},{7,6},{8,9},{9,8},{10,11... | collective-permute-start | bytes 442376 | tf_op jit(solution)/shard_map/ppermute | solution.py:454
  5.4 1.0 copy-done.1
  6.4 1.7 %shard_map.77 = (f32[4,96,192]{2,1,0:T(8,128)S(1)}, bf16[384,192]{1,0:T(8,128)(2,1)S(1)}, f32[4,96,128]{2,1,0:T(8,128)S(1)}, f32[4,96,128]{2,1,0:T(8,128)S(1)}, f32[4,96,192]{2,1,0:T(8,128)S(1)}) custom-call(bf16[96,768]{1,0:T(8,128)(2,1)S(1)} %pad_maximum_fusion.joined_ref, bf16[4,192,192]{2,1,0:T(8,128)(2,1)S(1)} %copy-done.1), custom_call_target="tpu_custom_call" | custom-call | flops 1000000000 | bytes 1048576 | tf_op jit(solution)/shard_map/pallas_call | solution.py:65
  8.1 0.0 collective-permute-done.other_ref
  8.1 0.0 copy-start
  8.1 2.3 %shard_map.78 = (f32[4,96,192]{2,1,0:T(8,128)S(1)}, bf16[144,128]{1,0:T(8,128)(2,1)S(1)}, bf16[144,128]{1,0:T(8,128)(2,1)S(1)}, bf16[144,128]{1,0:T(8,128)(2,1)S(1)}, bf16[144,128]{1,0:T(8,128)(2,1)S(1)}) custom-call(bf16[96,768]{1,0:T(8,128)(2,1)S(1)} %collective-permute-done.other_ref, bf16[4,192,192]{2,1,0:T(8,128)(2,1)S(1)} %copy-done.1, ...), custom_call_target="tpu_custom_call" | custom-call | flops 1000000000 | bytes 1048576 | tf_op jit(solution)/shard_map/pallas_call | solution.py:65
  10.4 2.3 %collective-permute-start.1 = (bf16[144,128]{1,0:T(8,128)(2,1)S(1)}, bf16[144,128]{1,0:T(8,128)(2,1)S(1)}, u32[]{:S(2)}, u32[]{:S(2)}) collective-permute-start(bf16[144,128]{1,0:T(8,128)(2,1)S(1)} %get-tuple-element.33), channel_id=1, source_target_pairs={{0,4},{4,0},{128,132},{132,128},{1,5},{5,1},{129,133},{133,129},{2... | collective-permute-start | bytes 110600 | tf_op jit(solution)/shard_map/ppermute | solution.py:218
  12.8 1.3 %collective-permute-start.2 = (bf16[144,128]{1,0:T(8,128)(2,1)S(1)}, bf16[144,128]{1,0:T(8,128)(2,1)S(1)}, u32[]{:S(2)}, u32[]{:S(2)}) collective-permute-start(bf16[144,128]{1,0:T(8,128)(2,1)S(1)} %get-tuple-element.34), channel_id=1, source_target_pairs={{0,128},{4,132},{128,0},{132,4},{1,129},{5,133},{129,1},{133,5},{2... | collective-permute-start | bytes 110600 | tf_op jit(solution)/shard_map/ppermute | solution.py:218
  14.1 0.0 collective-permute-start.3
  14.1 0.0 collective-permute-done.1.refs_1_
  14.1 1.5 %collective-permute-done.2.refs_2_ = bf16[144,128]{1,0:T(8,128)(2,1)S(1)} collective-permute-done((bf16[144,128]{1,0:T(8,128)(2,1)S(1)}, bf16[144,128]{1,0:T(8,128)(2,1)S(1)}, u32[]{:S(2)}, u32[]{:S(2)}) %collective-permute-start.2) | collective-permute-done | bytes 36896 | tf_op jit(solution)/shard_map/ppermute | solution.py:218
  15.6 2.2 %collective-permute-done.3.refs_3_ = bf16[144,128]{1,0:T(8,128)(2,1)S(1)} collective-permute-done((bf16[144,128]{1,0:T(8,128)(2,1)S(1)}, bf16[144,128]{1,0:T(8,128)(2,1)S(1)}, u32[]{:S(2)}, u32[]{:S(2)}) %collective-permute-start.3) | collective-permute-done | bytes 36896 | tf_op jit(solution)/shard_map/ppermute | solution.py:218
  17.9 3.3 %collective-permute-start.7 = (bf16[4,144,128]{2,1,0:T(8,128)(2,1)S(1)}, bf16[4,144,128]{2,1,0:T(8,128)(2,1)S(1)}, u32[]{:S(2)}, u32[]{:S(2)}) collective-permute-start(bf16[4,144,128]{2,1,0:T(8,128)(2,1)S(1)} %get-tuple-element.37.own_ref), channel_id=1, source_target_pairs={{0,2},{2,0},{1,3},{3,1},{4,6},{6,4},{5,7},{7,5},{8,10},{10,8},{9,1... | collective-permute-start | bytes 442376 | tf_op jit(solution)/shard_map/ppermute | solution.py:487
  21.2 5.1 %collective-permute-start.5 = (bf16[384,128]{1,0:T(8,128)(2,1)S(1)}, bf16[384,128]{1,0:T(8,128)(2,1)S(1)}, u32[]{:S(2)}, u32[]{:S(2)}) collective-permute-start(bf16[384,128]{1,0:T(8,128)(2,1)S(1)} %get-tuple-element.36.upper_ref), channel_id=1, source_target_pairs={{0,24},{8,0},{16,8},{24,16},{1,25},{9,1},{17,9},{25,17},{2,26},{10... | collective-permute-start | bytes 294920 | tf_op jit(solution)/shard_map/ppermute | solution.py:486
  26.3 1.2 %collective-permute-start.6 = (bf16[384,128]{1,0:T(8,128)(2,1)S(1)}, bf16[384,128]{1,0:T(8,128)(2,1)S(1)}, u32[]{:S(2)}, u32[]{:S(2)}) collective-permute-start(bf16[384,128]{1,0:T(8,128)(2,1)S(1)} %get-tuple-element.36.upper_ref), channel_id=1, source_target_pairs={{0,16},{8,24},{16,0},{24,8},{1,17},{9,25},{17,1},{25,9},{2,18},{10... | collective-permute-start | bytes 294920 | tf_op jit(solution)/shard_map/ppermute | solution.py:486
  27.4 2.1 %collective-permute-start.4 = (bf16[384,128]{1,0:T(8,128)(2,1)S(1)}, bf16[384,128]{1,0:T(8,128)(2,1)S(1)}, u32[]{:S(2)}, u32[]{:S(2)}) collective-permute-start(bf16[384,128]{1,0:T(8,128)(2,1)S(1)} %get-tuple-element.36.upper_ref), channel_id=1, source_target_pairs={{0,8},{8,16},{16,24},{24,0},{1,9},{9,17},{17,25},{25,1},{2,10},{10... | collective-permute-start | bytes 294920 | tf_op jit(solution)/shard_map/ppermute | solution.py:486
  29.5 0.0 collective-permute-done.5.upper_ref
  29.5 6.7 %collective-permute-done.6.lower_ref = bf16[384,128]{1,0:T(8,128)(2,1)S(1)} collective-permute-done((bf16[384,128]{1,0:T(8,128)(2,1)S(1)}, bf16[384,128]{1,0:T(8,128)(2,1)S(1)}, u32[]{:S(2)}, u32[]{:S(2)}) %collective-permute-start.6) | collective-permute-done | bytes 98336 | tf_op jit(solution)/shard_map/ppermute | solution.py:486
  36.2 1.2 %collective-permute-start.10 = (bf16[768,128]{1,0:T(8,128)(2,1)S(1)}, bf16[768,128]{1,0:T(8,128)(2,1)S(1)}, u32[]{:S(2)}, u32[]{:S(2)}) collective-permute-start(bf16[768,128]{1,0:T(8,128)(2,1)S(1)} %shard_map.81.refs_1_.refs_2_), channel_id=1, source_target_pairs={{0,32},{32,64},{64,96},{96,0},{1,33},{33,65},{65,97},{97,1},{2,34}... | collective-permute-start | bytes 589832 | tf_op jit(solution)/shard_map/ppermute | solution.py:501
  37.4 1.5 %collective-permute-start.11 = (bf16[768,128]{1,0:T(8,128)(2,1)S(1)}, bf16[768,128]{1,0:T(8,128)(2,1)S(1)}, u32[]{:S(2)}, u32[]{:S(2)}) collective-permute-start(bf16[768,128]{1,0:T(8,128)(2,1)S(1)} %shard_map.81.refs_1_.refs_2_), channel_id=1, source_target_pairs={{0,96},{32,0},{64,32},{96,64},{1,97},{33,1},{65,33},{97,65},{2,98}... | collective-permute-start | bytes 589832 | tf_op jit(solution)/shard_map/ppermute | solution.py:502
  39.0 0.0 collective-permute-done.4.lower_ref
  39.0 0.1 collective-permute-start.8
  39.1 2.7 %collective-permute-start.9 = (bf16[768,128]{1,0:T(8,128)(2,1)S(1)}, bf16[768,128]{1,0:T(8,128)(2,1)S(1)}, u32[]{:S(2)}, u32[]{:S(2)}) collective-permute-start(bf16[768,128]{1,0:T(8,128)(2,1)S(1)} %shard_map.80.refs_0_.refs_1_), channel_id=1, source_target_pairs={{0,96},{32,0},{64,32},{96,64},{1,97},{33,1},{65,33},{97,65},{2,98}... | collective-permute-start | bytes 589832 | tf_op jit(solution)/shard_map/ppermute | solution.py:490
  41.7 0.0 collective-permute-done.7.other_ref
  41.8 1.0 shard_map.82
  42.8 4.1 %shard_map.83.refs_6_ = f32[6,48,768]{2,1,0:T(8,128)S(1)} custom-call(bf16[768,128]{1,0:T(8,128)(2,1)S(1)} %shard_map.80.refs_0_.refs_1_, bf16[768,128]{1,0:T(8,128)(2,1)S(1)} %shard_map.81.refs_1_.refs_2_, bf16[192,192]{1,0:T(8,128)(2,1)S(1)} %get-tuple-element.38.refs_2_.refs_4_.refs_7_, bf16[6,208,768]{2,1,0:T(8,128)(2,1)S(1)} %get-tuple-element.39.refs_3_.refs_5_.refs_8_), custom_call_target="tpu_custom_call" | custom-call | flops 3623878656 | bytes 1048576 | tf_op jit(solution)/shard_map/pallas_call | solution.py:65
  46.9 0.0 collective-permute-done.10.late_above.refs_2_.refs_5_
  46.9 0.0 collective-permute-done.11.late_below.refs_3_.refs_6_
  46.9 0.0 collective-permute-done.8.early_above.refs_0_.refs_3_
  46.9 0.0 collective-permute-done.9.early_below.refs_1_.refs_4_
  47.0 1.9 %collective-permute-start.12 = (bf16[1536,128]{1,0:T(8,128)(2,1)S(1)}, bf16[1536,128]{1,0:T(8,128)(2,1)S(1)}, u32[]{:S(2)}, u32[]{:S(2)}) collective-permute-start(bf16[1536,128]{1,0:T(8,128)(2,1)S(1)} %shard_map.84), channel_id=1, source_target_pairs={{0,32},{32,64},{64,96},{96,0},{2,98},{34,2},{66,34},{98,66},{1,33}... | collective-permute-start | bytes 1179656 | tf_op jit(solution)/shard_map/ppermute | solution.py:511
  48.9 8.0 %shard_map.85.refs_9_ = f32[6,48,768]{2,1,0:T(8,128)S(1)} custom-call(bf16[768,128]{1,0:T(8,128)(2,1)S(1)} %collective-permute-done.8.early_above.refs_0_.refs_3_, bf16[768,128]{1,0:T(8,128)(2,1)S(1)} %collective-permute-done.9.early_below.refs_1_.refs_4_, bf16[768,128]{1,0:T(8,128)(2,1)S(1)} %collective-permute-done.10.late_above.refs_2_.refs_5_, ...), custom_call_target="tpu_custom_call" | custom-call | flops 7247757312 | bytes 1048576 | tf_op jit(solution)/shard_map/pallas_call | solution.py:65
  56.8 0.0 copy-start.3
  56.8 0.0 copy-start.2
  56.9 0.0 collective-permute-done.12.refs_0_
  56.9 36.6 %shard_map.86 = (f32[6,40,384]{2,1,0:T(8,128)S(1)}, f32[6,40,384]{2,1,0:T(8,128)S(1)}) custom-call(bf16[1536,128]{1,0:T(8,128)(2,1)S(1)} %collective-permute-done.12.refs_0_, bf16[768,128]{1,0:T(8,128)(2,1)S(1)} %shard_map.80.refs_0_.refs_1_, bf16[768,128]{1,0:T(8,128)(2,1)S(1)} %shard_map.81.refs_1_.refs_2_, ...), custom_call_target="tpu_custom_call" | custom-call | flops 3623878656 | bytes 1048576 | tf_op jit(solution)/shard_map/pallas_call | solution.py:65
  93.4 3.5 %collective-permute-start.13 = (f32[6,40,384]{2,1,0:T(8,128)S(1)}, f32[6,40,384]{2,1,0:T(8,128)S(1)}, u32[]{:S(2)}, u32[]{:S(2)}) collective-permute-start(f32[6,40,384]{2,1,0:T(8,128)S(1)} %get-tuple-element.46), channel_id=1, source_target_pairs={{0,2},{2,0},{1,3},{3,1},{4,6},{6,4},{5,7},{7,5},{8,10},{10,8},{9,1... | collective-permute-start | bytes 1105928 | tf_op jit(solution)/shard_map/ppermute | solution.py:515
  97.0 1.3 %collective-permute-done.13.came_ref = f32[6,40,384]{2,1,0:T(8,128)S(1)} collective-permute-done((f32[6,40,384]{2,1,0:T(8,128)S(1)}, f32[6,40,384]{2,1,0:T(8,128)S(1)}, u32[]{:S(2)}, u32[]{:S(2)}) %collective-permute-start.13) | collective-permute-done | bytes 368672 | tf_op jit(solution)/shard_map/ppermute | solution.py:515
  98.3 0.2 shard_map.87
  98.5 0.9 collective-permute-start.14
  99.4 0.2 collective-permute-start.15
  99.5 1.7 %collective-permute-start.16 = (bf16[144,128]{1,0:T(8,128)(2,1)S(1)}, bf16[144,128]{1,0:T(8,128)(2,1)S(1)}, u32[]{:S(2)}, u32[]{:S(2)}) collective-permute-start(bf16[144,128]{1,0:T(8,128)(2,1)S(1)} %get-tuple-element.50), channel_id=1, source_target_pairs={{0,132},{4,128},{128,4},{132,0},{1,133},{5,129},{129,5},{133,1},{2... | collective-permute-start | bytes 110600 | tf_op jit(solution)/shard_map/ppermute | solution.py:218
  101.2 0.2 copy.8.refs_7_
  101.4 0.0 collective-permute-done.14.refs_1_
  101.4 1.1 %collective-permute-done.15.refs_2_ = bf16[144,128]{1,0:T(8,128)(2,1)S(1)} collective-permute-done((bf16[144,128]{1,0:T(8,128)(2,1)S(1)}, bf16[144,128]{1,0:T(8,128)(2,1)S(1)}, u32[]{:S(2)}, u32[]{:S(2)}) %collective-permute-start.15) | collective-permute-done | bytes 36896 | tf_op jit(solution)/shard_map/ppermute | solution.py:218
  102.5 0.8 collective-permute-done.16.refs_3_
  103.3 1.7 %shard_map.88 = (bf16[64,768]{1,0:T(8,128)(2,1)}, bf16[32,768]{1,0:T(8,128)(2,1)}) custom-call(bf16[144,128]{1,0:T(8,128)(2,1)S(1)} %get-tuple-element.47.refs_0_, bf16[144,128]{1,0:T(8,128)(2,1)S(1)} %collective-permute-done.14.refs_1_, bf16[144,128]{1,0:T(8,128)(2,1)S(1)} %collective-permute-done.15.refs_2_, ...), custom_call_target="tpu_custom_call" | custom-call | flops 1000000000 | bytes 1048576 | tf_op jit(solution)/shard_map/pallas_call | solution.py:65
  (9 shorter events, 0.1 us)
Async XLA Ops:
  1.6 6.5 %collective-permute-start = (bf16[96,768]{1,0:T(8,128)(2,1)S(1)}, bf16[96,768]{1,0:T(8,128)(2,1)S(1)}, u32[]{:S(2)}, u32[]{:S(2)}) collective-permute-start(bf16[96,768]{1,0:T(8,128)(2,1)S(1)} %pad_maximum_fusion.joined_ref), channel_id=1, source_target_pairs={{0,1},{1,0},{2,3},{3,2},{4,5},{5,4},{6,7},{7,6},{8,9},{9,8},{10,11... | collective-permute-start | bytes 442376 | tf_op jit(solution)/shard_map/ppermute | solution.py:454
  5.4 1.0 copy-start.1
  8.1 33.7 %copy-start = (bf16[4,192,192]{2,1,0:T(8,128)(2,1)S(1)}, bf16[4,192,192]{2,1,0:T(8,128)(2,1)}, u32[]{:S(2)}) copy-start(bf16[4,192,192]{2,1,0:T(8,128)(2,1)} %weights_ref.5) | copy-start | bytes 884740
  10.4 3.7 %collective-permute-start.1 = (bf16[144,128]{1,0:T(8,128)(2,1)S(1)}, bf16[144,128]{1,0:T(8,128)(2,1)S(1)}, u32[]{:S(2)}, u32[]{:S(2)}) collective-permute-start(bf16[144,128]{1,0:T(8,128)(2,1)S(1)} %get-tuple-element.33), channel_id=1, source_target_pairs={{0,4},{4,0},{128,132},{132,128},{1,5},{5,1},{129,133},{133,129},{2... | collective-permute-start | bytes 110600 | tf_op jit(solution)/shard_map/ppermute | solution.py:218
  12.8 2.8 %collective-permute-start.2 = (bf16[144,128]{1,0:T(8,128)(2,1)S(1)}, bf16[144,128]{1,0:T(8,128)(2,1)S(1)}, u32[]{:S(2)}, u32[]{:S(2)}) collective-permute-start(bf16[144,128]{1,0:T(8,128)(2,1)S(1)} %get-tuple-element.34), channel_id=1, source_target_pairs={{0,128},{4,132},{128,0},{132,4},{1,129},{5,133},{129,1},{133,5},{2... | collective-permute-start | bytes 110600 | tf_op jit(solution)/shard_map/ppermute | solution.py:218
  14.1 3.7 %collective-permute-start.3 = (bf16[144,128]{1,0:T(8,128)(2,1)S(1)}, bf16[144,128]{1,0:T(8,128)(2,1)S(1)}, u32[]{:S(2)}, u32[]{:S(2)}) collective-permute-start(bf16[144,128]{1,0:T(8,128)(2,1)S(1)} %get-tuple-element.35), channel_id=1, source_target_pairs={{0,132},{4,128},{128,4},{132,0},{1,133},{5,129},{129,5},{133,1},{2... | collective-permute-start | bytes 110600 | tf_op jit(solution)/shard_map/ppermute | solution.py:218
  17.9 23.9 %collective-permute-start.7 = (bf16[4,144,128]{2,1,0:T(8,128)(2,1)S(1)}, bf16[4,144,128]{2,1,0:T(8,128)(2,1)S(1)}, u32[]{:S(2)}, u32[]{:S(2)}) collective-permute-start(bf16[4,144,128]{2,1,0:T(8,128)(2,1)S(1)} %get-tuple-element.37.own_ref), channel_id=1, source_target_pairs={{0,2},{2,0},{1,3},{3,1},{4,6},{6,4},{5,7},{7,5},{8,10},{10,8},{9,1... | collective-permute-start | bytes 442376 | tf_op jit(solution)/shard_map/ppermute | solution.py:487
  21.2 8.4 %collective-permute-start.5 = (bf16[384,128]{1,0:T(8,128)(2,1)S(1)}, bf16[384,128]{1,0:T(8,128)(2,1)S(1)}, u32[]{:S(2)}, u32[]{:S(2)}) collective-permute-start(bf16[384,128]{1,0:T(8,128)(2,1)S(1)} %get-tuple-element.36.upper_ref), channel_id=1, source_target_pairs={{0,24},{8,0},{16,8},{24,16},{1,25},{9,1},{17,9},{25,17},{2,26},{10... | collective-permute-start | bytes 294920 | tf_op jit(solution)/shard_map/ppermute | solution.py:486
  26.3 9.9 %collective-permute-start.6 = (bf16[384,128]{1,0:T(8,128)(2,1)S(1)}, bf16[384,128]{1,0:T(8,128)(2,1)S(1)}, u32[]{:S(2)}, u32[]{:S(2)}) collective-permute-start(bf16[384,128]{1,0:T(8,128)(2,1)S(1)} %get-tuple-element.36.upper_ref), channel_id=1, source_target_pairs={{0,16},{8,24},{16,0},{24,8},{1,17},{9,25},{17,1},{25,9},{2,18},{10... | collective-permute-start | bytes 294920 | tf_op jit(solution)/shard_map/ppermute | solution.py:486
  27.4 11.5 %collective-permute-start.4 = (bf16[384,128]{1,0:T(8,128)(2,1)S(1)}, bf16[384,128]{1,0:T(8,128)(2,1)S(1)}, u32[]{:S(2)}, u32[]{:S(2)}) collective-permute-start(bf16[384,128]{1,0:T(8,128)(2,1)S(1)} %get-tuple-element.36.upper_ref), channel_id=1, source_target_pairs={{0,8},{8,16},{16,24},{24,0},{1,9},{9,17},{17,25},{25,1},{2,10},{10... | collective-permute-start | bytes 294920 | tf_op jit(solution)/shard_map/ppermute | solution.py:486
  36.2 10.6 %collective-permute-start.10 = (bf16[768,128]{1,0:T(8,128)(2,1)S(1)}, bf16[768,128]{1,0:T(8,128)(2,1)S(1)}, u32[]{:S(2)}, u32[]{:S(2)}) collective-permute-start(bf16[768,128]{1,0:T(8,128)(2,1)S(1)} %shard_map.81.refs_1_.refs_2_), channel_id=1, source_target_pairs={{0,32},{32,64},{64,96},{96,0},{1,33},{33,65},{65,97},{97,1},{2,34}... | collective-permute-start | bytes 589832 | tf_op jit(solution)/shard_map/ppermute | solution.py:501
  37.4 9.4 %collective-permute-start.11 = (bf16[768,128]{1,0:T(8,128)(2,1)S(1)}, bf16[768,128]{1,0:T(8,128)(2,1)S(1)}, u32[]{:S(2)}, u32[]{:S(2)}) collective-permute-start(bf16[768,128]{1,0:T(8,128)(2,1)S(1)} %shard_map.81.refs_1_.refs_2_), channel_id=1, source_target_pairs={{0,96},{32,0},{64,32},{96,64},{1,97},{33,1},{65,33},{97,65},{2,98}... | collective-permute-start | bytes 589832 | tf_op jit(solution)/shard_map/ppermute | solution.py:502
  39.0 7.9 %collective-permute-start.8 = (bf16[768,128]{1,0:T(8,128)(2,1)S(1)}, bf16[768,128]{1,0:T(8,128)(2,1)S(1)}, u32[]{:S(2)}, u32[]{:S(2)}) collective-permute-start(bf16[768,128]{1,0:T(8,128)(2,1)S(1)} %shard_map.80.refs_0_.refs_1_), channel_id=1, source_target_pairs={{0,32},{32,64},{64,96},{96,0},{1,33},{33,65},{65,97},{97,1},{2,34}... | collective-permute-start | bytes 589832 | tf_op jit(solution)/shard_map/ppermute | solution.py:489
  39.1 7.8 %collective-permute-start.9 = (bf16[768,128]{1,0:T(8,128)(2,1)S(1)}, bf16[768,128]{1,0:T(8,128)(2,1)S(1)}, u32[]{:S(2)}, u32[]{:S(2)}) collective-permute-start(bf16[768,128]{1,0:T(8,128)(2,1)S(1)} %shard_map.80.refs_0_.refs_1_), channel_id=1, source_target_pairs={{0,96},{32,0},{64,32},{96,64},{1,97},{33,1},{65,33},{97,65},{2,98}... | collective-permute-start | bytes 589832 | tf_op jit(solution)/shard_map/ppermute | solution.py:490
  47.0 9.9 %collective-permute-start.12 = (bf16[1536,128]{1,0:T(8,128)(2,1)S(1)}, bf16[1536,128]{1,0:T(8,128)(2,1)S(1)}, u32[]{:S(2)}, u32[]{:S(2)}) collective-permute-start(bf16[1536,128]{1,0:T(8,128)(2,1)S(1)} %shard_map.84), channel_id=1, source_target_pairs={{0,32},{32,64},{64,96},{96,0},{2,98},{34,2},{66,34},{98,66},{1,33}... | collective-permute-start | bytes 1179656 | tf_op jit(solution)/shard_map/ppermute | solution.py:511
  56.8 44.4 %copy-start.3 = (bf16[768,192]{0,1:T(8,128)(2,1)S(1)}, bf16[768,192]{0,1:T(8,128)(2,1)}, u32[]{:S(2)}) copy-start(bf16[768,192]{0,1:T(8,128)(2,1)} %param.11) | copy-start | bytes 884740
  56.8 46.4 %copy-start.2 = (bf16[192,768]{1,0:T(8,128)(2,1)S(1)}, bf16[192,768]{1,0:T(8,128)(2,1)}, u32[]{:S(2)}) copy-start(bf16[192,768]{1,0:T(8,128)(2,1)} %refs_6_.1) | copy-start | bytes 884740
  93.4 4.8 %collective-permute-start.13 = (f32[6,40,384]{2,1,0:T(8,128)S(1)}, f32[6,40,384]{2,1,0:T(8,128)S(1)}, u32[]{:S(2)}, u32[]{:S(2)}) collective-permute-start(f32[6,40,384]{2,1,0:T(8,128)S(1)} %get-tuple-element.46), channel_id=1, source_target_pairs={{0,2},{2,0},{1,3},{3,1},{4,6},{6,4},{5,7},{7,5},{8,10},{10,8},{9,1... | collective-permute-start | bytes 1105928 | tf_op jit(solution)/shard_map/ppermute | solution.py:515
  98.5 2.9 %collective-permute-start.14 = (bf16[144,128]{1,0:T(8,128)(2,1)S(1)}, bf16[144,128]{1,0:T(8,128)(2,1)S(1)}, u32[]{:S(2)}, u32[]{:S(2)}) collective-permute-start(bf16[144,128]{1,0:T(8,128)(2,1)S(1)} %get-tuple-element.48), channel_id=1, source_target_pairs={{0,4},{4,0},{128,132},{132,128},{1,5},{5,1},{129,133},{133,129},{2... | collective-permute-start | bytes 110600 | tf_op jit(solution)/shard_map/ppermute | solution.py:218
  99.4 3.1 %collective-permute-start.15 = (bf16[144,128]{1,0:T(8,128)(2,1)S(1)}, bf16[144,128]{1,0:T(8,128)(2,1)S(1)}, u32[]{:S(2)}, u32[]{:S(2)}) collective-permute-start(bf16[144,128]{1,0:T(8,128)(2,1)S(1)} %get-tuple-element.49), channel_id=1, source_target_pairs={{0,128},{4,132},{128,0},{132,4},{1,129},{5,133},{129,1},{133,5},{2... | collective-permute-start | bytes 110600 | tf_op jit(solution)/shard_map/ppermute | solution.py:218
  99.5 3.7 %collective-permute-start.16 = (bf16[144,128]{1,0:T(8,128)(2,1)S(1)}, bf16[144,128]{1,0:T(8,128)(2,1)S(1)}, u32[]{:S(2)}, u32[]{:S(2)}) collective-permute-start(bf16[144,128]{1,0:T(8,128)(2,1)S(1)} %get-tuple-element.50), channel_id=1, source_target_pairs={{0,132},{4,128},{128,4},{132,0},{1,133},{5,129},{129,5},{133,1},{2... | collective-permute-start | bytes 110600 | tf_op jit(solution)/shard_map/ppermute | solution.py:218
